TPU v7x, 256 devices: a 8x8x2 block of a 8x8x16 slice. The times are simulated.
256 devices in a mesh: groups: 2 (over z), expert: 128 (over x, y, core).
Axes of the slice: x: 8, y: 8, z: 2, core: 2. Of those that a mesh axis runs over, the one named last changes fastest.
The devices are a block of a 8x8x16 slice.
Arguments:
- tokens: bfloat16 [1024, 6144], P(('groups', 'expert')), parts along dimension 0, may hold values from -64 to 64
- router_weight: bfloat16 [12288, 4], P('groups'), parts along dimension 0, may hold values from -1 to 1
- expert_ids: int32 [1024, 2], P(('groups', 'expert')), parts along dimension 0, may hold values from 0 to 3, as said below
- slots: int32 [1024, 2], P(('groups', 'expert')), parts along dimension 0, may hold values from 0 to 3, as said below
- gate_weight: bfloat16 [6144, 32768], P(None, 'expert'), may hold values from -0.078125 to 0.078125
- up_weight: bfloat16 [6144, 32768], P(None, 'expert'), may hold values from -0.078125 to 0.078125
- down_weight: bfloat16 [32768, 6144], P('expert'), may hold values from -0.0625 to 0.0625
Outputs:
- mixed_rows: bfloat16 [1024, 6144], P(('groups', 'expert')), parts along dimension 0
- balance: float32 [2], P('groups'), parts along dimension 0
There are 2 independent parts, one for each index of `groups`. A program takes and returns all parts, laid end to end along the dimension named above; an argument that names none is the same for every part. Nothing has to cross between parts.
Inputs may be any that keep to these rules, and one draw needn't show every extreme that they name: `expert_ids`: each row names two different experts; one expert, drawn from the seed, is named by every token. Within the rows of one device the slots of the assignments to one expert are distinct; on every device exactly 2 assignments of the expert that every token names have slots below 2, and no expert has more.
All inputs are finite; a program needn't handle non-finite values.
Results may differ from a plain program's by a relative error of at most 0.0058.
Values may be sent and summed in bfloat16 or wider, within the bound.
No kernel may reach another device: no remote copies, remote signals or barrier semaphores. Data moves between devices by JAX's collectives and lax.ppermute only.
A program may use at most 64 MiB of HBM per device.

v0:
```python
import functools

import jax
import jax.numpy as jnp
from jax import lax
from jax.experimental import pallas as pl
from jax.experimental.pallas import tpu as pltpu
from jax.sharding import Mesh
from jax.sharding import PartitionSpec as P


EXPERTS = 4
CAP = 2
PAIR, RING, CORES = 2, 8, 2
LANES = 128
CUTS = 1
STEP = 64
EXPERT = ("xo", "xi", "y", "core")
GROUPS_EXPERT = ("groups",) + EXPERT
F32, BF16 = jnp.float32, jnp.bfloat16
HALF = RING // 2
REACH = {(0, 1): HALF, (0, -1): HALF - 1, (1, 1): HALF - 1, (1, -1): HALF}
GROUPS = [
    [(b, sign, d) for d in distances for b in (0, 1) for sign in (1, -1) if d <= REACH[b, sign]]
    for distances in ((1, 2), (3,), (4,))
]


def vmem(count):
    return [pl.BlockSpec(memory_space=pltpu.VMEM)] * count


def call(kernel, outs, args, flops=200_000, in_specs=None, scratch=()):
    size = 1_000_000
    return pl.pallas_call(
        kernel,
        out_shape=outs,
        in_specs=in_specs or vmem(len(args)),
        out_specs=vmem(len(outs)),
        scratch_shapes=list(scratch),
        cost_estimate=pl.CostEstimate(flops=flops, bytes_accessed=size, transcendentals=0),
        compiler_params=pltpu.CompilerParams(vmem_limit_bytes=4 << 20),
    )(*args)


def shape(rows, width, dtype):
    return jax.ShapeDtypeStruct((rows, width), dtype)


def column_of(scalars, count):
    row = lax.broadcasted_iota(jnp.int32, (count, 1), 0)
    value = jnp.zeros((count, 1), jnp.int32)
    for t, scalar in enumerate(scalars):
        value = jnp.where(row == t, scalar, value)
    return value


def pack_kernel(
    ids_hbm,
    slots_hbm,
    tok_hbm,
    router_hbm,
    own,
    s1,
    s2,
    s3,
    cw_ref,
    tok_ref,
    router_ref,
    ids_s,
    slots_s,
    sems,
):
    copies = [
        pltpu.make_async_copy(tok_hbm, tok_ref, sems.at[0]),
        pltpu.make_async_copy(router_hbm, router_ref, sems.at[1]),
        pltpu.make_async_copy(ids_hbm, ids_s, sems.at[2]),
        pltpu.make_async_copy(slots_hbm, slots_s, sems.at[3]),
    ]
    for copy in copies:
        copy.start()
    here = lax.axis_index("xo")
    count, width = tok_ref.shape
    for copy in copies:
        copy.wait()
    ids = [column_of([ids_s[k, t] for t in range(count)], count) for k in range(2)]
    slots = [column_of([slots_s[k, t] for t in range(count)], count) for k in range(2)]
    tok = tok_ref[...].astype(F32)
    router = router_ref[...].astype(F32)
    logits = [
        jnp.sum(tok * router[e : e + 1, :], axis=1, keepdims=True) for e in range(EXPERTS)
    ]
    top = jnp.maximum(jnp.maximum(logits[0], logits[1]), jnp.maximum(logits[2], logits[3]))
    raised = [jnp.exp(v - top) for v in logits]
    inverse = 1.0 / (raised[0] + raised[1] + raised[2] + raised[3])
    lane = lax.broadcasted_iota(jnp.int32, (1, LANES), 1)
    count_row = jnp.zeros((1, LANES), F32)
    prob_row = jnp.zeros((1, LANES), F32)
    for e in range(EXPERTS):
        named = jnp.sum(
            (ids[0] == e).astype(F32) + (ids[1] == e).astype(F32), axis=0, keepdims=True
        )
        prob = jnp.sum(raised[e] * inverse, axis=0, keepdims=True)
        high = prob.astype(BF16).astype(F32)
        count_row = jnp.where((lane == e) | (lane == e + EXPERTS), named, count_row)
        prob_row = jnp.where(lane == e, high, prob_row)
        prob_row = jnp.where(lane == e + EXPERTS, prob - high, prob_row)
    statistic = jnp.concatenate([count_row, prob_row], axis=0).astype(BF16)
    chosen = []
    for k in range(2):
        picked = jnp.zeros_like(logits[0])
        for e in range(EXPERTS):
            picked = jnp.where(ids[k] == e, logits[e], picked)
        chosen.append(picked)
    top = jnp.maximum(chosen[0], chosen[1])
    chosen = [jnp.exp(v - top) for v in chosen]
    total = chosen[0] + chosen[1]
    gates = [v / total for v in chosen]
    lane = lax.broadcasted_iota(jnp.int32, (count, LANES), 1)
    weights = jnp.zeros((count, LANES), F32)
    for j, out in enumerate((own, s1, s2, s3)):
        expert = lax.rem(here + j, EXPERTS)
        rows = []
        for s in range(CAP):
            row = jnp.zeros((1, width), F32)
            for t in range(count):
                hit = ((ids_s[0, t] == expert) & (slots_s[0, t] == s)) | (
                    (ids_s[1, t] == expert) & (slots_s[1, t] == s)
                )
                row = jnp.where(hit, tok[t : t + 1, :], row)
            rows.append(row)
            column = jnp.zeros((count, 1), F32)
            for k in range(2):
                match = (ids[k] == expert) & (slots[k] == s)
                column = jnp.where(match, gates[k], column)
            weights = jnp.where(lane == j * CAP + s, column, weights)
        out[:, :width] = jnp.concatenate(rows, axis=0).astype(BF16)
        out[:, width:] = statistic
    cw_ref[...] = weights


def in_hbm(value):
    return pltpu.with_memory_space_constraint(value, pltpu.HBM)


def join_kernel(own, r1, r2, r3, unread, out):
    out[...] = jnp.concatenate([ref[...].astype(F32) for ref in (own, r1, r2, r3)], axis=0).astype(
        out.dtype
    )


def stack_kernel(count, *refs):
    start = 0
    for ref in refs[:count]:
        refs[-1][start : start + ref.shape[0], :] = ref[...]
        start += ref.shape[0]


def deep_dot(x_ref, weight_ref, cuts=CUTS):
    depth = weight_ref.shape[0] // cuts
    total = None
    for n in range(cuts):
        at = slice(n * depth, (n + 1) * depth)
        value = jnp.dot(x_ref[:, at], weight_ref[at, :], preferred_element_type=F32)
        total = value if n == 0 else total + value
    return total


def expert_rows(near, far, x_ref, hidden_ref, gate_ref, up_ref, down_ref, outs, lanes, ready):
    width = down_ref.shape[1]
    start = 0
    total = jnp.zeros((8, LANES), F32)
    for block in near + far:
        rows = block.shape[0]
        x_ref[start : start + rows, :] = block[:, :width]
        start += rows
        for n in range(0, rows, 8):
            total = total + block[n : n + 8, width:].astype(F32)
    lanes(total)
    gate = deep_dot(x_ref, gate_ref)
    ready()
    up = deep_dot(x_ref, up_ref)
    hidden_ref[...] = (gate * jax.nn.sigmoid(gate) * up).astype(BF16)
    tile = 512

    def down(i, carry):
        at = pl.ds(pl.multiple_of(i * tile, tile), tile)
        value = jnp.dot(hidden_ref[...], down_ref[:, at], preferred_element_type=F32)
        start = 0
        for out in outs:
            out[:, at] = value[start : start + out.shape[0], :].astype(out.dtype)
            start += out.shape[0]
        return carry

    lax.fori_loop(0, width // tile, down, 0)


def first_kernel(near, far, gate, down, up_hbm, kept, sent, up_ref, total_ref, x, hidden, sem):
    copy = pltpu.make_async_copy(up_hbm, up_ref, sem.at[0])
    copy.start()

    def lanes(total):
        total_ref[...] = total

    expert_rows([near], [far], x, hidden, gate, up_ref, down, [kept, sent], lanes, copy.wait)


def second_kernel(scale, near, near_4, far, far_4, gate, up, down, before, *refs):
    outs, balance_ref, x, hidden = refs[:4], refs[4], refs[5], refs[6]

    def lanes(total):
        total = before[...] + total
        parity = lax.broadcasted_iota(jnp.int32, total.shape, 0) % 2
        named = jnp.sum(jnp.where(parity == 0, total, 0.0), axis=0, keepdims=True)
        probs = jnp.sum(jnp.where(parity == 1, total, 0.0), axis=0, keepdims=True)
        balance_ref[...] = jnp.sum(named * probs, axis=1, keepdims=True) * scale

    expert_rows(
        [near, near_4], [far, far_4], x, hidden, gate, up, down, outs, lanes, lambda: None
    )


def fetch_kernel(*refs):
    count = (len(refs) - 2) // 2
    copies = [
        pltpu.make_async_copy(refs[n], refs[count + 1 + n], refs[-1].at[n]) for n in range(count)
    ]
    for copy in copies:
        copy.start()
    for copy in copies:
        copy.wait()


def fetch(weights, after):
    return pl.pallas_call(
        fetch_kernel,
        out_shape=[pltpu.VMEM(w.shape, w.dtype) for w in weights],
        in_specs=[pl.BlockSpec(memory_space=pltpu.HBM)] * len(weights)
        + [pl.BlockSpec(memory_space=pl.ANY)],
        out_specs=vmem(len(weights)),
        scratch_shapes=[pltpu.SemaphoreType.DMA((len(weights),))],
        cost_estimate=pl.CostEstimate(
            flops=1_000_000,
            bytes_accessed=sum(2 * w.size * w.dtype.itemsize for w in weights),
            transcendentals=0,
        ),
        compiler_params=pltpu.CompilerParams(vmem_limit_bytes=4 << 20),
    )(*[in_hbm(w) for w in weights], after)


def add_kernel(start, kept_ref, crossed_ref, *refs):
    out = refs[-1]
    at = slice(start, start + out.shape[0])
    value = kept_ref[at, :] + crossed_ref[at, :].astype(F32)
    for ref in refs[:-1]:
        value = value + ref[...].astype(F32)
    out[...] = value.astype(out.dtype)


def part_kernel(a_ref, came_ref, own, s1, s2, s3):
    total = a_ref[...] + came_ref[...].astype(F32)
    for j, out in enumerate((own, s1, s2, s3)):
        out[...] = total[j * CAP : (j + 1) * CAP].astype(out.dtype)


def mix_kernel(cw_ref, own, r1, r2, r3, out):
    weights = cw_ref[...]
    total = None
    for j, ref in enumerate((own, r1, r2, r3)):
        value = ref[...].astype(F32)
        for s in range(CAP):
            at = j * CAP + s
            term = weights[:, at : at + 1] * value[s : s + 1, :]
            total = term if total is None else total + term
    out[...] = total.astype(out.dtype)


def in_hbm(value):
    return pltpu.with_memory_space_constraint(value, pltpu.HBM)


def to_expert(value, step):
    return lax.ppermute(value, "xo", [(i, (i + step) % EXPERTS) for i in range(EXPERTS)])


def swap(value, axis):
    return lax.ppermute(value, axis, [(0, 1), (1, 0)])


def along(value, step):
    return lax.ppermute(value, "y", [(y, (y + step) % RING) for y in range(RING)])


def local(tokens, router_weight, expert_ids, slots, gate_weight, up_weight, down_weight):
    devices = lax.axis_size(EXPERT)
    count, width = tokens.shape
    wide = width + LANES
    hbm = pl.BlockSpec(memory_space=pltpu.HBM)
    *sends, weights = call(
        pack_kernel,
        [shape(CAP, wide, BF16)] * EXPERTS + [shape(count, LANES, F32)],
        [in_hbm(a) for a in (expert_ids.T, slots.T, tokens, router_weight.T)],
        in_specs=[hbm] * 4,
        scratch=[
            pltpu.VMEM(tokens.shape, BF16),
            pltpu.VMEM(router_weight.shape[::-1], BF16),
            pltpu.SMEM(slots.shape[::-1], jnp.int32),
            pltpu.SMEM(slots.shape[::-1], jnp.int32),
            pltpu.SemaphoreType.DMA((4,)),
        ],
    )
    arrived = [sends[0]] + [to_expert(sends[k], k) for k in range(1, EXPERTS)]
    size = EXPERTS * CAP
    gate_near, down_near = fetch([gate_weight, down_weight], sends[0])
    block_a = call(
        join_kernel,
        [shape(size, wide, BF16)],
        (*arrived, gate_near),
        in_specs=vmem(EXPERTS) + [pl.BlockSpec(memory_space=pl.ANY)],
    )[0]
    block_b = swap(block_a, "xi")

    got = {}
    for b, block in enumerate((block_a, block_b)):
        for sign in (1, -1):
            moving = block
            for d in range(1, REACH[b, sign] + 1):
                moving = along(moving, sign)
                got[b, sign, d] = moving
    parts = [[got[key] for key in keys] for keys in GROUPS]
    parts[0] = [block_a, block_b] + parts[0]
    rows = [size * len(part) for part in parts]
    near, far = [], []
    for group, part in enumerate(parts):
        near += call(
            functools.partial(stack_kernel, len(part)), [shape(rows[group], wide, BF16)], part
        )
        far.append(swap(near[group], "core"))

    units = gate_weight.shape[1]
    total_tokens = count * devices
    scale = EXPERTS / (2.0 * total_tokens * total_tokens)

    def expert(kernel, rows, args, in_specs, outs, scratch=()):
        return pl.pallas_call(
            kernel,
            out_shape=[shape(n, width, dtype) for dtype in (F32, BF16) for n in rows] + outs,
            in_specs=in_specs,
            out_specs=vmem(2 * len(rows) + len(outs)),
            scratch_shapes=[
                pltpu.VMEM((-(-2 * sum(rows) // STEP) * STEP, width), BF16),
                pltpu.VMEM((-(-2 * sum(rows) // STEP) * STEP, units), BF16),
                *scratch,
            ],
            cost_estimate=pl.CostEstimate(
                flops=12 * sum(rows) * width * units, bytes_accessed=9_000_000, transcendentals=0
            ),
            compiler_params=pltpu.CompilerParams(vmem_limit_bytes=24 << 20),
        )(*args)

    *first, up_near, total = expert(
        first_kernel,
        rows[:1],
        (near[0], far[0], gate_near, down_near, in_hbm(up_weight)),
        vmem(4) + [hbm],
        [pltpu.VMEM(up_weight.shape, BF16), shape(8, LANES, F32)],
        [pltpu.SemaphoreType.DMA((1,))],
    )
    *second, balance = expert(
        functools.partial(second_kernel, scale),
        rows[1:],
        (*near[1:], *far[1:], gate_near, up_near, down_near, total),
        vmem(8),
        [shape(1, 1, F32)],
    )
    balance = balance.reshape(1)
    kept = [first[0], second[0], second[1]]
    crossed = {}
    for group, value in ((2, second[3]), (1, second[2]), (0, first[1])):
        crossed[group] = swap(value, "core")

    moving = {}
    for group in reversed(range(len(GROUPS))):
        for d in sorted({key[2] for key in GROUPS[group]}, reverse=True):
            for b, sign in REACH:
                key = (b, sign, d)
                if key not in GROUPS[group]:
                    continue
                start = size * (GROUPS[group].index(key) + (2 if group == 0 else 0))
                came = [moving[b, sign]] if (b, sign) in moving else []
                value = call(
                    functools.partial(add_kernel, start),
                    [shape(size, width, BF16)],
                    [kept[group], crossed[group]] + came,
                )[0]
                moving[b, sign] = along(value, -sign)
    sums = []
    for b, dtype in ((1, BF16), (0, F32)):
        sums += call(
            functools.partial(add_kernel, b * size),
            [shape(size, width, dtype)],
            (kept[0], crossed[0], moving[b, 1], moving[b, -1]),
        )
    pieces = call(
        part_kernel,
        [shape(CAP, width, F32)] + [shape(CAP, width, BF16)] * 3,
        (sums[1], swap(sums[0], "xi")),
    )
    returned = [pieces[0]] + [to_expert(pieces[k], -k) for k in range(1, EXPERTS)]
    mixed_rows = call(mix_kernel, [shape(count, width, BF16)], (weights, *returned))[0]
    return (mixed_rows, balance)


def solution(mesh):
    split = Mesh(
        mesh.devices.reshape(mesh.shape["groups"], EXPERTS, PAIR, RING, CORES),
        GROUPS_EXPERT,
    )
    placed = (
        P(GROUPS_EXPERT, None),
        P("groups", None),
        P(GROUPS_EXPERT, None),
        P(GROUPS_EXPERT, None),
        P(None, EXPERT),
        P(None, EXPERT),
        P(EXPERT, None),
    )

    return jax.shard_map(
        local,
        mesh=split,
        in_specs=placed,
        out_specs=(P(GROUPS_EXPERT, None), P("groups")),
        check_vma=False,
    )
```

profile of v0, /device:TPU:514, one launch (start us, length us, event | category | flops | bytes accessed | tf_op | source)
XLA Modules:
  0.0 119.1 jit_solution(12903569826098076407)
XLA Ops:
  0.6 1.4 %shard_map.86 = (bf16[2,6272]{1,0:T(2,128)(2,1)S(1)}, bf16[2,6272]{1,0:T(2,128)(2,1)S(1)}, bf16[2,6272]{1,0:T(2,128)(2,1)S(1)}, bf16[2,6272]{1,0:T(2,128)(2,1)S(1)}, f32[4,128]{1,0:T(4,128)S(1)}) custom-call(s32[2,4]{1,0:T(2,128)} %bitcast.5, s32[2,4]{1,0:T(2,128)} %bitcast.6, bf16[4,6144]{1,0:T(4,128)(2,1)} %tok_hbm.1, bf16[4,6144]{1,0:T(4,128)(2,1)} %bitcast.4), custom_call_target="tpu_custom_call" | custom-call | flops 200000 | bytes 1000000 | tf_op jit(solution)/shard_map/pallas_call | solution.py:35
  2.1 2.8 %collective-permute-start = (bf16[2,6272]{1,0:T(2,128)(2,1)S(1)}, bf16[2,6272]{1,0:T(2,128)(2,1)S(1)}, u32[]{:S(2)}, u32[]{:S(2)}) collective-permute-start(bf16[2,6272]{1,0:T(2,128)(2,1)S(1)} %get-tuple-element.24), channel_id=1, source_target_pairs={{0,32},{32,64},{64,96},{96,0},{1,33},{33,65},{65,97},{97,1},{2,34}... | collective-permute-start | bytes 75272 | tf_op jit(solution)/shard_map/ppermute | solution.py:283
  4.9 3.3 %collective-permute-start.1 = (bf16[2,6272]{1,0:T(2,128)(2,1)S(1)}, bf16[2,6272]{1,0:T(2,128)(2,1)S(1)}, u32[]{:S(2)}, u32[]{:S(2)}) collective-permute-start(bf16[2,6272]{1,0:T(2,128)(2,1)S(1)} %get-tuple-element.25), channel_id=1, source_target_pairs={{0,64},{32,96},{64,0},{96,32},{1,65},{33,97},{65,1},{97,33},{2,66}... | collective-permute-start | bytes 75272 | tf_op jit(solution)/shard_map/ppermute | solution.py:283
  8.2 3.2 %collective-permute-start.2 = (bf16[2,6272]{1,0:T(2,128)(2,1)S(1)}, bf16[2,6272]{1,0:T(2,128)(2,1)S(1)}, u32[]{:S(2)}, u32[]{:S(2)}) collective-permute-start(bf16[2,6272]{1,0:T(2,128)(2,1)S(1)} %get-tuple-element.26), channel_id=1, source_target_pairs={{0,96},{32,0},{64,32},{96,64},{1,97},{33,1},{65,33},{97,65},{2,98}... | collective-permute-start | bytes 75272 | tf_op jit(solution)/shard_map/ppermute | solution.py:283
  11.4 2.9 %shard_map.87 = (bf16[6144,256]{1,0:T(8,128)(2,1)S(1)}, bf16[256,6144]{1,0:T(8,128)(2,1)S(1)}) custom-call(bf16[6144,256]{1,0:T(8,128)(2,1)} %refs_0_.1, bf16[256,6144]{1,0:T(8,128)(2,1)} %refs_1_.1, bf16[2,6272]{1,0:T(2,128)(2,1)S(1)} %get-tuple-element.23.refs_2_.own), custom_call_target="tpu_custom_call" | custom-call | flops 1000000 | bytes 12582912 | tf_op jit(solution)/shard_map/pallas_call | solution.py:235
  14.4 15.6 %collective-permute-start.3 = (bf16[8,6272]{1,0:T(8,128)(2,1)S(1)}, bf16[8,6272]{1,0:T(8,128)(2,1)S(1)}, u32[]{:S(2)}, u32[]{:S(2)}) collective-permute-start(bf16[8,6272]{1,0:T(8,128)(2,1)S(1)} %shard_map.88.refs_0_), channel_id=1, source_target_pairs={{0,16},{16,0},{1,17},{17,1},{2,18},{18,2},{3,19},{19,3},{4,20},{20... | collective-permute-start | bytes 301064 | tf_op jit(solution)/shard_map/ppermute | solution.py:287
  30.1 3.2 %collective-permute-start.5 = (bf16[8,6272]{1,0:T(8,128)(2,1)S(1)}, bf16[8,6272]{1,0:T(8,128)(2,1)S(1)}, u32[]{:S(2)}, u32[]{:S(2)}) collective-permute-start(bf16[8,6272]{1,0:T(8,128)(2,1)S(1)} %shard_map.88.refs_0_), channel_id=1, source_target_pairs={{0,14},{2,0},{4,2},{6,4},{8,6},{10,8},{12,10},{14,12},{1,15},{3,1}... | collective-permute-start | bytes 301064 | tf_op jit(solution)/shard_map/ppermute | solution.py:291
  33.3 3.2 %collective-permute-start.7 = (bf16[8,6272]{1,0:T(8,128)(2,1)S(1)}, bf16[8,6272]{1,0:T(8,128)(2,1)S(1)}, u32[]{:S(2)}, u32[]{:S(2)}) collective-permute-start(bf16[8,6272]{1,0:T(8,128)(2,1)S(1)} %collective-permute-done.3.refs_1_), channel_id=1, source_target_pairs={{0,14},{2,0},{4,2},{6,4},{8,6},{10,8},{12,10},{14,12},{1,15},{3,1}... | collective-permute-start | bytes 301064 | tf_op jit(solution)/shard_map/ppermute | solution.py:291
  36.5 3.4 %collective-permute-start.9 = (bf16[8,6272]{1,0:T(8,128)(2,1)S(1)}, bf16[8,6272]{1,0:T(8,128)(2,1)S(1)}, u32[]{:S(2)}, u32[]{:S(2)}) collective-permute-start(bf16[8,6272]{1,0:T(8,128)(2,1)S(1)} %collective-permute-done.5.refs_3_), channel_id=1, source_target_pairs={{0,14},{2,0},{4,2},{6,4},{8,6},{10,8},{12,10},{14,12},{1,15},{3,1}... | collective-permute-start | bytes 301064 | tf_op jit(solution)/shard_map/ppermute | solution.py:291
  40.0 3.2 %collective-permute-start.11 = (bf16[8,6272]{1,0:T(8,128)(2,1)S(1)}, bf16[8,6272]{1,0:T(8,128)(2,1)S(1)}, u32[]{:S(2)}, u32[]{:S(2)}) collective-permute-start(bf16[8,6272]{1,0:T(8,128)(2,1)S(1)} %collective-permute-done.7.refs_5_), channel_id=1, source_target_pairs={{0,14},{2,0},{4,2},{6,4},{8,6},{10,8},{12,10},{14,12},{1,15},{3,1}... | collective-permute-start | bytes 301064 | tf_op jit(solution)/shard_map/ppermute | solution.py:291
  43.2 2.6 %collective-permute-done.10.refs_8_ = bf16[8,6272]{1,0:T(8,128)(2,1)S(1)} collective-permute-done((bf16[8,6272]{1,0:T(8,128)(2,1)S(1)}, bf16[8,6272]{1,0:T(8,128)(2,1)S(1)}, u32[]{:S(2)}, u32[]{:S(2)}) %collective-permute-start.10) | collective-permute-done | bytes 100384 | tf_op jit(solution)/shard_map/ppermute | solution.py:291
  46.2 3.5 %collective-permute-start.15 = (bf16[8,6272]{1,0:T(8,128)(2,1)S(1)}, bf16[8,6272]{1,0:T(8,128)(2,1)S(1)}, u32[]{:S(2)}, u32[]{:S(2)}) collective-permute-start(bf16[8,6272]{1,0:T(8,128)(2,1)S(1)} %collective-permute-done.9.refs_7_), channel_id=1, source_target_pairs={{0,14},{2,0},{4,2},{6,4},{8,6},{10,8},{12,10},{14,12},{1,15},{3,1}... | collective-permute-start | bytes 301064 | tf_op jit(solution)/shard_map/ppermute | solution.py:291
  49.7 3.2 %collective-permute-start.17 = (bf16[8,6272]{1,0:T(8,128)(2,1)S(1)}, bf16[8,6272]{1,0:T(8,128)(2,1)S(1)}, u32[]{:S(2)}, u32[]{:S(2)}) collective-permute-start(bf16[8,6272]{1,0:T(8,128)(2,1)S(1)} %collective-permute-done.11.refs_9_), channel_id=1, source_target_pairs={{0,14},{2,0},{4,2},{6,4},{8,6},{10,8},{12,10},{14,12},{1,15},{3,1}... | collective-permute-start | bytes 301064 | tf_op jit(solution)/shard_map/ppermute | solution.py:291
  52.9 5.8 %shard_map.90 = (f32[80,6144]{1,0:T(8,128)S(1)}, bf16[80,6144]{1,0:T(8,128)(2,1)S(1)}, bf16[6144,256]{1,0:T(8,128)(2,1)S(1)}, f32[8,128]{1,0:T(8,128)S(1)}) custom-call(bf16[80,6272]{1,0:T(8,128)(2,1)S(1)} %shard_map.89.near, bf16[80,6272]{1,0:T(8,128)(2,1)S(1)} %collective-permute-done.12.far, bf16[6144,256]{1,0:T(8,128)(2,1)S(1)} %get-tuple-element.27.unread.gate, ...), custom_call_target="tpu_custom_call" | custom-call | flops 1509949440 | bytes 9000000 | tf_op jit(solution)/shard_map/pallas_call | solution.py:345
  59.6 3.2 %collective-permute-start.19 = (bf16[8,6272]{1,0:T(8,128)(2,1)S(1)}, bf16[8,6272]{1,0:T(8,128)(2,1)S(1)}, u32[]{:S(2)}, u32[]{:S(2)}) collective-permute-start(bf16[8,6272]{1,0:T(8,128)(2,1)S(1)} %collective-permute-done.17.refs_3_), channel_id=1, source_target_pairs={{0,14},{2,0},{4,2},{6,4},{8,6},{10,8},{12,10},{14,12},{1,15},{3,1}... | collective-permute-start | bytes 301064 | tf_op jit(solution)/shard_map/ppermute | solution.py:291
  62.8 2.9 %collective-permute-done.18.refs_0_ = bf16[8,6272]{1,0:T(8,128)(2,1)S(1)} collective-permute-done((bf16[8,6272]{1,0:T(8,128)(2,1)S(1)}, bf16[8,6272]{1,0:T(8,128)(2,1)S(1)}, u32[]{:S(2)}, u32[]{:S(2)}) %collective-permute-start.18) | collective-permute-done | bytes 100384 | tf_op jit(solution)/shard_map/ppermute | solution.py:291
  65.9 1.4 %collective-permute-done.21.far_4 = bf16[16,6272]{1,0:T(8,128)(2,1)S(1)} collective-permute-done((bf16[16,6272]{1,0:T(8,128)(2,1)S(1)}, bf16[16,6272]{1,0:T(8,128)(2,1)S(1)}, u32[]{:S(2)}, u32[]{:S(2)}) %collective-permute-start.21) | collective-permute-done | bytes 200736 | tf_op jit(solution)/shard_map/ppermute | solution.py:287
  67.3 3.7 %shard_map.93 = (f32[32,6144]{1,0:T(8,128)S(1)}, f32[16,6144]{1,0:T(8,128)S(1)}, bf16[32,6144]{1,0:T(8,128)(2,1)S(1)}, bf16[16,6144]{1,0:T(8,128)(2,1)S(1)}, f32[1,1]{1,0:T(1,128)}) custom-call(bf16[32,6272]{1,0:T(8,128)(2,1)S(1)} %shard_map.91.near, bf16[16,6272]{1,0:T(8,128)(2,1)S(1)} %shard_map.92.near_4, ...), custom_call_target="tpu_custom_call" | custom-call | flops 905969664 | bytes 9000000 | tf_op jit(solution)/shard_map/pallas_call | solution.py:345
  71.5 1.5 %collective-permute-done.23.crossed_ref = bf16[16,6144]{1,0:T(8,128)(2,1)S(1)} collective-permute-done((bf16[16,6144]{1,0:T(8,128)(2,1)S(1)}, bf16[16,6144]{1,0:T(8,128)(2,1)S(1)}, u32[]{:S(2)}, u32[]{:S(2)}) %collective-permute-start.23) | collective-permute-done | bytes 196640 | tf_op jit(solution)/shard_map/ppermute | solution.py:287
  73.2 3.3 %collective-permute-start.24 = (bf16[8,6144]{1,0:T(8,128)(2,1)S(1)}, bf16[8,6144]{1,0:T(8,128)(2,1)S(1)}, u32[]{:S(2)}, u32[]{:S(2)}) collective-permute-start(bf16[8,6144]{1,0:T(8,128)(2,1)S(1)} %shard_map.94), channel_id=1, source_target_pairs={{0,14},{2,0},{4,2},{6,4},{8,6},{10,8},{12,10},{14,12},{1,15},{3,1}... | collective-permute-start | bytes 294920 | tf_op jit(solution)/shard_map/ppermute | solution.py:291
  76.5 1.9 %collective-permute-start.31 = (bf16[8,6144]{1,0:T(8,128)(2,1)S(1)}, bf16[8,6144]{1,0:T(8,128)(2,1)S(1)}, u32[]{:S(2)}, u32[]{:S(2)}) collective-permute-start(bf16[8,6144]{1,0:T(8,128)(2,1)S(1)} %shard_map.102), channel_id=1, source_target_pairs={{0,14},{2,0},{4,2},{6,4},{8,6},{10,8},{12,10},{14,12},{1,15},{3,1}... | collective-permute-start | bytes 294920 | tf_op jit(solution)/shard_map/ppermute | solution.py:291
  79.7 3.3 %collective-permute-start.25 = (bf16[8,6144]{1,0:T(8,128)(2,1)S(1)}, bf16[8,6144]{1,0:T(8,128)(2,1)S(1)}, u32[]{:S(2)}, u32[]{:S(2)}) collective-permute-start(bf16[8,6144]{1,0:T(8,128)(2,1)S(1)} %shard_map.95), channel_id=1, source_target_pairs={{0,14},{2,0},{4,2},{6,4},{8,6},{10,8},{12,10},{14,12},{1,15},{3,1}... | collective-permute-start | bytes 294920 | tf_op jit(solution)/shard_map/ppermute | solution.py:291
  83.2 3.3 %collective-permute-start.32 = (bf16[8,6144]{1,0:T(8,128)(2,1)S(1)}, bf16[8,6144]{1,0:T(8,128)(2,1)S(1)}, u32[]{:S(2)}, u32[]{:S(2)}) collective-permute-start(bf16[8,6144]{1,0:T(8,128)(2,1)S(1)} %shard_map.103), channel_id=1, source_target_pairs={{0,14},{2,0},{4,2},{6,4},{8,6},{10,8},{12,10},{14,12},{1,15},{3,1}... | collective-permute-start | bytes 294920 | tf_op jit(solution)/shard_map/ppermute | solution.py:291
  86.8 3.3 %collective-permute-start.26 = (bf16[8,6144]{1,0:T(8,128)(2,1)S(1)}, bf16[8,6144]{1,0:T(8,128)(2,1)S(1)}, u32[]{:S(2)}, u32[]{:S(2)}) collective-permute-start(bf16[8,6144]{1,0:T(8,128)(2,1)S(1)} %shard_map.96), channel_id=1, source_target_pairs={{0,14},{2,0},{4,2},{6,4},{8,6},{10,8},{12,10},{14,12},{1,15},{3,1}... | collective-permute-start | bytes 294920 | tf_op jit(solution)/shard_map/ppermute | solution.py:291
  90.3 3.3 %collective-permute-start.33 = (bf16[8,6144]{1,0:T(8,128)(2,1)S(1)}, bf16[8,6144]{1,0:T(8,128)(2,1)S(1)}, u32[]{:S(2)}, u32[]{:S(2)}) collective-permute-start(bf16[8,6144]{1,0:T(8,128)(2,1)S(1)} %shard_map.104), channel_id=1, source_target_pairs={{0,14},{2,0},{4,2},{6,4},{8,6},{10,8},{12,10},{14,12},{1,15},{3,1}... | collective-permute-start | bytes 294920 | tf_op jit(solution)/shard_map/ppermute | solution.py:291
  93.9 3.3 %collective-permute-start.27 = (bf16[8,6144]{1,0:T(8,128)(2,1)S(1)}, bf16[8,6144]{1,0:T(8,128)(2,1)S(1)}, u32[]{:S(2)}, u32[]{:S(2)}) collective-permute-start(bf16[8,6144]{1,0:T(8,128)(2,1)S(1)} %shard_map.97), channel_id=1, source_target_pairs={{0,14},{2,0},{4,2},{6,4},{8,6},{10,8},{12,10},{14,12},{1,15},{3,1}... | collective-permute-start | bytes 294920 | tf_op jit(solution)/shard_map/ppermute | solution.py:291
  97.4 2.4 %collective-permute-done.37.refs_1_ = bf16[8,6144]{1,0:T(8,128)(2,1)S(1)} collective-permute-done((bf16[8,6144]{1,0:T(8,128)(2,1)S(1)}, bf16[8,6144]{1,0:T(8,128)(2,1)S(1)}, u32[]{:S(2)}, u32[]{:S(2)}) %collective-permute-start.37) | collective-permute-done | bytes 98336 | tf_op jit(solution)/shard_map/ppermute | solution.py:291
  101.1 2.0 %collective-permute-done.30.refs_1_ = bf16[8,6144]{1,0:T(8,128)(2,1)S(1)} collective-permute-done((bf16[8,6144]{1,0:T(8,128)(2,1)S(1)}, bf16[8,6144]{1,0:T(8,128)(2,1)S(1)}, u32[]{:S(2)}, u32[]{:S(2)}) %collective-permute-start.30) | collective-permute-done | bytes 98336 | tf_op jit(solution)/shard_map/ppermute | solution.py:291
  104.6 3.5 %collective-permute-start.39 = (bf16[2,6144]{1,0:T(2,128)(2,1)S(1)}, bf16[2,6144]{1,0:T(2,128)(2,1)S(1)}, u32[]{:S(2)}, u32[]{:S(2)}) collective-permute-start(bf16[2,6144]{1,0:T(2,128)(2,1)S(1)} %get-tuple-element.38), channel_id=1, source_target_pairs={{0,96},{32,0},{64,32},{96,64},{1,97},{33,1},{65,33},{97,65},{2,98}... | collective-permute-start | bytes 73736 | tf_op jit(solution)/shard_map/ppermute | solution.py:283
  108.1 4.2 %collective-permute-start.40 = (bf16[2,6144]{1,0:T(2,128)(2,1)S(1)}, bf16[2,6144]{1,0:T(2,128)(2,1)S(1)}, u32[]{:S(2)}, u32[]{:S(2)}) collective-permute-start(bf16[2,6144]{1,0:T(2,128)(2,1)S(1)} %get-tuple-element.39), channel_id=1, source_target_pairs={{0,64},{32,96},{64,0},{96,32},{1,65},{33,97},{65,1},{97,33},{2,66}... | collective-permute-start | bytes 73736 | tf_op jit(solution)/shard_map/ppermute | solution.py:283
  112.2 3.6 %collective-permute-done.40.r2 = bf16[2,6144]{1,0:T(2,128)(2,1)S(1)} collective-permute-done((bf16[2,6144]{1,0:T(2,128)(2,1)S(1)}, bf16[2,6144]{1,0:T(2,128)(2,1)S(1)}, u32[]{:S(2)}, u32[]{:S(2)}) %collective-permute-start.40) | collective-permute-done | bytes 24608 | tf_op jit(solution)/shard_map/ppermute | solution.py:283
  115.8 2.3 %collective-permute-done.41.r3 = bf16[2,6144]{1,0:T(2,128)(2,1)S(1)} collective-permute-done((bf16[2,6144]{1,0:T(2,128)(2,1)S(1)}, bf16[2,6144]{1,0:T(2,128)(2,1)S(1)}, u32[]{:S(2)}, u32[]{:S(2)}) %collective-permute-start.41) | collective-permute-done | bytes 24608 | tf_op jit(solution)/shard_map/ppermute | solution.py:283
  (78 shorter events, 8.1 us)
Async XLA Ops:
  2.1 12.2 %collective-permute-start = (bf16[2,6272]{1,0:T(2,128)(2,1)S(1)}, bf16[2,6272]{1,0:T(2,128)(2,1)S(1)}, u32[]{:S(2)}, u32[]{:S(2)}) collective-permute-start(bf16[2,6272]{1,0:T(2,128)(2,1)S(1)} %get-tuple-element.24), channel_id=1, source_target_pairs={{0,32},{32,64},{64,96},{96,0},{1,33},{33,65},{65,97},{97,1},{2,34}... | collective-permute-start | bytes 75272 | tf_op jit(solution)/shard_map/ppermute | solution.py:283
  4.9 9.5 %collective-permute-start.1 = (bf16[2,6272]{1,0:T(2,128)(2,1)S(1)}, bf16[2,6272]{1,0:T(2,128)(2,1)S(1)}, u32[]{:S(2)}, u32[]{:S(2)}) collective-permute-start(bf16[2,6272]{1,0:T(2,128)(2,1)S(1)} %get-tuple-element.25), channel_id=1, source_target_pairs={{0,64},{32,96},{64,0},{96,32},{1,65},{33,97},{65,1},{97,33},{2,66}... | collective-permute-start | bytes 75272 | tf_op jit(solution)/shard_map/ppermute | solution.py:283
  8.2 6.1 %collective-permute-start.2 = (bf16[2,6272]{1,0:T(2,128)(2,1)S(1)}, bf16[2,6272]{1,0:T(2,128)(2,1)S(1)}, u32[]{:S(2)}, u32[]{:S(2)}) collective-permute-start(bf16[2,6272]{1,0:T(2,128)(2,1)S(1)} %get-tuple-element.26), channel_id=1, source_target_pairs={{0,96},{32,0},{64,32},{96,64},{1,97},{33,1},{65,33},{97,65},{2,98}... | collective-permute-start | bytes 75272 | tf_op jit(solution)/shard_map/ppermute | solution.py:283
  14.4 18.9 %collective-permute-start.3 = (bf16[8,6272]{1,0:T(8,128)(2,1)S(1)}, bf16[8,6272]{1,0:T(8,128)(2,1)S(1)}, u32[]{:S(2)}, u32[]{:S(2)}) collective-permute-start(bf16[8,6272]{1,0:T(8,128)(2,1)S(1)} %shard_map.88.refs_0_), channel_id=1, source_target_pairs={{0,16},{16,0},{1,17},{17,1},{2,18},{18,2},{3,19},{19,3},{4,20},{20... | collective-permute-start | bytes 301064 | tf_op jit(solution)/shard_map/ppermute | solution.py:287
  30.1 6.5 %collective-permute-start.4 = (bf16[8,6272]{1,0:T(8,128)(2,1)S(1)}, bf16[8,6272]{1,0:T(8,128)(2,1)S(1)}, u32[]{:S(2)}, u32[]{:S(2)}) collective-permute-start(bf16[8,6272]{1,0:T(8,128)(2,1)S(1)} %shard_map.88.refs_0_), channel_id=1, source_target_pairs={{0,2},{2,4},{4,6},{6,8},{8,10},{10,12},{12,14},{14,0},{1,3},{3,5},... | collective-permute-start | bytes 301064 | tf_op jit(solution)/shard_map/ppermute | solution.py:291
  30.1 6.5 %collective-permute-start.5 = (bf16[8,6272]{1,0:T(8,128)(2,1)S(1)}, bf16[8,6272]{1,0:T(8,128)(2,1)S(1)}, u32[]{:S(2)}, u32[]{:S(2)}) collective-permute-start(bf16[8,6272]{1,0:T(8,128)(2,1)S(1)} %shard_map.88.refs_0_), channel_id=1, source_target_pairs={{0,14},{2,0},{4,2},{6,4},{8,6},{10,8},{12,10},{14,12},{1,15},{3,1}... | collective-permute-start | bytes 301064 | tf_op jit(solution)/shard_map/ppermute | solution.py:291
  33.3 6.7 %collective-permute-start.6 = (bf16[8,6272]{1,0:T(8,128)(2,1)S(1)}, bf16[8,6272]{1,0:T(8,128)(2,1)S(1)}, u32[]{:S(2)}, u32[]{:S(2)}) collective-permute-start(bf16[8,6272]{1,0:T(8,128)(2,1)S(1)} %collective-permute-done.3.refs_1_), channel_id=1, source_target_pairs={{0,2},{2,4},{4,6},{6,8},{8,10},{10,12},{12,14},{14,0},{1,3},{3,5},... | collective-permute-start | bytes 301064 | tf_op jit(solution)/shard_map/ppermute | solution.py:291
  33.3 6.7 %collective-permute-start.7 = (bf16[8,6272]{1,0:T(8,128)(2,1)S(1)}, bf16[8,6272]{1,0:T(8,128)(2,1)S(1)}, u32[]{:S(2)}, u32[]{:S(2)}) collective-permute-start(bf16[8,6272]{1,0:T(8,128)(2,1)S(1)} %collective-permute-done.3.refs_1_), channel_id=1, source_target_pairs={{0,14},{2,0},{4,2},{6,4},{8,6},{10,8},{12,10},{14,12},{1,15},{3,1}... | collective-permute-start | bytes 301064 | tf_op jit(solution)/shard_map/ppermute | solution.py:291
  36.5 6.7 %collective-permute-start.8 = (bf16[8,6272]{1,0:T(8,128)(2,1)S(1)}, bf16[8,6272]{1,0:T(8,128)(2,1)S(1)}, u32[]{:S(2)}, u32[]{:S(2)}) collective-permute-start(bf16[8,6272]{1,0:T(8,128)(2,1)S(1)} %collective-permute-done.4.refs_2_), channel_id=1, source_target_pairs={{0,2},{2,4},{4,6},{6,8},{8,10},{10,12},{12,14},{14,0},{1,3},{3,5},... | collective-permute-start | bytes 301064 | tf_op jit(solution)/shard_map/ppermute | solution.py:291
  36.5 6.6 %collective-permute-start.9 = (bf16[8,6272]{1,0:T(8,128)(2,1)S(1)}, bf16[8,6272]{1,0:T(8,128)(2,1)S(1)}, u32[]{:S(2)}, u32[]{:S(2)}) collective-permute-start(bf16[8,6272]{1,0:T(8,128)(2,1)S(1)} %collective-permute-done.5.refs_3_), channel_id=1, source_target_pairs={{0,14},{2,0},{4,2},{6,4},{8,6},{10,8},{12,10},{14,12},{1,15},{3,1}... | collective-permute-start | bytes 301064 | tf_op jit(solution)/shard_map/ppermute | solution.py:291
  45.9 7.1 %collective-permute-start.12 = (bf16[80,6272]{1,0:T(8,128)(2,1)S(1)}, bf16[80,6272]{1,0:T(8,128)(2,1)S(1)}, u32[]{:S(2)}, u32[]{:S(2)}) collective-permute-start(bf16[80,6272]{1,0:T(8,128)(2,1)S(1)} %shard_map.89.near), channel_id=1, source_target_pairs={{0,1},{1,0},{2,3},{3,2},{4,5},{5,4},{6,7},{7,6},{8,9},{9,8},{10,11... | collective-permute-start | bytes 3010568 | tf_op jit(solution)/shard_map/ppermute | solution.py:287
  46.0 12.9 %collective-permute-start.14 = (bf16[8,6272]{1,0:T(8,128)(2,1)S(1)}, bf16[8,6272]{1,0:T(8,128)(2,1)S(1)}, u32[]{:S(2)}, u32[]{:S(2)}) collective-permute-start(bf16[8,6272]{1,0:T(8,128)(2,1)S(1)} %collective-permute-done.8.refs_6_), channel_id=1, source_target_pairs={{0,2},{2,4},{4,6},{6,8},{8,10},{10,12},{12,14},{14,0},{1,3},{3,5},... | collective-permute-start | bytes 301064 | tf_op jit(solution)/shard_map/ppermute | solution.py:291
  46.2 12.8 %collective-permute-start.15 = (bf16[8,6272]{1,0:T(8,128)(2,1)S(1)}, bf16[8,6272]{1,0:T(8,128)(2,1)S(1)}, u32[]{:S(2)}, u32[]{:S(2)}) collective-permute-start(bf16[8,6272]{1,0:T(8,128)(2,1)S(1)} %collective-permute-done.9.refs_7_), channel_id=1, source_target_pairs={{0,14},{2,0},{4,2},{6,4},{8,6},{10,8},{12,10},{14,12},{1,15},{3,1}... | collective-permute-start | bytes 301064 | tf_op jit(solution)/shard_map/ppermute | solution.py:291
  49.7 9.3 %collective-permute-start.16 = (bf16[8,6272]{1,0:T(8,128)(2,1)S(1)}, bf16[8,6272]{1,0:T(8,128)(2,1)S(1)}, u32[]{:S(2)}, u32[]{:S(2)}) collective-permute-start(bf16[8,6272]{1,0:T(8,128)(2,1)S(1)} %collective-permute-done.10.refs_8_), channel_id=1, source_target_pairs={{0,2},{2,4},{4,6},{6,8},{8,10},{10,12},{12,14},{14,0},{1,3},{3,5},... | collective-permute-start | bytes 301064 | tf_op jit(solution)/shard_map/ppermute | solution.py:291
  49.7 9.3 %collective-permute-start.17 = (bf16[8,6272]{1,0:T(8,128)(2,1)S(1)}, bf16[8,6272]{1,0:T(8,128)(2,1)S(1)}, u32[]{:S(2)}, u32[]{:S(2)}) collective-permute-start(bf16[8,6272]{1,0:T(8,128)(2,1)S(1)} %collective-permute-done.11.refs_9_), channel_id=1, source_target_pairs={{0,14},{2,0},{4,2},{6,4},{8,6},{10,8},{12,10},{14,12},{1,15},{3,1}... | collective-permute-start | bytes 301064 | tf_op jit(solution)/shard_map/ppermute | solution.py:291
  58.8 24.4 %collective-permute-start.13 = (bf16[80,6144]{1,0:T(8,128)(2,1)S(1)}, bf16[80,6144]{1,0:T(8,128)(2,1)S(1)}, u32[]{:S(2)}, u32[]{:S(2)}) collective-permute-start(bf16[80,6144]{1,0:T(8,128)(2,1)S(1)} %get-tuple-element.30), channel_id=1, source_target_pairs={{0,1},{1,0},{2,3},{3,2},{4,5},{5,4},{6,7},{7,6},{8,9},{9,8},{10,11... | collective-permute-start | bytes 2949128 | tf_op jit(solution)/shard_map/ppermute | solution.py:287
  59.0 8.3 %collective-permute-start.20 = (bf16[32,6272]{1,0:T(8,128)(2,1)S(1)}, bf16[32,6272]{1,0:T(8,128)(2,1)S(1)}, u32[]{:S(2)}, u32[]{:S(2)}) collective-permute-start(bf16[32,6272]{1,0:T(8,128)(2,1)S(1)} %shard_map.91.near), channel_id=1, source_target_pairs={{0,1},{1,0},{2,3},{3,2},{4,5},{5,4},{6,7},{7,6},{8,9},{9,8},{10,11... | collective-permute-start | bytes 1204232 | tf_op jit(solution)/shard_map/ppermute | solution.py:287
  59.6 6.1 %collective-permute-start.18 = (bf16[8,6272]{1,0:T(8,128)(2,1)S(1)}, bf16[8,6272]{1,0:T(8,128)(2,1)S(1)}, u32[]{:S(2)}, u32[]{:S(2)}) collective-permute-start(bf16[8,6272]{1,0:T(8,128)(2,1)S(1)} %collective-permute-done.14.refs_0_), channel_id=1, source_target_pairs={{0,2},{2,4},{4,6},{6,8},{8,10},{10,12},{12,14},{14,0},{1,3},{3,5},... | collective-permute-start | bytes 301064 | tf_op jit(solution)/shard_map/ppermute | solution.py:291
  73.0 6.2 %collective-permute-start.34 = (bf16[8,6144]{1,0:T(8,128)(2,1)S(1)}, bf16[8,6144]{1,0:T(8,128)(2,1)S(1)}, u32[]{:S(2)}, u32[]{:S(2)}) collective-permute-start(bf16[8,6144]{1,0:T(8,128)(2,1)S(1)} %shard_map.105), channel_id=1, source_target_pairs={{0,2},{2,4},{4,6},{6,8},{8,10},{10,12},{12,14},{14,0},{1,3},{3,5},... | collective-permute-start | bytes 294920 | tf_op jit(solution)/shard_map/ppermute | solution.py:291
  73.2 6.5 %collective-permute-start.24 = (bf16[8,6144]{1,0:T(8,128)(2,1)S(1)}, bf16[8,6144]{1,0:T(8,128)(2,1)S(1)}, u32[]{:S(2)}, u32[]{:S(2)}) collective-permute-start(bf16[8,6144]{1,0:T(8,128)(2,1)S(1)} %shard_map.94), channel_id=1, source_target_pairs={{0,14},{2,0},{4,2},{6,4},{8,6},{10,8},{12,10},{14,12},{1,15},{3,1}... | collective-permute-start | bytes 294920 | tf_op jit(solution)/shard_map/ppermute | solution.py:291
  76.5 6.6 %collective-permute-start.31 = (bf16[8,6144]{1,0:T(8,128)(2,1)S(1)}, bf16[8,6144]{1,0:T(8,128)(2,1)S(1)}, u32[]{:S(2)}, u32[]{:S(2)}) collective-permute-start(bf16[8,6144]{1,0:T(8,128)(2,1)S(1)} %shard_map.102), channel_id=1, source_target_pairs={{0,14},{2,0},{4,2},{6,4},{8,6},{10,8},{12,10},{14,12},{1,15},{3,1}... | collective-permute-start | bytes 294920 | tf_op jit(solution)/shard_map/ppermute | solution.py:291
  79.3 7.3 %collective-permute-start.35 = (bf16[8,6144]{1,0:T(8,128)(2,1)S(1)}, bf16[8,6144]{1,0:T(8,128)(2,1)S(1)}, u32[]{:S(2)}, u32[]{:S(2)}) collective-permute-start(bf16[8,6144]{1,0:T(8,128)(2,1)S(1)} %shard_map.106), channel_id=1, source_target_pairs={{0,2},{2,4},{4,6},{6,8},{8,10},{10,12},{12,14},{14,0},{1,3},{3,5},... | collective-permute-start | bytes 294920 | tf_op jit(solution)/shard_map/ppermute | solution.py:291
  79.7 7.0 %collective-permute-start.25 = (bf16[8,6144]{1,0:T(8,128)(2,1)S(1)}, bf16[8,6144]{1,0:T(8,128)(2,1)S(1)}, u32[]{:S(2)}, u32[]{:S(2)}) collective-permute-start(bf16[8,6144]{1,0:T(8,128)(2,1)S(1)} %shard_map.95), channel_id=1, source_target_pairs={{0,14},{2,0},{4,2},{6,4},{8,6},{10,8},{12,10},{14,12},{1,15},{3,1}... | collective-permute-start | bytes 294920 | tf_op jit(solution)/shard_map/ppermute | solution.py:291
  83.0 7.1 %collective-permute-start.28 = (bf16[8,6144]{1,0:T(8,128)(2,1)S(1)}, bf16[8,6144]{1,0:T(8,128)(2,1)S(1)}, u32[]{:S(2)}, u32[]{:S(2)}) collective-permute-start(bf16[8,6144]{1,0:T(8,128)(2,1)S(1)} %shard_map.98), channel_id=1, source_target_pairs={{0,2},{2,4},{4,6},{6,8},{8,10},{10,12},{12,14},{14,0},{1,3},{3,5},... | collective-permute-start | bytes 294920 | tf_op jit(solution)/shard_map/ppermute | solution.py:291
  83.2 7.0 %collective-permute-start.32 = (bf16[8,6144]{1,0:T(8,128)(2,1)S(1)}, bf16[8,6144]{1,0:T(8,128)(2,1)S(1)}, u32[]{:S(2)}, u32[]{:S(2)}) collective-permute-start(bf16[8,6144]{1,0:T(8,128)(2,1)S(1)} %shard_map.103), channel_id=1, source_target_pairs={{0,14},{2,0},{4,2},{6,4},{8,6},{10,8},{12,10},{14,12},{1,15},{3,1}... | collective-permute-start | bytes 294920 | tf_op jit(solution)/shard_map/ppermute | solution.py:291
  86.6 7.0 %collective-permute-start.36 = (bf16[8,6144]{1,0:T(8,128)(2,1)S(1)}, bf16[8,6144]{1,0:T(8,128)(2,1)S(1)}, u32[]{:S(2)}, u32[]{:S(2)}) collective-permute-start(bf16[8,6144]{1,0:T(8,128)(2,1)S(1)} %shard_map.107), channel_id=1, source_target_pairs={{0,2},{2,4},{4,6},{6,8},{8,10},{10,12},{12,14},{14,0},{1,3},{3,5},... | collective-permute-start | bytes 294920 | tf_op jit(solution)/shard_map/ppermute | solution.py:291
  86.8 7.0 %collective-permute-start.26 = (bf16[8,6144]{1,0:T(8,128)(2,1)S(1)}, bf16[8,6144]{1,0:T(8,128)(2,1)S(1)}, u32[]{:S(2)}, u32[]{:S(2)}) collective-permute-start(bf16[8,6144]{1,0:T(8,128)(2,1)S(1)} %shard_map.96), channel_id=1, source_target_pairs={{0,14},{2,0},{4,2},{6,4},{8,6},{10,8},{12,10},{14,12},{1,15},{3,1}... | collective-permute-start | bytes 294920 | tf_op jit(solution)/shard_map/ppermute | solution.py:291
  90.1 7.0 %collective-permute-start.29 = (bf16[8,6144]{1,0:T(8,128)(2,1)S(1)}, bf16[8,6144]{1,0:T(8,128)(2,1)S(1)}, u32[]{:S(2)}, u32[]{:S(2)}) collective-permute-start(bf16[8,6144]{1,0:T(8,128)(2,1)S(1)} %shard_map.99), channel_id=1, source_target_pairs={{0,2},{2,4},{4,6},{6,8},{8,10},{10,12},{12,14},{14,0},{1,3},{3,5},... | collective-permute-start | bytes 294920 | tf_op jit(solution)/shard_map/ppermute | solution.py:291
  90.3 7.0 %collective-permute-start.33 = (bf16[8,6144]{1,0:T(8,128)(2,1)S(1)}, bf16[8,6144]{1,0:T(8,128)(2,1)S(1)}, u32[]{:S(2)}, u32[]{:S(2)}) collective-permute-start(bf16[8,6144]{1,0:T(8,128)(2,1)S(1)} %shard_map.104), channel_id=1, source_target_pairs={{0,14},{2,0},{4,2},{6,4},{8,6},{10,8},{12,10},{14,12},{1,15},{3,1}... | collective-permute-start | bytes 294920 | tf_op jit(solution)/shard_map/ppermute | solution.py:291
  93.9 7.3 %collective-permute-start.27 = (bf16[8,6144]{1,0:T(8,128)(2,1)S(1)}, bf16[8,6144]{1,0:T(8,128)(2,1)S(1)}, u32[]{:S(2)}, u32[]{:S(2)}) collective-permute-start(bf16[8,6144]{1,0:T(8,128)(2,1)S(1)} %shard_map.97), channel_id=1, source_target_pairs={{0,14},{2,0},{4,2},{6,4},{8,6},{10,8},{12,10},{14,12},{1,15},{3,1}... | collective-permute-start | bytes 294920 | tf_op jit(solution)/shard_map/ppermute | solution.py:291
  104.6 7.7 %collective-permute-start.39 = (bf16[2,6144]{1,0:T(2,128)(2,1)S(1)}, bf16[2,6144]{1,0:T(2,128)(2,1)S(1)}, u32[]{:S(2)}, u32[]{:S(2)}) collective-permute-start(bf16[2,6144]{1,0:T(2,128)(2,1)S(1)} %get-tuple-element.38), channel_id=1, source_target_pairs={{0,96},{32,0},{64,32},{96,64},{1,97},{33,1},{65,33},{97,65},{2,98}... | collective-permute-start | bytes 73736 | tf_op jit(solution)/shard_map/ppermute | solution.py:283
  108.1 7.7 %collective-permute-start.40 = (bf16[2,6144]{1,0:T(2,128)(2,1)S(1)}, bf16[2,6144]{1,0:T(2,128)(2,1)S(1)}, u32[]{:S(2)}, u32[]{:S(2)}) collective-permute-start(bf16[2,6144]{1,0:T(2,128)(2,1)S(1)} %get-tuple-element.39), channel_id=1, source_target_pairs={{0,64},{32,96},{64,0},{96,32},{1,65},{33,97},{65,1},{97,33},{2,66}... | collective-permute-start | bytes 73736 | tf_op jit(solution)/shard_map/ppermute | solution.py:283
  (10 other events, 49.4 us)
where the time goes:
time: 119 us
  starting transfers between devices  81.7 us (69%)
  waiting for transfers between devices  20.9 us (18%)
  Pallas kernels  15.5 us (13%)
    ppermute x28, starting transfers between devices, along(): lax.ppermute(value, 'y', [(y, (y + step) % RING) for y in range(RING)])  46.1 us
    ppermute x8, starting transfers between devices, swap(): return lax.ppermute(value, axis, [(0, 1), (1, 0)])  18.5 us
    ppermute x6, starting transfers between devices, to_expert(): lax.ppermute(value, 'xo', [(i, (i + step) % EXPERTS) for i in range(EXPER...  17 us
    ppermute x28, waiting for transfers between devices, along(): lax.ppermute(value, 'y', [(y, (y + step) % RING) for y in range(RING)])  10.7 us
    pallas_call x2, Pallas kernels, expert(): pl.pallas_call(kernel, out_shape=[shape(n, width, dtype) for dtype in (F3...  9.53 us
    ppermute x6, waiting for transfers between devices, to_expert(): lax.ppermute(value, 'xo', [(i, (i + step) % EXPERTS) for i in range(EXPER...  5.94 us
    ppermute x8, waiting for transfers between devices, swap(): return lax.ppermute(value, axis, [(0, 1), (1, 0)])  4.27 us
    pallas_call x23, Pallas kernels, call(): pl.pallas_call(kernel, out_shape=outs, in_specs=in_specs or vmem(len(args...  3.07 us
  transfers between devices with their start and end apart: 42, of which 10 were waited for; matrix products, arithmetic and copies ran while one was open for 0% of the time, Pallas kernels for 11%

commit v1 on v0

--- a/solution.py
+++ b/solution.py
@@ -13,8 +13,6 @@
 CAP = 2
 PAIR, RING, CORES = 2, 8, 2
 LANES = 128
-CUTS = 1
-STEP = 64
 EXPERT = ("xo", "xi", "y", "core")
 GROUPS_EXPERT = ("groups",) + EXPERT
 F32, BF16 = jnp.float32, jnp.bfloat16
@@ -22,7 +20,7 @@
 REACH = {(0, 1): HALF, (0, -1): HALF - 1, (1, 1): HALF - 1, (1, -1): HALF}
 GROUPS = [
     [(b, sign, d) for d in distances for b in (0, 1) for sign in (1, -1) if d <= REACH[b, sign]]
-    for distances in ((1, 2), (3,), (4,))
+    for distances in ((1,), (2,), (3,), (4,))
 ]
 
 
@@ -156,68 +154,43 @@
         start += ref.shape[0]
 
 
-def deep_dot(x_ref, weight_ref, cuts=CUTS):
-    depth = weight_ref.shape[0] // cuts
-    total = None
-    for n in range(cuts):
-        at = slice(n * depth, (n + 1) * depth)
-        value = jnp.dot(x_ref[:, at], weight_ref[at, :], preferred_element_type=F32)
-        total = value if n == 0 else total + value
-    return total
-
-
-def expert_rows(near, far, x_ref, hidden_ref, gate_ref, up_ref, down_ref, outs, lanes, ready):
-    width = down_ref.shape[1]
+def expert_kernel(scale, groups, *refs):
+    blocks, (gate, down, up_hbm) = refs[: 2 * groups], refs[2 * groups : 2 * groups + 3]
+    refs = refs[2 * groups + 3 :]
+    outs, balance_ref = refs[: 2 * groups], refs[2 * groups]
+    x_ref, hidden_ref, up, sem = refs[2 * groups + 1 :]
+    width = down.shape[1]
+    copy = pltpu.make_async_copy(up_hbm, up, sem.at[0])
+    copy.start()
     start = 0
     total = jnp.zeros((8, LANES), F32)
-    for block in near + far:
+    for block in blocks:
         rows = block.shape[0]
         x_ref[start : start + rows, :] = block[:, :width]
         start += rows
         for n in range(0, rows, 8):
             total = total + block[n : n + 8, width:].astype(F32)
-    lanes(total)
-    gate = deep_dot(x_ref, gate_ref)
-    ready()
-    up = deep_dot(x_ref, up_ref)
-    hidden_ref[...] = (gate * jax.nn.sigmoid(gate) * up).astype(BF16)
+    parity = lax.broadcasted_iota(jnp.int32, total.shape, 0) % 2
+    named = jnp.sum(jnp.where(parity == 0, total, 0.0), axis=0, keepdims=True)
+    probs = jnp.sum(jnp.where(parity == 1, total, 0.0), axis=0, keepdims=True)
+    balance_ref[...] = jnp.sum(named * probs, axis=1, keepdims=True) * scale
+
+    gate_pre = jnp.dot(x_ref[...], gate[...], preferred_element_type=F32)
+    copy.wait()
+    up_pre = jnp.dot(x_ref[...], up[...], preferred_element_type=F32)
+    hidden_ref[...] = (gate_pre * jax.nn.sigmoid(gate_pre) * up_pre).astype(BF16)
     tile = 512
 
-    def down(i, carry):
+    def lower(i, carry):
         at = pl.ds(pl.multiple_of(i * tile, tile), tile)
-        value = jnp.dot(hidden_ref[...], down_ref[:, at], preferred_element_type=F32)
+        value = jnp.dot(hidden_ref[...], down[:, at], preferred_element_type=F32)
         start = 0
         for out in outs:
             out[:, at] = value[start : start + out.shape[0], :].astype(out.dtype)
             start += out.shape[0]
         return carry
 
-    lax.fori_loop(0, width // tile, down, 0)
-
-
-def first_kernel(near, far, gate, down, up_hbm, kept, sent, up_ref, total_ref, x, hidden, sem):
-    copy = pltpu.make_async_copy(up_hbm, up_ref, sem.at[0])
-    copy.start()
-
-    def lanes(total):
-        total_ref[...] = total
-
-    expert_rows([near], [far], x, hidden, gate, up_ref, down, [kept, sent], lanes, copy.wait)
-
-
-def second_kernel(scale, near, near_4, far, far_4, gate, up, down, before, *refs):
-    outs, balance_ref, x, hidden = refs[:4], refs[4], refs[5], refs[6]
-
-    def lanes(total):
-        total = before[...] + total
-        parity = lax.broadcasted_iota(jnp.int32, total.shape, 0) % 2
-        named = jnp.sum(jnp.where(parity == 0, total, 0.0), axis=0, keepdims=True)
-        probs = jnp.sum(jnp.where(parity == 1, total, 0.0), axis=0, keepdims=True)
-        balance_ref[...] = jnp.sum(named * probs, axis=1, keepdims=True) * scale
-
-    expert_rows(
-        [near, near_4], [far, far_4], x, hidden, gate, up, down, outs, lanes, lambda: None
-    )
+    lax.fori_loop(0, width // tile, lower, 0)
 
 
 def fetch_kernel(*refs):
@@ -341,42 +314,28 @@
     total_tokens = count * devices
     scale = EXPERTS / (2.0 * total_tokens * total_tokens)
 
-    def expert(kernel, rows, args, in_specs, outs, scratch=()):
-        return pl.pallas_call(
-            kernel,
-            out_shape=[shape(n, width, dtype) for dtype in (F32, BF16) for n in rows] + outs,
-            in_specs=in_specs,
-            out_specs=vmem(2 * len(rows) + len(outs)),
-            scratch_shapes=[
-                pltpu.VMEM((-(-2 * sum(rows) // STEP) * STEP, width), BF16),
-                pltpu.VMEM((-(-2 * sum(rows) // STEP) * STEP, units), BF16),
-                *scratch,
-            ],
-            cost_estimate=pl.CostEstimate(
-                flops=12 * sum(rows) * width * units, bytes_accessed=9_000_000, transcendentals=0
-            ),
-            compiler_params=pltpu.CompilerParams(vmem_limit_bytes=24 << 20),
-        )(*args)
-
-    *first, up_near, total = expert(
-        first_kernel,
-        rows[:1],
-        (near[0], far[0], gate_near, down_near, in_hbm(up_weight)),
-        vmem(4) + [hbm],
-        [pltpu.VMEM(up_weight.shape, BF16), shape(8, LANES, F32)],
-        [pltpu.SemaphoreType.DMA((1,))],
-    )
-    *second, balance = expert(
-        functools.partial(second_kernel, scale),
-        rows[1:],
-        (*near[1:], *far[1:], gate_near, up_near, down_near, total),
-        vmem(8),
-        [shape(1, 1, F32)],
-    )
-    balance = balance.reshape(1)
-    kept = [first[0], second[0], second[1]]
+    groups = len(GROUPS)
+    outs = pl.pallas_call(
+        functools.partial(expert_kernel, scale, groups),
+        out_shape=[shape(n, width, dtype) for dtype in (F32, BF16) for n in rows]
+        + [shape(1, 1, F32)],
+        in_specs=vmem(2 * groups + 2) + [hbm],
+        out_specs=vmem(2 * groups + 1),
+        scratch_shapes=[
+            pltpu.VMEM((2 * sum(rows), width), BF16),
+            pltpu.VMEM((2 * sum(rows), units), BF16),
+            pltpu.VMEM((width, units), BF16),
+            pltpu.SemaphoreType.DMA((1,)),
+        ],
+        cost_estimate=pl.CostEstimate(
+            flops=12 * sum(rows) * width * units, bytes_accessed=9_000_000, transcendentals=0
+        ),
+        compiler_params=pltpu.CompilerParams(vmem_limit_bytes=12 << 20),
+    )(*near, *far, gate_near, down_near, in_hbm(up_weight))
+    kept, sent = outs[:groups], outs[groups : 2 * groups]
+    balance = outs[2 * groups].reshape(1)
     crossed = {}
-    for group, value in ((2, second[3]), (1, second[2]), (0, first[1])):
+    for group, value in reversed(list(enumerate(sent))):
         crossed[group] = swap(value, "core")
 
     moving = {}

time: 119 us -> 118 us (level)
  starting transfers between devices: 81.7 us -> 75.2 us
  waiting for transfers between devices: 20.9 us -> 27.4 us
    ppermute x28, starting transfers between devices: 46.1 us -> 39.3 us  [along(): lax.ppermute(value, 'y', [(y, (y + step) % RING) for y in range(RING)])]
    ppermute x28, waiting for transfers between devices: 10.7 us -> 16.2 us  [along(): lax.ppermute(value, 'y', [(y, (y + step) % RING) for y in range(RING)])]
    ppermute x8 -> x10, waiting for transfers between devices: 4.27 us -> 5.28 us  [swap(): return lax.ppermute(value, axis, [(0, 1), (1, 0)])]
    pallas_call x2 -> x1, Pallas kernels: 9.53 us -> 8.58 us  [local(): pl.pallas_call(functools.partial(expert_kernel, scale, groups), out_shape...]
    ppermute x8 -> x10, starting transfers between devices: 18.5 us -> 18.8 us  [swap(): return lax.ppermute(value, axis, [(0, 1), (1, 0)])]
    pallas_call x23 -> x24, Pallas kernels: 3.07 us -> 3.05 us  [call(): pl.pallas_call(kernel, out_shape=outs, in_specs=in_specs or vmem(len(args...]
  transfers between devices with their start and end apart: 42 -> 44, of which waited for: 10 -> 18; matrix products, arithmetic and copies ran while one was open for 0% -> 0% of each run, Pallas kernels for 11% -> 3%
where the time goes in v1:
time: 118 us
  starting transfers between devices  75.2 us (64%)
  waiting for transfers between devices  27.4 us (23%)
  Pallas kernels  14.5 us (12%)
    ppermute x28, starting transfers between devices, along(): lax.ppermute(value, 'y', [(y, (y + step) % RING) for y in range(RING)])  39.3 us
    ppermute x10, starting transfers between devices, swap(): return lax.ppermute(value, axis, [(0, 1), (1, 0)])  18.8 us
    ppermute x6, starting transfers between devices, to_expert(): lax.ppermute(value, 'xo', [(i, (i + step) % EXPERTS) for i in range(EXPER...  17.1 us
    ppermute x28, waiting for transfers between devices, along(): lax.ppermute(value, 'y', [(y, (y + step) % RING) for y in range(RING)])  16.2 us
    pallas_call x1, Pallas kernels, local(): pl.pallas_call(functools.partial(expert_kernel, scale, groups), out_shape...  8.58 us
    ppermute x6, waiting for transfers between devices, to_expert(): lax.ppermute(value, 'xo', [(i, (i + step) % EXPERTS) for i in range(EXPER...  5.94 us
    ppermute x10, waiting for transfers between devices, swap(): return lax.ppermute(value, axis, [(0, 1), (1, 0)])  5.28 us
    pallas_call x24, Pallas kernels, call(): pl.pallas_call(kernel, out_shape=outs, in_specs=in_specs or vmem(len(args...  3.05 us
  transfers between devices with their start and end apart: 44, of which 18 were waited for; matrix products, arithmetic and copies ran while one was open for 0% of the time, Pallas kernels for 3%

profile of v1, /device:TPU:514, one launch (start us, length us, event | category | flops | bytes accessed | tf_op | source)
XLA Modules:
  0.0 118.1 jit_solution(841952495878896046)
XLA Ops:
  0.6 1.4 %shard_map.86 = (bf16[2,6272]{1,0:T(2,128)(2,1)S(1)}, bf16[2,6272]{1,0:T(2,128)(2,1)S(1)}, bf16[2,6272]{1,0:T(2,128)(2,1)S(1)}, bf16[2,6272]{1,0:T(2,128)(2,1)S(1)}, f32[4,128]{1,0:T(4,128)S(1)}) custom-call(s32[2,4]{1,0:T(2,128)} %bitcast.5, s32[2,4]{1,0:T(2,128)} %bitcast.6, bf16[4,6144]{1,0:T(4,128)(2,1)} %tok_hbm.1, bf16[4,6144]{1,0:T(4,128)(2,1)} %bitcast.4), custom_call_target="tpu_custom_call" | custom-call | flops 200000 | bytes 1000000 | tf_op jit(solution)/shard_map/pallas_call | solution.py:33
  2.1 2.8 %collective-permute-start = (bf16[2,6272]{1,0:T(2,128)(2,1)S(1)}, bf16[2,6272]{1,0:T(2,128)(2,1)S(1)}, u32[]{:S(2)}, u32[]{:S(2)}) collective-permute-start(bf16[2,6272]{1,0:T(2,128)(2,1)S(1)} %get-tuple-element.24), channel_id=1, source_target_pairs={{0,32},{32,64},{64,96},{96,0},{1,33},{33,65},{65,97},{97,1},{2,34}... | collective-permute-start | bytes 75272 | tf_op jit(solution)/shard_map/ppermute | solution.py:256
  4.9 3.3 %collective-permute-start.1 = (bf16[2,6272]{1,0:T(2,128)(2,1)S(1)}, bf16[2,6272]{1,0:T(2,128)(2,1)S(1)}, u32[]{:S(2)}, u32[]{:S(2)}) collective-permute-start(bf16[2,6272]{1,0:T(2,128)(2,1)S(1)} %get-tuple-element.25), channel_id=1, source_target_pairs={{0,64},{32,96},{64,0},{96,32},{1,65},{33,97},{65,1},{97,33},{2,66}... | collective-permute-start | bytes 75272 | tf_op jit(solution)/shard_map/ppermute | solution.py:256
  8.2 3.2 %collective-permute-start.2 = (bf16[2,6272]{1,0:T(2,128)(2,1)S(1)}, bf16[2,6272]{1,0:T(2,128)(2,1)S(1)}, u32[]{:S(2)}, u32[]{:S(2)}) collective-permute-start(bf16[2,6272]{1,0:T(2,128)(2,1)S(1)} %get-tuple-element.26), channel_id=1, source_target_pairs={{0,96},{32,0},{64,32},{96,64},{1,97},{33,1},{65,33},{97,65},{2,98}... | collective-permute-start | bytes 75272 | tf_op jit(solution)/shard_map/ppermute | solution.py:256
  11.4 2.9 %shard_map.87 = (bf16[6144,256]{1,0:T(8,128)(2,1)S(1)}, bf16[256,6144]{1,0:T(8,128)(2,1)S(1)}) custom-call(bf16[6144,256]{1,0:T(8,128)(2,1)} %refs_0_.1, bf16[256,6144]{1,0:T(8,128)(2,1)} %refs_1_.1, bf16[2,6272]{1,0:T(2,128)(2,1)S(1)} %get-tuple-element.23.refs_2_.own), custom_call_target="tpu_custom_call" | custom-call | flops 1000000 | bytes 12582912 | tf_op jit(solution)/shard_map/pallas_call | solution.py:208
  14.4 15.6 %collective-permute-start.3 = (bf16[8,6272]{1,0:T(8,128)(2,1)S(1)}, bf16[8,6272]{1,0:T(8,128)(2,1)S(1)}, u32[]{:S(2)}, u32[]{:S(2)}) collective-permute-start(bf16[8,6272]{1,0:T(8,128)(2,1)S(1)} %shard_map.88.refs_0_), channel_id=1, source_target_pairs={{0,16},{16,0},{1,17},{17,1},{2,18},{18,2},{3,19},{19,3},{4,20},{20... | collective-permute-start | bytes 301064 | tf_op jit(solution)/shard_map/ppermute | solution.py:260
  30.1 2.0 %collective-permute-start.4 = (bf16[8,6272]{1,0:T(8,128)(2,1)S(1)}, bf16[8,6272]{1,0:T(8,128)(2,1)S(1)}, u32[]{:S(2)}, u32[]{:S(2)}) collective-permute-start(bf16[8,6272]{1,0:T(8,128)(2,1)S(1)} %shard_map.88.refs_0_), channel_id=1, source_target_pairs={{0,2},{2,4},{4,6},{6,8},{8,10},{10,12},{12,14},{14,0},{1,3},{3,5},... | collective-permute-start | bytes 301064 | tf_op jit(solution)/shard_map/ppermute | solution.py:264
  33.3 1.4 %collective-permute-start.6 = (bf16[8,6272]{1,0:T(8,128)(2,1)S(1)}, bf16[8,6272]{1,0:T(8,128)(2,1)S(1)}, u32[]{:S(2)}, u32[]{:S(2)}) collective-permute-start(bf16[8,6272]{1,0:T(8,128)(2,1)S(1)} %collective-permute-done.3.refs_1_), channel_id=1, source_target_pairs={{0,2},{2,4},{4,6},{6,8},{8,10},{10,12},{12,14},{14,0},{1,3},{3,5},... | collective-permute-start | bytes 301064 | tf_op jit(solution)/shard_map/ppermute | solution.py:264
  35.1 1.4 %collective-permute-start.9 = (bf16[8,6272]{1,0:T(8,128)(2,1)S(1)}, bf16[8,6272]{1,0:T(8,128)(2,1)S(1)}, u32[]{:S(2)}, u32[]{:S(2)}) collective-permute-start(bf16[8,6272]{1,0:T(8,128)(2,1)S(1)} %collective-permute-done.5.refs_3_), channel_id=1, source_target_pairs={{0,14},{2,0},{4,2},{6,4},{8,6},{10,8},{12,10},{14,12},{1,15},{3,1}... | collective-permute-start | bytes 301064 | tf_op jit(solution)/shard_map/ppermute | solution.py:264
  37.3 2.6 %collective-permute-start.11 = (bf16[8,6272]{1,0:T(8,128)(2,1)S(1)}, bf16[8,6272]{1,0:T(8,128)(2,1)S(1)}, u32[]{:S(2)}, u32[]{:S(2)}) collective-permute-start(bf16[8,6272]{1,0:T(8,128)(2,1)S(1)} %collective-permute-done.7.refs_5_), channel_id=1, source_target_pairs={{0,14},{2,0},{4,2},{6,4},{8,6},{10,8},{12,10},{14,12},{1,15},{3,1}... | collective-permute-start | bytes 301064 | tf_op jit(solution)/shard_map/ppermute | solution.py:264
  40.4 3.3 %collective-permute-start.13 = (bf16[8,6272]{1,0:T(8,128)(2,1)S(1)}, bf16[8,6272]{1,0:T(8,128)(2,1)S(1)}, u32[]{:S(2)}, u32[]{:S(2)}) collective-permute-start(bf16[8,6272]{1,0:T(8,128)(2,1)S(1)} %collective-permute-done.9.refs_1_), channel_id=1, source_target_pairs={{0,14},{2,0},{4,2},{6,4},{8,6},{10,8},{12,10},{14,12},{1,15},{3,1}... | collective-permute-start | bytes 301064 | tf_op jit(solution)/shard_map/ppermute | solution.py:264
  43.8 3.2 %collective-permute-start.15 = (bf16[8,6272]{1,0:T(8,128)(2,1)S(1)}, bf16[8,6272]{1,0:T(8,128)(2,1)S(1)}, u32[]{:S(2)}, u32[]{:S(2)}) collective-permute-start(bf16[8,6272]{1,0:T(8,128)(2,1)S(1)} %collective-permute-done.11.refs_3_), channel_id=1, source_target_pairs={{0,14},{2,0},{4,2},{6,4},{8,6},{10,8},{12,10},{14,12},{1,15},{3,1}... | collective-permute-start | bytes 301064 | tf_op jit(solution)/shard_map/ppermute | solution.py:264
  47.2 2.6 %collective-permute-done.12.refs_0_ = bf16[8,6272]{1,0:T(8,128)(2,1)S(1)} collective-permute-done((bf16[8,6272]{1,0:T(8,128)(2,1)S(1)}, bf16[8,6272]{1,0:T(8,128)(2,1)S(1)}, u32[]{:S(2)}, u32[]{:S(2)}) %collective-permute-start.12) | collective-permute-done | bytes 100384 | tf_op jit(solution)/shard_map/ppermute | solution.py:264
  49.8 3.1 %collective-permute-done.14.refs_2_ = bf16[8,6272]{1,0:T(8,128)(2,1)S(1)} collective-permute-done((bf16[8,6272]{1,0:T(8,128)(2,1)S(1)}, bf16[8,6272]{1,0:T(8,128)(2,1)S(1)}, u32[]{:S(2)}, u32[]{:S(2)}) %collective-permute-start.14) | collective-permute-done | bytes 100384 | tf_op jit(solution)/shard_map/ppermute | solution.py:264
  53.2 3.2 %collective-permute-start.17 = (bf16[8,6272]{1,0:T(8,128)(2,1)S(1)}, bf16[8,6272]{1,0:T(8,128)(2,1)S(1)}, u32[]{:S(2)}, u32[]{:S(2)}) collective-permute-start(bf16[8,6272]{1,0:T(8,128)(2,1)S(1)} %collective-permute-done.15.refs_3_), channel_id=1, source_target_pairs={{0,14},{2,0},{4,2},{6,4},{8,6},{10,8},{12,10},{14,12},{1,15},{3,1}... | collective-permute-start | bytes 301064 | tf_op jit(solution)/shard_map/ppermute | solution.py:264
  56.4 3.1 %collective-permute-done.16.refs_0_ = bf16[8,6272]{1,0:T(8,128)(2,1)S(1)} collective-permute-done((bf16[8,6272]{1,0:T(8,128)(2,1)S(1)}, bf16[8,6272]{1,0:T(8,128)(2,1)S(1)}, u32[]{:S(2)}, u32[]{:S(2)}) %collective-permute-start.16) | collective-permute-done | bytes 100384 | tf_op jit(solution)/shard_map/ppermute | solution.py:264
  59.7 1.4 %collective-permute-done.21.refs_7_ = bf16[16,6272]{1,0:T(8,128)(2,1)S(1)} collective-permute-done((bf16[16,6272]{1,0:T(8,128)(2,1)S(1)}, bf16[16,6272]{1,0:T(8,128)(2,1)S(1)}, u32[]{:S(2)}, u32[]{:S(2)}) %collective-permute-start.21) | collective-permute-done | bytes 200736 | tf_op jit(solution)/shard_map/ppermute | solution.py:260
  61.1 8.6 %shard_map.93 = (f32[48,6144]{1,0:T(8,128)S(1)}, f32[32,6144]{1,0:T(8,128)S(1)}, f32[32,6144]{1,0:T(8,128)S(1)}, f32[16,6144]{1,0:T(8,128)S(1)}, bf16[48,6144]{1...) custom-call(bf16[48,6272]{1,0:T(8,128)(2,1)S(1)} %shard_map.89.refs_, ...), custom_call_target="tpu_custom_call" | custom-call | flops 2415919104 | bytes 9000000 | tf_op jit(solution)/shard_map/pallas_call | solution.py:318
  70.8 2.4 %collective-permute-done.25.crossed_ref = bf16[16,6144]{1,0:T(8,128)(2,1)S(1)} collective-permute-done((bf16[16,6144]{1,0:T(8,128)(2,1)S(1)}, bf16[16,6144]{1,0:T(8,128)(2,1)S(1)}, u32[]{:S(2)}, u32[]{:S(2)}) %collective-permute-start.25) | collective-permute-done | bytes 196640 | tf_op jit(solution)/shard_map/ppermute | solution.py:260
  73.4 3.3 %collective-permute-start.26 = (bf16[8,6144]{1,0:T(8,128)(2,1)S(1)}, bf16[8,6144]{1,0:T(8,128)(2,1)S(1)}, u32[]{:S(2)}, u32[]{:S(2)}) collective-permute-start(bf16[8,6144]{1,0:T(8,128)(2,1)S(1)} %shard_map.94), channel_id=1, source_target_pairs={{0,14},{2,0},{4,2},{6,4},{8,6},{10,8},{12,10},{14,12},{1,15},{3,1}... | collective-permute-start | bytes 294920 | tf_op jit(solution)/shard_map/ppermute | solution.py:264
  76.7 1.8 %collective-permute-start.33 = (bf16[8,6144]{1,0:T(8,128)(2,1)S(1)}, bf16[8,6144]{1,0:T(8,128)(2,1)S(1)}, u32[]{:S(2)}, u32[]{:S(2)}) collective-permute-start(bf16[8,6144]{1,0:T(8,128)(2,1)S(1)} %shard_map.102), channel_id=1, source_target_pairs={{0,14},{2,0},{4,2},{6,4},{8,6},{10,8},{12,10},{14,12},{1,15},{3,1}... | collective-permute-start | bytes 294920 | tf_op jit(solution)/shard_map/ppermute | solution.py:264
  80.0 3.3 %collective-permute-start.27 = (bf16[8,6144]{1,0:T(8,128)(2,1)S(1)}, bf16[8,6144]{1,0:T(8,128)(2,1)S(1)}, u32[]{:S(2)}, u32[]{:S(2)}) collective-permute-start(bf16[8,6144]{1,0:T(8,128)(2,1)S(1)} %shard_map.95), channel_id=1, source_target_pairs={{0,14},{2,0},{4,2},{6,4},{8,6},{10,8},{12,10},{14,12},{1,15},{3,1}... | collective-permute-start | bytes 294920 | tf_op jit(solution)/shard_map/ppermute | solution.py:264
  83.4 2.1 %collective-permute-start.34 = (bf16[8,6144]{1,0:T(8,128)(2,1)S(1)}, bf16[8,6144]{1,0:T(8,128)(2,1)S(1)}, u32[]{:S(2)}, u32[]{:S(2)}) collective-permute-start(bf16[8,6144]{1,0:T(8,128)(2,1)S(1)} %shard_map.103), channel_id=1, source_target_pairs={{0,14},{2,0},{4,2},{6,4},{8,6},{10,8},{12,10},{14,12},{1,15},{3,1}... | collective-permute-start | bytes 294920 | tf_op jit(solution)/shard_map/ppermute | solution.py:264
  87.3 3.3 %collective-permute-start.28 = (bf16[8,6144]{1,0:T(8,128)(2,1)S(1)}, bf16[8,6144]{1,0:T(8,128)(2,1)S(1)}, u32[]{:S(2)}, u32[]{:S(2)}) collective-permute-start(bf16[8,6144]{1,0:T(8,128)(2,1)S(1)} %shard_map.96), channel_id=1, source_target_pairs={{0,14},{2,0},{4,2},{6,4},{8,6},{10,8},{12,10},{14,12},{1,15},{3,1}... | collective-permute-start | bytes 294920 | tf_op jit(solution)/shard_map/ppermute | solution.py:264
  93.0 3.6 %collective-permute-start.29 = (bf16[8,6144]{1,0:T(8,128)(2,1)S(1)}, bf16[8,6144]{1,0:T(8,128)(2,1)S(1)}, u32[]{:S(2)}, u32[]{:S(2)}) collective-permute-start(bf16[8,6144]{1,0:T(8,128)(2,1)S(1)} %shard_map.97), channel_id=1, source_target_pairs={{0,14},{2,0},{4,2},{6,4},{8,6},{10,8},{12,10},{14,12},{1,15},{3,1}... | collective-permute-start | bytes 294920 | tf_op jit(solution)/shard_map/ppermute | solution.py:264
  96.8 1.9 %collective-permute-done.39.refs_1_ = bf16[8,6144]{1,0:T(8,128)(2,1)S(1)} collective-permute-done((bf16[8,6144]{1,0:T(8,128)(2,1)S(1)}, bf16[8,6144]{1,0:T(8,128)(2,1)S(1)}, u32[]{:S(2)}, u32[]{:S(2)}) %collective-permute-start.39) | collective-permute-done | bytes 98336 | tf_op jit(solution)/shard_map/ppermute | solution.py:264
  98.7 1.5 %collective-permute-start.40 = (bf16[8,6144]{1,0:T(8,128)(2,1)S(1)}, bf16[8,6144]{1,0:T(8,128)(2,1)S(1)}, u32[]{:S(2)}, u32[]{:S(2)}) collective-permute-start(bf16[8,6144]{1,0:T(8,128)(2,1)S(1)} %shard_map.109), channel_id=1, source_target_pairs={{0,16},{16,0},{1,17},{17,1},{2,18},{18,2},{3,19},{19,3},{4,20},{20... | collective-permute-start | bytes 294920 | tf_op jit(solution)/shard_map/ppermute | solution.py:260
  100.2 2.3 %collective-permute-done.32.refs_1_ = bf16[8,6144]{1,0:T(8,128)(2,1)S(1)} collective-permute-done((bf16[8,6144]{1,0:T(8,128)(2,1)S(1)}, bf16[8,6144]{1,0:T(8,128)(2,1)S(1)}, u32[]{:S(2)}, u32[]{:S(2)}) %collective-permute-start.32) | collective-permute-done | bytes 98336 | tf_op jit(solution)/shard_map/ppermute | solution.py:264
  103.5 3.4 %collective-permute-start.41 = (bf16[2,6144]{1,0:T(2,128)(2,1)S(1)}, bf16[2,6144]{1,0:T(2,128)(2,1)S(1)}, u32[]{:S(2)}, u32[]{:S(2)}) collective-permute-start(bf16[2,6144]{1,0:T(2,128)(2,1)S(1)} %get-tuple-element.38), channel_id=1, source_target_pairs={{0,96},{32,0},{64,32},{96,64},{1,97},{33,1},{65,33},{97,65},{2,98}... | collective-permute-start | bytes 73736 | tf_op jit(solution)/shard_map/ppermute | solution.py:256
  106.9 4.3 %collective-permute-start.42 = (bf16[2,6144]{1,0:T(2,128)(2,1)S(1)}, bf16[2,6144]{1,0:T(2,128)(2,1)S(1)}, u32[]{:S(2)}, u32[]{:S(2)}) collective-permute-start(bf16[2,6144]{1,0:T(2,128)(2,1)S(1)} %get-tuple-element.39), channel_id=1, source_target_pairs={{0,64},{32,96},{64,0},{96,32},{1,65},{33,97},{65,1},{97,33},{2,66}... | collective-permute-start | bytes 73736 | tf_op jit(solution)/shard_map/ppermute | solution.py:256
  111.2 3.4 %collective-permute-done.42.r2 = bf16[2,6144]{1,0:T(2,128)(2,1)S(1)} collective-permute-done((bf16[2,6144]{1,0:T(2,128)(2,1)S(1)}, bf16[2,6144]{1,0:T(2,128)(2,1)S(1)}, u32[]{:S(2)}, u32[]{:S(2)}) %collective-permute-start.42) | collective-permute-done | bytes 24608 | tf_op jit(solution)/shard_map/ppermute | solution.py:256
  114.6 2.5 %collective-permute-done.43.r3 = bf16[2,6144]{1,0:T(2,128)(2,1)S(1)} collective-permute-done((bf16[2,6144]{1,0:T(2,128)(2,1)S(1)}, bf16[2,6144]{1,0:T(2,128)(2,1)S(1)}, u32[]{:S(2)}, u32[]{:S(2)}) %collective-permute-start.43) | collective-permute-done | bytes 24608 | tf_op jit(solution)/shard_map/ppermute | solution.py:256
  (82 shorter events, 12.5 us)
Async XLA Ops:
  2.1 12.2 %collective-permute-start = (bf16[2,6272]{1,0:T(2,128)(2,1)S(1)}, bf16[2,6272]{1,0:T(2,128)(2,1)S(1)}, u32[]{:S(2)}, u32[]{:S(2)}) collective-permute-start(bf16[2,6272]{1,0:T(2,128)(2,1)S(1)} %get-tuple-element.24), channel_id=1, source_target_pairs={{0,32},{32,64},{64,96},{96,0},{1,33},{33,65},{65,97},{97,1},{2,34}... | collective-permute-start | bytes 75272 | tf_op jit(solution)/shard_map/ppermute | solution.py:256
  4.9 9.5 %collective-permute-start.1 = (bf16[2,6272]{1,0:T(2,128)(2,1)S(1)}, bf16[2,6272]{1,0:T(2,128)(2,1)S(1)}, u32[]{:S(2)}, u32[]{:S(2)}) collective-permute-start(bf16[2,6272]{1,0:T(2,128)(2,1)S(1)} %get-tuple-element.25), channel_id=1, source_target_pairs={{0,64},{32,96},{64,0},{96,32},{1,65},{33,97},{65,1},{97,33},{2,66}... | collective-permute-start | bytes 75272 | tf_op jit(solution)/shard_map/ppermute | solution.py:256
  8.2 6.1 %collective-permute-start.2 = (bf16[2,6272]{1,0:T(2,128)(2,1)S(1)}, bf16[2,6272]{1,0:T(2,128)(2,1)S(1)}, u32[]{:S(2)}, u32[]{:S(2)}) collective-permute-start(bf16[2,6272]{1,0:T(2,128)(2,1)S(1)} %get-tuple-element.26), channel_id=1, source_target_pairs={{0,96},{32,0},{64,32},{96,64},{1,97},{33,1},{65,33},{97,65},{2,98}... | collective-permute-start | bytes 75272 | tf_op jit(solution)/shard_map/ppermute | solution.py:256
  14.4 18.3 %collective-permute-start.3 = (bf16[8,6272]{1,0:T(8,128)(2,1)S(1)}, bf16[8,6272]{1,0:T(8,128)(2,1)S(1)}, u32[]{:S(2)}, u32[]{:S(2)}) collective-permute-start(bf16[8,6272]{1,0:T(8,128)(2,1)S(1)} %shard_map.88.refs_0_), channel_id=1, source_target_pairs={{0,16},{16,0},{1,17},{17,1},{2,18},{18,2},{3,19},{19,3},{4,20},{20... | collective-permute-start | bytes 301064 | tf_op jit(solution)/shard_map/ppermute | solution.py:260
  30.1 6.5 %collective-permute-start.4 = (bf16[8,6272]{1,0:T(8,128)(2,1)S(1)}, bf16[8,6272]{1,0:T(8,128)(2,1)S(1)}, u32[]{:S(2)}, u32[]{:S(2)}) collective-permute-start(bf16[8,6272]{1,0:T(8,128)(2,1)S(1)} %shard_map.88.refs_0_), channel_id=1, source_target_pairs={{0,2},{2,4},{4,6},{6,8},{8,10},{10,12},{12,14},{14,0},{1,3},{3,5},... | collective-permute-start | bytes 301064 | tf_op jit(solution)/shard_map/ppermute | solution.py:264
  33.3 6.9 %collective-permute-start.6 = (bf16[8,6272]{1,0:T(8,128)(2,1)S(1)}, bf16[8,6272]{1,0:T(8,128)(2,1)S(1)}, u32[]{:S(2)}, u32[]{:S(2)}) collective-permute-start(bf16[8,6272]{1,0:T(8,128)(2,1)S(1)} %collective-permute-done.3.refs_1_), channel_id=1, source_target_pairs={{0,2},{2,4},{4,6},{6,8},{8,10},{10,12},{12,14},{14,0},{1,3},{3,5},... | collective-permute-start | bytes 301064 | tf_op jit(solution)/shard_map/ppermute | solution.py:264
  36.5 7.2 %collective-permute-start.8 = (bf16[8,6272]{1,0:T(8,128)(2,1)S(1)}, bf16[8,6272]{1,0:T(8,128)(2,1)S(1)}, u32[]{:S(2)}, u32[]{:S(2)}) collective-permute-start(bf16[8,6272]{1,0:T(8,128)(2,1)S(1)} %collective-permute-done.4.refs_2_), channel_id=1, source_target_pairs={{0,2},{2,4},{4,6},{6,8},{8,10},{10,12},{12,14},{14,0},{1,3},{3,5},... | collective-permute-start | bytes 301064 | tf_op jit(solution)/shard_map/ppermute | solution.py:264
  37.3 6.4 %collective-permute-start.11 = (bf16[8,6272]{1,0:T(8,128)(2,1)S(1)}, bf16[8,6272]{1,0:T(8,128)(2,1)S(1)}, u32[]{:S(2)}, u32[]{:S(2)}) collective-permute-start(bf16[8,6272]{1,0:T(8,128)(2,1)S(1)} %collective-permute-done.7.refs_5_), channel_id=1, source_target_pairs={{0,14},{2,0},{4,2},{6,4},{8,6},{10,8},{12,10},{14,12},{1,15},{3,1}... | collective-permute-start | bytes 301064 | tf_op jit(solution)/shard_map/ppermute | solution.py:264
  40.2 6.8 %collective-permute-start.10 = (bf16[8,6272]{1,0:T(8,128)(2,1)S(1)}, bf16[8,6272]{1,0:T(8,128)(2,1)S(1)}, u32[]{:S(2)}, u32[]{:S(2)}) collective-permute-start(bf16[8,6272]{1,0:T(8,128)(2,1)S(1)} %collective-permute-done.6.refs_4_), channel_id=1, source_target_pairs={{0,2},{2,4},{4,6},{6,8},{8,10},{10,12},{12,14},{14,0},{1,3},{3,5},... | collective-permute-start | bytes 301064 | tf_op jit(solution)/shard_map/ppermute | solution.py:264
  40.3 20.8 %collective-permute-start.18 = (bf16[48,6272]{1,0:T(8,128)(2,1)S(1)}, bf16[48,6272]{1,0:T(8,128)(2,1)S(1)}, u32[]{:S(2)}, u32[]{:S(2)}) collective-permute-start(bf16[48,6272]{1,0:T(8,128)(2,1)S(1)} %shard_map.89.refs_0_), channel_id=1, source_target_pairs={{0,1},{1,0},{2,3},{3,2},{4,5},{5,4},{6,7},{7,6},{8,9},{9,8},{10,11... | collective-permute-start | bytes 1806344 | tf_op jit(solution)/shard_map/ppermute | solution.py:260
  40.4 6.6 %collective-permute-start.13 = (bf16[8,6272]{1,0:T(8,128)(2,1)S(1)}, bf16[8,6272]{1,0:T(8,128)(2,1)S(1)}, u32[]{:S(2)}, u32[]{:S(2)}) collective-permute-start(bf16[8,6272]{1,0:T(8,128)(2,1)S(1)} %collective-permute-done.9.refs_1_), channel_id=1, source_target_pairs={{0,14},{2,0},{4,2},{6,4},{8,6},{10,8},{12,10},{14,12},{1,15},{3,1}... | collective-permute-start | bytes 301064 | tf_op jit(solution)/shard_map/ppermute | solution.py:264
  43.8 6.0 %collective-permute-start.12 = (bf16[8,6272]{1,0:T(8,128)(2,1)S(1)}, bf16[8,6272]{1,0:T(8,128)(2,1)S(1)}, u32[]{:S(2)}, u32[]{:S(2)}) collective-permute-start(bf16[8,6272]{1,0:T(8,128)(2,1)S(1)} %collective-permute-done.8.refs_0_), channel_id=1, source_target_pairs={{0,2},{2,4},{4,6},{6,8},{8,10},{10,12},{12,14},{14,0},{1,3},{3,5},... | collective-permute-start | bytes 301064 | tf_op jit(solution)/shard_map/ppermute | solution.py:264
  47.1 14.0 %collective-permute-start.19 = (bf16[32,6272]{1,0:T(8,128)(2,1)S(1)}, bf16[32,6272]{1,0:T(8,128)(2,1)S(1)}, u32[]{:S(2)}, u32[]{:S(2)}) collective-permute-start(bf16[32,6272]{1,0:T(8,128)(2,1)S(1)} %shard_map.90.refs_1_), channel_id=1, source_target_pairs={{0,1},{1,0},{2,3},{3,2},{4,5},{5,4},{6,7},{7,6},{8,9},{9,8},{10,11... | collective-permute-start | bytes 1204232 | tf_op jit(solution)/shard_map/ppermute | solution.py:260
  52.9 8.2 %collective-permute-start.20 = (bf16[32,6272]{1,0:T(8,128)(2,1)S(1)}, bf16[32,6272]{1,0:T(8,128)(2,1)S(1)}, u32[]{:S(2)}, u32[]{:S(2)}) collective-permute-start(bf16[32,6272]{1,0:T(8,128)(2,1)S(1)} %shard_map.91.refs_2_), channel_id=1, source_target_pairs={{0,1},{1,0},{2,3},{3,2},{4,5},{5,4},{6,7},{7,6},{8,9},{9,8},{10,11... | collective-permute-start | bytes 1204232 | tf_op jit(solution)/shard_map/ppermute | solution.py:260
  53.0 6.4 %collective-permute-start.16 = (bf16[8,6272]{1,0:T(8,128)(2,1)S(1)}, bf16[8,6272]{1,0:T(8,128)(2,1)S(1)}, u32[]{:S(2)}, u32[]{:S(2)}) collective-permute-start(bf16[8,6272]{1,0:T(8,128)(2,1)S(1)} %collective-permute-done.12.refs_0_), channel_id=1, source_target_pairs={{0,2},{2,4},{4,6},{6,8},{8,10},{10,12},{12,14},{14,0},{1,3},{3,5},... | collective-permute-start | bytes 301064 | tf_op jit(solution)/shard_map/ppermute | solution.py:264
  53.2 6.3 %collective-permute-start.17 = (bf16[8,6272]{1,0:T(8,128)(2,1)S(1)}, bf16[8,6272]{1,0:T(8,128)(2,1)S(1)}, u32[]{:S(2)}, u32[]{:S(2)}) collective-permute-start(bf16[8,6272]{1,0:T(8,128)(2,1)S(1)} %collective-permute-done.15.refs_3_), channel_id=1, source_target_pairs={{0,14},{2,0},{4,2},{6,4},{8,6},{10,8},{12,10},{14,12},{1,15},{3,1}... | collective-permute-start | bytes 301064 | tf_op jit(solution)/shard_map/ppermute | solution.py:264
  69.7 7.0 %collective-permute-start.24 = (bf16[32,6144]{1,0:T(8,128)(2,1)S(1)}, bf16[32,6144]{1,0:T(8,128)(2,1)S(1)}, u32[]{:S(2)}, u32[]{:S(2)}) collective-permute-start(bf16[32,6144]{1,0:T(8,128)(2,1)S(1)} %get-tuple-element.34), channel_id=1, source_target_pairs={{0,1},{1,0},{2,3},{3,2},{4,5},{5,4},{6,7},{7,6},{8,9},{9,8},{10,11... | collective-permute-start | bytes 1179656 | tf_op jit(solution)/shard_map/ppermute | solution.py:260
  69.9 20.7 %collective-permute-start.22 = (bf16[48,6144]{1,0:T(8,128)(2,1)S(1)}, bf16[48,6144]{1,0:T(8,128)(2,1)S(1)}, u32[]{:S(2)}, u32[]{:S(2)}) collective-permute-start(bf16[48,6144]{1,0:T(8,128)(2,1)S(1)} %get-tuple-element.30), channel_id=1, source_target_pairs={{0,1},{1,0},{2,3},{3,2},{4,5},{5,4},{6,7},{7,6},{8,9},{9,8},{10,11... | collective-permute-start | bytes 1769480 | tf_op jit(solution)/shard_map/ppermute | solution.py:260
  70.3 9.7 %collective-permute-start.23 = (bf16[32,6144]{1,0:T(8,128)(2,1)S(1)}, bf16[32,6144]{1,0:T(8,128)(2,1)S(1)}, u32[]{:S(2)}, u32[]{:S(2)}) collective-permute-start(bf16[32,6144]{1,0:T(8,128)(2,1)S(1)} %get-tuple-element.32), channel_id=1, source_target_pairs={{0,1},{1,0},{2,3},{3,2},{4,5},{5,4},{6,7},{7,6},{8,9},{9,8},{10,11... | collective-permute-start | bytes 1179656 | tf_op jit(solution)/shard_map/ppermute | solution.py:260
  73.2 6.2 %collective-permute-start.36 = (bf16[8,6144]{1,0:T(8,128)(2,1)S(1)}, bf16[8,6144]{1,0:T(8,128)(2,1)S(1)}, u32[]{:S(2)}, u32[]{:S(2)}) collective-permute-start(bf16[8,6144]{1,0:T(8,128)(2,1)S(1)} %shard_map.105), channel_id=1, source_target_pairs={{0,2},{2,4},{4,6},{6,8},{8,10},{10,12},{12,14},{14,0},{1,3},{3,5},... | collective-permute-start | bytes 294920 | tf_op jit(solution)/shard_map/ppermute | solution.py:264
  73.4 6.4 %collective-permute-start.26 = (bf16[8,6144]{1,0:T(8,128)(2,1)S(1)}, bf16[8,6144]{1,0:T(8,128)(2,1)S(1)}, u32[]{:S(2)}, u32[]{:S(2)}) collective-permute-start(bf16[8,6144]{1,0:T(8,128)(2,1)S(1)} %shard_map.94), channel_id=1, source_target_pairs={{0,14},{2,0},{4,2},{6,4},{8,6},{10,8},{12,10},{14,12},{1,15},{3,1}... | collective-permute-start | bytes 294920 | tf_op jit(solution)/shard_map/ppermute | solution.py:264
  76.7 6.6 %collective-permute-start.33 = (bf16[8,6144]{1,0:T(8,128)(2,1)S(1)}, bf16[8,6144]{1,0:T(8,128)(2,1)S(1)}, u32[]{:S(2)}, u32[]{:S(2)}) collective-permute-start(bf16[8,6144]{1,0:T(8,128)(2,1)S(1)} %shard_map.102), channel_id=1, source_target_pairs={{0,14},{2,0},{4,2},{6,4},{8,6},{10,8},{12,10},{14,12},{1,15},{3,1}... | collective-permute-start | bytes 294920 | tf_op jit(solution)/shard_map/ppermute | solution.py:264
  79.4 6.6 %collective-permute-start.37 = (bf16[8,6144]{1,0:T(8,128)(2,1)S(1)}, bf16[8,6144]{1,0:T(8,128)(2,1)S(1)}, u32[]{:S(2)}, u32[]{:S(2)}) collective-permute-start(bf16[8,6144]{1,0:T(8,128)(2,1)S(1)} %shard_map.106), channel_id=1, source_target_pairs={{0,2},{2,4},{4,6},{6,8},{8,10},{10,12},{12,14},{14,0},{1,3},{3,5},... | collective-permute-start | bytes 294920 | tf_op jit(solution)/shard_map/ppermute | solution.py:264
  79.8 7.2 %collective-permute-start.30 = (bf16[8,6144]{1,0:T(8,128)(2,1)S(1)}, bf16[8,6144]{1,0:T(8,128)(2,1)S(1)}, u32[]{:S(2)}, u32[]{:S(2)}) collective-permute-start(bf16[8,6144]{1,0:T(8,128)(2,1)S(1)} %shard_map.98), channel_id=1, source_target_pairs={{0,2},{2,4},{4,6},{6,8},{8,10},{10,12},{12,14},{14,0},{1,3},{3,5},... | collective-permute-start | bytes 294920 | tf_op jit(solution)/shard_map/ppermute | solution.py:264
  80.0 7.2 %collective-permute-start.27 = (bf16[8,6144]{1,0:T(8,128)(2,1)S(1)}, bf16[8,6144]{1,0:T(8,128)(2,1)S(1)}, u32[]{:S(2)}, u32[]{:S(2)}) collective-permute-start(bf16[8,6144]{1,0:T(8,128)(2,1)S(1)} %shard_map.95), channel_id=1, source_target_pairs={{0,14},{2,0},{4,2},{6,4},{8,6},{10,8},{12,10},{14,12},{1,15},{3,1}... | collective-permute-start | bytes 294920 | tf_op jit(solution)/shard_map/ppermute | solution.py:264
  83.4 7.2 %collective-permute-start.34 = (bf16[8,6144]{1,0:T(8,128)(2,1)S(1)}, bf16[8,6144]{1,0:T(8,128)(2,1)S(1)}, u32[]{:S(2)}, u32[]{:S(2)}) collective-permute-start(bf16[8,6144]{1,0:T(8,128)(2,1)S(1)} %shard_map.103), channel_id=1, source_target_pairs={{0,14},{2,0},{4,2},{6,4},{8,6},{10,8},{12,10},{14,12},{1,15},{3,1}... | collective-permute-start | bytes 294920 | tf_op jit(solution)/shard_map/ppermute | solution.py:264
  87.1 9.5 %collective-permute-start.31 = (bf16[8,6144]{1,0:T(8,128)(2,1)S(1)}, bf16[8,6144]{1,0:T(8,128)(2,1)S(1)}, u32[]{:S(2)}, u32[]{:S(2)}) collective-permute-start(bf16[8,6144]{1,0:T(8,128)(2,1)S(1)} %shard_map.99), channel_id=1, source_target_pairs={{0,2},{2,4},{4,6},{6,8},{8,10},{10,12},{12,14},{14,0},{1,3},{3,5},... | collective-permute-start | bytes 294920 | tf_op jit(solution)/shard_map/ppermute | solution.py:264
  90.6 6.1 %collective-permute-start.35 = (bf16[8,6144]{1,0:T(8,128)(2,1)S(1)}, bf16[8,6144]{1,0:T(8,128)(2,1)S(1)}, u32[]{:S(2)}, u32[]{:S(2)}) collective-permute-start(bf16[8,6144]{1,0:T(8,128)(2,1)S(1)} %shard_map.104), channel_id=1, source_target_pairs={{0,14},{2,0},{4,2},{6,4},{8,6},{10,8},{12,10},{14,12},{1,15},{3,1}... | collective-permute-start | bytes 294920 | tf_op jit(solution)/shard_map/ppermute | solution.py:264
  92.0 6.6 %collective-permute-start.39 = (bf16[8,6144]{1,0:T(8,128)(2,1)S(1)}, bf16[8,6144]{1,0:T(8,128)(2,1)S(1)}, u32[]{:S(2)}, u32[]{:S(2)}) collective-permute-start(bf16[8,6144]{1,0:T(8,128)(2,1)S(1)} %shard_map.108), channel_id=1, source_target_pairs={{0,2},{2,4},{4,6},{6,8},{8,10},{10,12},{12,14},{14,0},{1,3},{3,5},... | collective-permute-start | bytes 294920 | tf_op jit(solution)/shard_map/ppermute | solution.py:264
  93.0 7.2 %collective-permute-start.29 = (bf16[8,6144]{1,0:T(8,128)(2,1)S(1)}, bf16[8,6144]{1,0:T(8,128)(2,1)S(1)}, u32[]{:S(2)}, u32[]{:S(2)}) collective-permute-start(bf16[8,6144]{1,0:T(8,128)(2,1)S(1)} %shard_map.97), channel_id=1, source_target_pairs={{0,14},{2,0},{4,2},{6,4},{8,6},{10,8},{12,10},{14,12},{1,15},{3,1}... | collective-permute-start | bytes 294920 | tf_op jit(solution)/shard_map/ppermute | solution.py:264
  103.5 7.7 %collective-permute-start.41 = (bf16[2,6144]{1,0:T(2,128)(2,1)S(1)}, bf16[2,6144]{1,0:T(2,128)(2,1)S(1)}, u32[]{:S(2)}, u32[]{:S(2)}) collective-permute-start(bf16[2,6144]{1,0:T(2,128)(2,1)S(1)} %get-tuple-element.38), channel_id=1, source_target_pairs={{0,96},{32,0},{64,32},{96,64},{1,97},{33,1},{65,33},{97,65},{2,98}... | collective-permute-start | bytes 73736 | tf_op jit(solution)/shard_map/ppermute | solution.py:256
  106.9 7.7 %collective-permute-start.42 = (bf16[2,6144]{1,0:T(2,128)(2,1)S(1)}, bf16[2,6144]{1,0:T(2,128)(2,1)S(1)}, u32[]{:S(2)}, u32[]{:S(2)}) collective-permute-start(bf16[2,6144]{1,0:T(2,128)(2,1)S(1)} %get-tuple-element.39), channel_id=1, source_target_pairs={{0,64},{32,96},{64,0},{96,32},{1,65},{33,97},{65,1},{97,33},{2,66}... | collective-permute-start | bytes 73736 | tf_op jit(solution)/shard_map/ppermute | solution.py:256
  (12 other events, 59.4 us)

commit v2 on v1

--- a/solution.py
+++ b/solution.py
@@ -155,13 +155,11 @@
 
 
 def expert_kernel(scale, groups, *refs):
-    blocks, (gate, down, up_hbm) = refs[: 2 * groups], refs[2 * groups : 2 * groups + 3]
+    blocks, (gate, up, down) = refs[: 2 * groups], refs[2 * groups : 2 * groups + 3]
     refs = refs[2 * groups + 3 :]
     outs, balance_ref = refs[: 2 * groups], refs[2 * groups]
-    x_ref, hidden_ref, up, sem = refs[2 * groups + 1 :]
+    x_ref, hidden_ref = refs[2 * groups + 1 :]
     width = down.shape[1]
-    copy = pltpu.make_async_copy(up_hbm, up, sem.at[0])
-    copy.start()
     start = 0
     total = jnp.zeros((8, LANES), F32)
     for block in blocks:
@@ -176,7 +174,6 @@
     balance_ref[...] = jnp.sum(named * probs, axis=1, keepdims=True) * scale
 
     gate_pre = jnp.dot(x_ref[...], gate[...], preferred_element_type=F32)
-    copy.wait()
     up_pre = jnp.dot(x_ref[...], up[...], preferred_element_type=F32)
     hidden_ref[...] = (gate_pre * jax.nn.sigmoid(gate_pre) * up_pre).astype(BF16)
     tile = 512
@@ -284,7 +281,7 @@
     )
     arrived = [sends[0]] + [to_expert(sends[k], k) for k in range(1, EXPERTS)]
     size = EXPERTS * CAP
-    gate_near, down_near = fetch([gate_weight, down_weight], sends[0])
+    gate_near, up_near, down_near = fetch([gate_weight, up_weight, down_weight], sends[0])
     block_a = call(
         join_kernel,
         [shape(size, wide, BF16)],
@@ -319,19 +316,17 @@
         functools.partial(expert_kernel, scale, groups),
         out_shape=[shape(n, width, dtype) for dtype in (F32, BF16) for n in rows]
         + [shape(1, 1, F32)],
-        in_specs=vmem(2 * groups + 2) + [hbm],
+        in_specs=vmem(2 * groups + 3),
         out_specs=vmem(2 * groups + 1),
         scratch_shapes=[
             pltpu.VMEM((2 * sum(rows), width), BF16),
             pltpu.VMEM((2 * sum(rows), units), BF16),
-            pltpu.VMEM((width, units), BF16),
-            pltpu.SemaphoreType.DMA((1,)),
         ],
         cost_estimate=pl.CostEstimate(
             flops=12 * sum(rows) * width * units, bytes_accessed=9_000_000, transcendentals=0
         ),
         compiler_params=pltpu.CompilerParams(vmem_limit_bytes=12 << 20),
-    )(*near, *far, gate_near, down_near, in_hbm(up_weight))
+    )(*near, *far, gate_near, up_near, down_near)
     kept, sent = outs[:groups], outs[groups : 2 * groups]
     balance = outs[2 * groups].reshape(1)
     crossed = {}

time: 118 us -> 114 us (0.966)
  Pallas kernels: 14.5 us -> 11.9 us
  waiting for transfers between devices: 27.4 us -> 25.7 us
    pallas_call x1, Pallas kernels: 8.58 us -> 5.11 us  [local(): pl.pallas_call(functools.partial(expert_kernel, scale, groups), out_shape...]
  transfers between devices with their start and end apart: 44 -> 44, of which waited for: 18 -> 15; matrix products, arithmetic and copies ran while one was open for 0% -> 0% of each run, Pallas kernels for 3% -> 4%
where the time goes in v2:
time: 114 us
  starting transfers between devices  75.7 us (66%)
  waiting for transfers between devices  25.7 us (23%)
  Pallas kernels  11.9 us (10%)
    ppermute x28, starting transfers between devices, along(): lax.ppermute(value, 'y', [(y, (y + step) % RING) for y in range(RING)])  39.7 us
    ppermute x6, starting transfers between devices, to_expert(): lax.ppermute(value, 'xo', [(i, (i + step) % EXPERTS) for i in range(EXPER...  18.1 us
    ppermute x10, starting transfers between devices, swap(): return lax.ppermute(value, axis, [(0, 1), (1, 0)])  17.8 us
    ppermute x28, waiting for transfers between devices, along(): lax.ppermute(value, 'y', [(y, (y + step) % RING) for y in range(RING)])  15.1 us
    ppermute x6, waiting for transfers between devices, to_expert(): lax.ppermute(value, 'xo', [(i, (i + step) % EXPERTS) for i in range(EXPER...  5.3 us
    ppermute x10, waiting for transfers between devices, swap(): return lax.ppermute(value, axis, [(0, 1), (1, 0)])  5.24 us
    pallas_call x1, Pallas kernels, local(): pl.pallas_call(functools.partial(expert_kernel, scale, groups), out_shape...  5.11 us
    pallas_call x1, Pallas kernels, fetch(): pl.pallas_call(fetch_kernel, out_shape=[pltpu.VMEM(w.shape, w.dtype) for...  3.78 us
  transfers between devices with their start and end apart: 44, of which 15 were waited for; matrix products, arithmetic and copies ran while one was open for 0% of the time, Pallas kernels for 4%

profile of v2, /device:TPU:514, one launch (start us, length us, event | category | flops | bytes accessed | tf_op | source)
XLA Modules:
  0.0 114.2 jit_solution(2207503906620090731)
XLA Ops:
  0.6 1.4 %shard_map.86 = (bf16[2,6272]{1,0:T(2,128)(2,1)S(1)}, bf16[2,6272]{1,0:T(2,128)(2,1)S(1)}, bf16[2,6272]{1,0:T(2,128)(2,1)S(1)}, bf16[2,6272]{1,0:T(2,128)(2,1)S(1)}, f32[4,128]{1,0:T(4,128)S(1)}) custom-call(s32[2,4]{1,0:T(2,128)} %bitcast.5, s32[2,4]{1,0:T(2,128)} %bitcast.6, bf16[4,6144]{1,0:T(4,128)(2,1)} %tok_hbm.1, bf16[4,6144]{1,0:T(4,128)(2,1)} %bitcast.4), custom_call_target="tpu_custom_call" | custom-call | flops 200000 | bytes 1000000 | tf_op jit(solution)/shard_map/pallas_call | solution.py:33
  2.1 2.8 %collective-permute-start = (bf16[2,6272]{1,0:T(2,128)(2,1)S(1)}, bf16[2,6272]{1,0:T(2,128)(2,1)S(1)}, u32[]{:S(2)}, u32[]{:S(2)}) collective-permute-start(bf16[2,6272]{1,0:T(2,128)(2,1)S(1)} %get-tuple-element.25), channel_id=1, source_target_pairs={{0,32},{32,64},{64,96},{96,0},{1,33},{33,65},{65,97},{97,1},{2,34}... | collective-permute-start | bytes 75272 | tf_op jit(solution)/shard_map/ppermute | solution.py:253
  4.9 3.3 %collective-permute-start.1 = (bf16[2,6272]{1,0:T(2,128)(2,1)S(1)}, bf16[2,6272]{1,0:T(2,128)(2,1)S(1)}, u32[]{:S(2)}, u32[]{:S(2)}) collective-permute-start(bf16[2,6272]{1,0:T(2,128)(2,1)S(1)} %get-tuple-element.26), channel_id=1, source_target_pairs={{0,64},{32,96},{64,0},{96,32},{1,65},{33,97},{65,1},{97,33},{2,66}... | collective-permute-start | bytes 75272 | tf_op jit(solution)/shard_map/ppermute | solution.py:253
  8.2 3.2 %collective-permute-start.2 = (bf16[2,6272]{1,0:T(2,128)(2,1)S(1)}, bf16[2,6272]{1,0:T(2,128)(2,1)S(1)}, u32[]{:S(2)}, u32[]{:S(2)}) collective-permute-start(bf16[2,6272]{1,0:T(2,128)(2,1)S(1)} %get-tuple-element.27), channel_id=1, source_target_pairs={{0,96},{32,0},{64,32},{96,64},{1,97},{33,1},{65,33},{97,65},{2,98}... | collective-permute-start | bytes 75272 | tf_op jit(solution)/shard_map/ppermute | solution.py:253
  11.4 3.8 %shard_map.87 = (bf16[6144,256]{1,0:T(8,128)(2,1)S(1)}, bf16[6144,256]{1,0:T(8,128)(2,1)S(1)}, bf16[256,6144]{1,0:T(8,128)(2,1)S(1)}) custom-call(bf16[6144,256]{1,0:T(8,128)(2,1)} %refs_0_.1, bf16[6144,256]{1,0:T(8,128)(2,1)} %refs_1_.1, bf16[256,6144]{1,0:T(8,128)(2,1)} %refs_2_.1, bf16[2,6272]{1,0:T(2,128)(2,1)S(1)} %get-tuple-element.24.refs_3_.own), custom_call_target="tpu_custom_call" | custom-call | flops 1000000 | bytes 18874368 | tf_op jit(solution)/shard_map/pallas_call | solution.py:205
  15.3 14.7 %collective-permute-start.3 = (bf16[8,6272]{1,0:T(8,128)(2,1)S(1)}, bf16[8,6272]{1,0:T(8,128)(2,1)S(1)}, u32[]{:S(2)}, u32[]{:S(2)}) collective-permute-start(bf16[8,6272]{1,0:T(8,128)(2,1)S(1)} %shard_map.88.refs_0_), channel_id=1, source_target_pairs={{0,16},{16,0},{1,17},{17,1},{2,18},{18,2},{3,19},{19,3},{4,20},{20... | collective-permute-start | bytes 301064 | tf_op jit(solution)/shard_map/ppermute | solution.py:257
  30.1 2.0 %collective-permute-start.4 = (bf16[8,6272]{1,0:T(8,128)(2,1)S(1)}, bf16[8,6272]{1,0:T(8,128)(2,1)S(1)}, u32[]{:S(2)}, u32[]{:S(2)}) collective-permute-start(bf16[8,6272]{1,0:T(8,128)(2,1)S(1)} %shard_map.88.refs_0_), channel_id=1, source_target_pairs={{0,2},{2,4},{4,6},{6,8},{8,10},{10,12},{12,14},{14,0},{1,3},{3,5},... | collective-permute-start | bytes 301064 | tf_op jit(solution)/shard_map/ppermute | solution.py:261
  33.3 1.4 %collective-permute-start.6 = (bf16[8,6272]{1,0:T(8,128)(2,1)S(1)}, bf16[8,6272]{1,0:T(8,128)(2,1)S(1)}, u32[]{:S(2)}, u32[]{:S(2)}) collective-permute-start(bf16[8,6272]{1,0:T(8,128)(2,1)S(1)} %collective-permute-done.3.refs_1_), channel_id=1, source_target_pairs={{0,2},{2,4},{4,6},{6,8},{8,10},{10,12},{12,14},{14,0},{1,3},{3,5},... | collective-permute-start | bytes 301064 | tf_op jit(solution)/shard_map/ppermute | solution.py:261
  34.7 1.8 %collective-permute-start.9 = (bf16[8,6272]{1,0:T(8,128)(2,1)S(1)}, bf16[8,6272]{1,0:T(8,128)(2,1)S(1)}, u32[]{:S(2)}, u32[]{:S(2)}) collective-permute-start(bf16[8,6272]{1,0:T(8,128)(2,1)S(1)} %collective-permute-done.5.refs_3_), channel_id=1, source_target_pairs={{0,14},{2,0},{4,2},{6,4},{8,6},{10,8},{12,10},{14,12},{1,15},{3,1}... | collective-permute-start | bytes 301064 | tf_op jit(solution)/shard_map/ppermute | solution.py:261
  37.5 2.3 %collective-permute-start.11 = (bf16[8,6272]{1,0:T(8,128)(2,1)S(1)}, bf16[8,6272]{1,0:T(8,128)(2,1)S(1)}, u32[]{:S(2)}, u32[]{:S(2)}) collective-permute-start(bf16[8,6272]{1,0:T(8,128)(2,1)S(1)} %collective-permute-done.7.refs_5_), channel_id=1, source_target_pairs={{0,14},{2,0},{4,2},{6,4},{8,6},{10,8},{12,10},{14,12},{1,15},{3,1}... | collective-permute-start | bytes 301064 | tf_op jit(solution)/shard_map/ppermute | solution.py:261
  40.4 2.9 %collective-permute-start.13 = (bf16[8,6272]{1,0:T(8,128)(2,1)S(1)}, bf16[8,6272]{1,0:T(8,128)(2,1)S(1)}, u32[]{:S(2)}, u32[]{:S(2)}) collective-permute-start(bf16[8,6272]{1,0:T(8,128)(2,1)S(1)} %collective-permute-done.9.refs_1_), channel_id=1, source_target_pairs={{0,14},{2,0},{4,2},{6,4},{8,6},{10,8},{12,10},{14,12},{1,15},{3,1}... | collective-permute-start | bytes 301064 | tf_op jit(solution)/shard_map/ppermute | solution.py:261
  43.4 3.2 %collective-permute-start.15 = (bf16[8,6272]{1,0:T(8,128)(2,1)S(1)}, bf16[8,6272]{1,0:T(8,128)(2,1)S(1)}, u32[]{:S(2)}, u32[]{:S(2)}) collective-permute-start(bf16[8,6272]{1,0:T(8,128)(2,1)S(1)} %collective-permute-done.11.refs_3_), channel_id=1, source_target_pairs={{0,14},{2,0},{4,2},{6,4},{8,6},{10,8},{12,10},{14,12},{1,15},{3,1}... | collective-permute-start | bytes 301064 | tf_op jit(solution)/shard_map/ppermute | solution.py:261
  46.8 2.6 %collective-permute-done.12.refs_0_ = bf16[8,6272]{1,0:T(8,128)(2,1)S(1)} collective-permute-done((bf16[8,6272]{1,0:T(8,128)(2,1)S(1)}, bf16[8,6272]{1,0:T(8,128)(2,1)S(1)}, u32[]{:S(2)}, u32[]{:S(2)}) %collective-permute-start.12) | collective-permute-done | bytes 100384 | tf_op jit(solution)/shard_map/ppermute | solution.py:261
  49.4 3.1 %collective-permute-done.14.refs_2_ = bf16[8,6272]{1,0:T(8,128)(2,1)S(1)} collective-permute-done((bf16[8,6272]{1,0:T(8,128)(2,1)S(1)}, bf16[8,6272]{1,0:T(8,128)(2,1)S(1)}, u32[]{:S(2)}, u32[]{:S(2)}) %collective-permute-start.14) | collective-permute-done | bytes 100384 | tf_op jit(solution)/shard_map/ppermute | solution.py:261
  52.8 3.2 %collective-permute-start.17 = (bf16[8,6272]{1,0:T(8,128)(2,1)S(1)}, bf16[8,6272]{1,0:T(8,128)(2,1)S(1)}, u32[]{:S(2)}, u32[]{:S(2)}) collective-permute-start(bf16[8,6272]{1,0:T(8,128)(2,1)S(1)} %collective-permute-done.15.refs_3_), channel_id=1, source_target_pairs={{0,14},{2,0},{4,2},{6,4},{8,6},{10,8},{12,10},{14,12},{1,15},{3,1}... | collective-permute-start | bytes 301064 | tf_op jit(solution)/shard_map/ppermute | solution.py:261
  56.0 3.1 %collective-permute-done.16.refs_0_ = bf16[8,6272]{1,0:T(8,128)(2,1)S(1)} collective-permute-done((bf16[8,6272]{1,0:T(8,128)(2,1)S(1)}, bf16[8,6272]{1,0:T(8,128)(2,1)S(1)}, u32[]{:S(2)}, u32[]{:S(2)}) %collective-permute-start.16) | collective-permute-done | bytes 100384 | tf_op jit(solution)/shard_map/ppermute | solution.py:261
  59.2 1.4 %collective-permute-done.21.refs_7_ = bf16[16,6272]{1,0:T(8,128)(2,1)S(1)} collective-permute-done((bf16[16,6272]{1,0:T(8,128)(2,1)S(1)}, bf16[16,6272]{1,0:T(8,128)(2,1)S(1)}, u32[]{:S(2)}, u32[]{:S(2)}) %collective-permute-start.21) | collective-permute-done | bytes 200736 | tf_op jit(solution)/shard_map/ppermute | solution.py:257
  60.7 5.1 %shard_map.93 = (f32[48,6144]{1,0:T(8,128)S(1)}, f32[32,6144]{1,0:T(8,128)S(1)}, f32[32,6144]{1,0:T(8,128)S(1)}, f32[16,6144]{1,0:T(8,128)S(1)}, bf16[48,6144]{1...) custom-call(bf16[48,6272]{1,0:T(8,128)(2,1)S(1)} %shard_map.89.refs_, ...), custom_call_target="tpu_custom_call" | custom-call | flops 2415919104 | bytes 9000000 | tf_op jit(solution)/shard_map/pallas_call | solution.py:315
  66.8 2.4 %collective-permute-done.25.crossed_ref = bf16[16,6144]{1,0:T(8,128)(2,1)S(1)} collective-permute-done((bf16[16,6144]{1,0:T(8,128)(2,1)S(1)}, bf16[16,6144]{1,0:T(8,128)(2,1)S(1)}, u32[]{:S(2)}, u32[]{:S(2)}) %collective-permute-start.25) | collective-permute-done | bytes 196640 | tf_op jit(solution)/shard_map/ppermute | solution.py:257
  69.4 3.3 %collective-permute-start.26 = (bf16[8,6144]{1,0:T(8,128)(2,1)S(1)}, bf16[8,6144]{1,0:T(8,128)(2,1)S(1)}, u32[]{:S(2)}, u32[]{:S(2)}) collective-permute-start(bf16[8,6144]{1,0:T(8,128)(2,1)S(1)} %shard_map.94), channel_id=1, source_target_pairs={{0,14},{2,0},{4,2},{6,4},{8,6},{10,8},{12,10},{14,12},{1,15},{3,1}... | collective-permute-start | bytes 294920 | tf_op jit(solution)/shard_map/ppermute | solution.py:261
  72.7 1.9 %collective-permute-start.33 = (bf16[8,6144]{1,0:T(8,128)(2,1)S(1)}, bf16[8,6144]{1,0:T(8,128)(2,1)S(1)}, u32[]{:S(2)}, u32[]{:S(2)}) collective-permute-start(bf16[8,6144]{1,0:T(8,128)(2,1)S(1)} %shard_map.102), channel_id=1, source_target_pairs={{0,14},{2,0},{4,2},{6,4},{8,6},{10,8},{12,10},{14,12},{1,15},{3,1}... | collective-permute-start | bytes 294920 | tf_op jit(solution)/shard_map/ppermute | solution.py:261
  76.0 3.3 %collective-permute-start.27 = (bf16[8,6144]{1,0:T(8,128)(2,1)S(1)}, bf16[8,6144]{1,0:T(8,128)(2,1)S(1)}, u32[]{:S(2)}, u32[]{:S(2)}) collective-permute-start(bf16[8,6144]{1,0:T(8,128)(2,1)S(1)} %shard_map.95), channel_id=1, source_target_pairs={{0,14},{2,0},{4,2},{6,4},{8,6},{10,8},{12,10},{14,12},{1,15},{3,1}... | collective-permute-start | bytes 294920 | tf_op jit(solution)/shard_map/ppermute | solution.py:261
  79.4 2.1 %collective-permute-start.34 = (bf16[8,6144]{1,0:T(8,128)(2,1)S(1)}, bf16[8,6144]{1,0:T(8,128)(2,1)S(1)}, u32[]{:S(2)}, u32[]{:S(2)}) collective-permute-start(bf16[8,6144]{1,0:T(8,128)(2,1)S(1)} %shard_map.103), channel_id=1, source_target_pairs={{0,14},{2,0},{4,2},{6,4},{8,6},{10,8},{12,10},{14,12},{1,15},{3,1}... | collective-permute-start | bytes 294920 | tf_op jit(solution)/shard_map/ppermute | solution.py:261
  83.1 3.3 %collective-permute-start.28 = (bf16[8,6144]{1,0:T(8,128)(2,1)S(1)}, bf16[8,6144]{1,0:T(8,128)(2,1)S(1)}, u32[]{:S(2)}, u32[]{:S(2)}) collective-permute-start(bf16[8,6144]{1,0:T(8,128)(2,1)S(1)} %shard_map.96), channel_id=1, source_target_pairs={{0,14},{2,0},{4,2},{6,4},{8,6},{10,8},{12,10},{14,12},{1,15},{3,1}... | collective-permute-start | bytes 294920 | tf_op jit(solution)/shard_map/ppermute | solution.py:261
  88.8 3.6 %collective-permute-start.29 = (bf16[8,6144]{1,0:T(8,128)(2,1)S(1)}, bf16[8,6144]{1,0:T(8,128)(2,1)S(1)}, u32[]{:S(2)}, u32[]{:S(2)}) collective-permute-start(bf16[8,6144]{1,0:T(8,128)(2,1)S(1)} %shard_map.97), channel_id=1, source_target_pairs={{0,14},{2,0},{4,2},{6,4},{8,6},{10,8},{12,10},{14,12},{1,15},{3,1}... | collective-permute-start | bytes 294920 | tf_op jit(solution)/shard_map/ppermute | solution.py:261
  92.6 1.9 %collective-permute-done.39.refs_1_ = bf16[8,6144]{1,0:T(8,128)(2,1)S(1)} collective-permute-done((bf16[8,6144]{1,0:T(8,128)(2,1)S(1)}, bf16[8,6144]{1,0:T(8,128)(2,1)S(1)}, u32[]{:S(2)}, u32[]{:S(2)}) %collective-permute-start.39) | collective-permute-done | bytes 98336 | tf_op jit(solution)/shard_map/ppermute | solution.py:261
  94.5 1.5 %collective-permute-start.40 = (bf16[8,6144]{1,0:T(8,128)(2,1)S(1)}, bf16[8,6144]{1,0:T(8,128)(2,1)S(1)}, u32[]{:S(2)}, u32[]{:S(2)}) collective-permute-start(bf16[8,6144]{1,0:T(8,128)(2,1)S(1)} %shard_map.109), channel_id=1, source_target_pairs={{0,16},{16,0},{1,17},{17,1},{2,18},{18,2},{3,19},{19,3},{4,20},{20... | collective-permute-start | bytes 294920 | tf_op jit(solution)/shard_map/ppermute | solution.py:257
  96.0 2.4 %collective-permute-done.32.refs_1_ = bf16[8,6144]{1,0:T(8,128)(2,1)S(1)} collective-permute-done((bf16[8,6144]{1,0:T(8,128)(2,1)S(1)}, bf16[8,6144]{1,0:T(8,128)(2,1)S(1)}, u32[]{:S(2)}, u32[]{:S(2)}) %collective-permute-start.32) | collective-permute-done | bytes 98336 | tf_op jit(solution)/shard_map/ppermute | solution.py:261
  99.3 3.8 %collective-permute-start.41 = (bf16[2,6144]{1,0:T(2,128)(2,1)S(1)}, bf16[2,6144]{1,0:T(2,128)(2,1)S(1)}, u32[]{:S(2)}, u32[]{:S(2)}) collective-permute-start(bf16[2,6144]{1,0:T(2,128)(2,1)S(1)} %get-tuple-element.40), channel_id=1, source_target_pairs={{0,96},{32,0},{64,32},{96,64},{1,97},{33,1},{65,33},{97,65},{2,98}... | collective-permute-start | bytes 73736 | tf_op jit(solution)/shard_map/ppermute | solution.py:253
  103.1 4.3 %collective-permute-start.42 = (bf16[2,6144]{1,0:T(2,128)(2,1)S(1)}, bf16[2,6144]{1,0:T(2,128)(2,1)S(1)}, u32[]{:S(2)}, u32[]{:S(2)}) collective-permute-start(bf16[2,6144]{1,0:T(2,128)(2,1)S(1)} %get-tuple-element.41), channel_id=1, source_target_pairs={{0,64},{32,96},{64,0},{96,32},{1,65},{33,97},{65,1},{97,33},{2,66}... | collective-permute-start | bytes 73736 | tf_op jit(solution)/shard_map/ppermute | solution.py:253
  108.1 2.8 %collective-permute-done.42.r2 = bf16[2,6144]{1,0:T(2,128)(2,1)S(1)} collective-permute-done((bf16[2,6144]{1,0:T(2,128)(2,1)S(1)}, bf16[2,6144]{1,0:T(2,128)(2,1)S(1)}, u32[]{:S(2)}, u32[]{:S(2)}) %collective-permute-start.42) | collective-permute-done | bytes 24608 | tf_op jit(solution)/shard_map/ppermute | solution.py:253
  110.9 2.5 %collective-permute-done.43.r3 = bf16[2,6144]{1,0:T(2,128)(2,1)S(1)} collective-permute-done((bf16[2,6144]{1,0:T(2,128)(2,1)S(1)}, bf16[2,6144]{1,0:T(2,128)(2,1)S(1)}, u32[]{:S(2)}, u32[]{:S(2)}) %collective-permute-start.43) | collective-permute-done | bytes 24608 | tf_op jit(solution)/shard_map/ppermute | solution.py:253
  (82 shorter events, 12.8 us)
Async XLA Ops:
  2.1 13.2 %collective-permute-start = (bf16[2,6272]{1,0:T(2,128)(2,1)S(1)}, bf16[2,6272]{1,0:T(2,128)(2,1)S(1)}, u32[]{:S(2)}, u32[]{:S(2)}) collective-permute-start(bf16[2,6272]{1,0:T(2,128)(2,1)S(1)} %get-tuple-element.25), channel_id=1, source_target_pairs={{0,32},{32,64},{64,96},{96,0},{1,33},{33,65},{65,97},{97,1},{2,34}... | collective-permute-start | bytes 75272 | tf_op jit(solution)/shard_map/ppermute | solution.py:253
  4.9 10.4 %collective-permute-start.1 = (bf16[2,6272]{1,0:T(2,128)(2,1)S(1)}, bf16[2,6272]{1,0:T(2,128)(2,1)S(1)}, u32[]{:S(2)}, u32[]{:S(2)}) collective-permute-start(bf16[2,6272]{1,0:T(2,128)(2,1)S(1)} %get-tuple-element.26), channel_id=1, source_target_pairs={{0,64},{32,96},{64,0},{96,32},{1,65},{33,97},{65,1},{97,33},{2,66}... | collective-permute-start | bytes 75272 | tf_op jit(solution)/shard_map/ppermute | solution.py:253
  8.2 7.1 %collective-permute-start.2 = (bf16[2,6272]{1,0:T(2,128)(2,1)S(1)}, bf16[2,6272]{1,0:T(2,128)(2,1)S(1)}, u32[]{:S(2)}, u32[]{:S(2)}) collective-permute-start(bf16[2,6272]{1,0:T(2,128)(2,1)S(1)} %get-tuple-element.27), channel_id=1, source_target_pairs={{0,96},{32,0},{64,32},{96,64},{1,97},{33,1},{65,33},{97,65},{2,98}... | collective-permute-start | bytes 75272 | tf_op jit(solution)/shard_map/ppermute | solution.py:253
  15.3 17.4 %collective-permute-start.3 = (bf16[8,6272]{1,0:T(8,128)(2,1)S(1)}, bf16[8,6272]{1,0:T(8,128)(2,1)S(1)}, u32[]{:S(2)}, u32[]{:S(2)}) collective-permute-start(bf16[8,6272]{1,0:T(8,128)(2,1)S(1)} %shard_map.88.refs_0_), channel_id=1, source_target_pairs={{0,16},{16,0},{1,17},{17,1},{2,18},{18,2},{3,19},{19,3},{4,20},{20... | collective-permute-start | bytes 301064 | tf_op jit(solution)/shard_map/ppermute | solution.py:257
  30.1 6.5 %collective-permute-start.4 = (bf16[8,6272]{1,0:T(8,128)(2,1)S(1)}, bf16[8,6272]{1,0:T(8,128)(2,1)S(1)}, u32[]{:S(2)}, u32[]{:S(2)}) collective-permute-start(bf16[8,6272]{1,0:T(8,128)(2,1)S(1)} %shard_map.88.refs_0_), channel_id=1, source_target_pairs={{0,2},{2,4},{4,6},{6,8},{8,10},{10,12},{12,14},{14,0},{1,3},{3,5},... | collective-permute-start | bytes 301064 | tf_op jit(solution)/shard_map/ppermute | solution.py:261
  33.3 6.5 %collective-permute-start.6 = (bf16[8,6272]{1,0:T(8,128)(2,1)S(1)}, bf16[8,6272]{1,0:T(8,128)(2,1)S(1)}, u32[]{:S(2)}, u32[]{:S(2)}) collective-permute-start(bf16[8,6272]{1,0:T(8,128)(2,1)S(1)} %collective-permute-done.3.refs_1_), channel_id=1, source_target_pairs={{0,2},{2,4},{4,6},{6,8},{8,10},{10,12},{12,14},{14,0},{1,3},{3,5},... | collective-permute-start | bytes 301064 | tf_op jit(solution)/shard_map/ppermute | solution.py:261
  36.5 6.8 %collective-permute-start.8 = (bf16[8,6272]{1,0:T(8,128)(2,1)S(1)}, bf16[8,6272]{1,0:T(8,128)(2,1)S(1)}, u32[]{:S(2)}, u32[]{:S(2)}) collective-permute-start(bf16[8,6272]{1,0:T(8,128)(2,1)S(1)} %collective-permute-done.4.refs_2_), channel_id=1, source_target_pairs={{0,2},{2,4},{4,6},{6,8},{8,10},{10,12},{12,14},{14,0},{1,3},{3,5},... | collective-permute-start | bytes 301064 | tf_op jit(solution)/shard_map/ppermute | solution.py:261
  39.8 6.8 %collective-permute-start.10 = (bf16[8,6272]{1,0:T(8,128)(2,1)S(1)}, bf16[8,6272]{1,0:T(8,128)(2,1)S(1)}, u32[]{:S(2)}, u32[]{:S(2)}) collective-permute-start(bf16[8,6272]{1,0:T(8,128)(2,1)S(1)} %collective-permute-done.6.refs_4_), channel_id=1, source_target_pairs={{0,2},{2,4},{4,6},{6,8},{8,10},{10,12},{12,14},{14,0},{1,3},{3,5},... | collective-permute-start | bytes 301064 | tf_op jit(solution)/shard_map/ppermute | solution.py:261
  40.2 20.4 %collective-permute-start.18 = (bf16[48,6272]{1,0:T(8,128)(2,1)S(1)}, bf16[48,6272]{1,0:T(8,128)(2,1)S(1)}, u32[]{:S(2)}, u32[]{:S(2)}) collective-permute-start(bf16[48,6272]{1,0:T(8,128)(2,1)S(1)} %shard_map.89.refs_0_), channel_id=1, source_target_pairs={{0,1},{1,0},{2,3},{3,2},{4,5},{5,4},{6,7},{7,6},{8,9},{9,8},{10,11... | collective-permute-start | bytes 1806344 | tf_op jit(solution)/shard_map/ppermute | solution.py:257
  40.4 6.2 %collective-permute-start.13 = (bf16[8,6272]{1,0:T(8,128)(2,1)S(1)}, bf16[8,6272]{1,0:T(8,128)(2,1)S(1)}, u32[]{:S(2)}, u32[]{:S(2)}) collective-permute-start(bf16[8,6272]{1,0:T(8,128)(2,1)S(1)} %collective-permute-done.9.refs_1_), channel_id=1, source_target_pairs={{0,14},{2,0},{4,2},{6,4},{8,6},{10,8},{12,10},{14,12},{1,15},{3,1}... | collective-permute-start | bytes 301064 | tf_op jit(solution)/shard_map/ppermute | solution.py:261
  43.3 6.0 %collective-permute-start.12 = (bf16[8,6272]{1,0:T(8,128)(2,1)S(1)}, bf16[8,6272]{1,0:T(8,128)(2,1)S(1)}, u32[]{:S(2)}, u32[]{:S(2)}) collective-permute-start(bf16[8,6272]{1,0:T(8,128)(2,1)S(1)} %collective-permute-done.8.refs_0_), channel_id=1, source_target_pairs={{0,2},{2,4},{4,6},{6,8},{8,10},{10,12},{12,14},{14,0},{1,3},{3,5},... | collective-permute-start | bytes 301064 | tf_op jit(solution)/shard_map/ppermute | solution.py:261
  43.4 6.0 %collective-permute-start.15 = (bf16[8,6272]{1,0:T(8,128)(2,1)S(1)}, bf16[8,6272]{1,0:T(8,128)(2,1)S(1)}, u32[]{:S(2)}, u32[]{:S(2)}) collective-permute-start(bf16[8,6272]{1,0:T(8,128)(2,1)S(1)} %collective-permute-done.11.refs_3_), channel_id=1, source_target_pairs={{0,14},{2,0},{4,2},{6,4},{8,6},{10,8},{12,10},{14,12},{1,15},{3,1}... | collective-permute-start | bytes 301064 | tf_op jit(solution)/shard_map/ppermute | solution.py:261
  46.6 14.0 %collective-permute-start.19 = (bf16[32,6272]{1,0:T(8,128)(2,1)S(1)}, bf16[32,6272]{1,0:T(8,128)(2,1)S(1)}, u32[]{:S(2)}, u32[]{:S(2)}) collective-permute-start(bf16[32,6272]{1,0:T(8,128)(2,1)S(1)} %shard_map.90.refs_1_), channel_id=1, source_target_pairs={{0,1},{1,0},{2,3},{3,2},{4,5},{5,4},{6,7},{7,6},{8,9},{9,8},{10,11... | collective-permute-start | bytes 1204232 | tf_op jit(solution)/shard_map/ppermute | solution.py:257
  52.5 8.2 %collective-permute-start.20 = (bf16[32,6272]{1,0:T(8,128)(2,1)S(1)}, bf16[32,6272]{1,0:T(8,128)(2,1)S(1)}, u32[]{:S(2)}, u32[]{:S(2)}) collective-permute-start(bf16[32,6272]{1,0:T(8,128)(2,1)S(1)} %shard_map.91.refs_2_), channel_id=1, source_target_pairs={{0,1},{1,0},{2,3},{3,2},{4,5},{5,4},{6,7},{7,6},{8,9},{9,8},{10,11... | collective-permute-start | bytes 1204232 | tf_op jit(solution)/shard_map/ppermute | solution.py:257
  52.6 6.4 %collective-permute-start.16 = (bf16[8,6272]{1,0:T(8,128)(2,1)S(1)}, bf16[8,6272]{1,0:T(8,128)(2,1)S(1)}, u32[]{:S(2)}, u32[]{:S(2)}) collective-permute-start(bf16[8,6272]{1,0:T(8,128)(2,1)S(1)} %collective-permute-done.12.refs_0_), channel_id=1, source_target_pairs={{0,2},{2,4},{4,6},{6,8},{8,10},{10,12},{12,14},{14,0},{1,3},{3,5},... | collective-permute-start | bytes 301064 | tf_op jit(solution)/shard_map/ppermute | solution.py:261
  52.8 6.3 %collective-permute-start.17 = (bf16[8,6272]{1,0:T(8,128)(2,1)S(1)}, bf16[8,6272]{1,0:T(8,128)(2,1)S(1)}, u32[]{:S(2)}, u32[]{:S(2)}) collective-permute-start(bf16[8,6272]{1,0:T(8,128)(2,1)S(1)} %collective-permute-done.15.refs_3_), channel_id=1, source_target_pairs={{0,14},{2,0},{4,2},{6,4},{8,6},{10,8},{12,10},{14,12},{1,15},{3,1}... | collective-permute-start | bytes 301064 | tf_op jit(solution)/shard_map/ppermute | solution.py:261
  65.8 6.9 %collective-permute-start.24 = (bf16[32,6144]{1,0:T(8,128)(2,1)S(1)}, bf16[32,6144]{1,0:T(8,128)(2,1)S(1)}, u32[]{:S(2)}, u32[]{:S(2)}) collective-permute-start(bf16[32,6144]{1,0:T(8,128)(2,1)S(1)} %get-tuple-element.36), channel_id=1, source_target_pairs={{0,1},{1,0},{2,3},{3,2},{4,5},{5,4},{6,7},{7,6},{8,9},{9,8},{10,11... | collective-permute-start | bytes 1179656 | tf_op jit(solution)/shard_map/ppermute | solution.py:257
  65.9 20.5 %collective-permute-start.22 = (bf16[48,6144]{1,0:T(8,128)(2,1)S(1)}, bf16[48,6144]{1,0:T(8,128)(2,1)S(1)}, u32[]{:S(2)}, u32[]{:S(2)}) collective-permute-start(bf16[48,6144]{1,0:T(8,128)(2,1)S(1)} %get-tuple-element.32), channel_id=1, source_target_pairs={{0,1},{1,0},{2,3},{3,2},{4,5},{5,4},{6,7},{7,6},{8,9},{9,8},{10,11... | collective-permute-start | bytes 1769480 | tf_op jit(solution)/shard_map/ppermute | solution.py:257
  66.3 9.8 %collective-permute-start.23 = (bf16[32,6144]{1,0:T(8,128)(2,1)S(1)}, bf16[32,6144]{1,0:T(8,128)(2,1)S(1)}, u32[]{:S(2)}, u32[]{:S(2)}) collective-permute-start(bf16[32,6144]{1,0:T(8,128)(2,1)S(1)} %get-tuple-element.34), channel_id=1, source_target_pairs={{0,1},{1,0},{2,3},{3,2},{4,5},{5,4},{6,7},{7,6},{8,9},{9,8},{10,11... | collective-permute-start | bytes 1179656 | tf_op jit(solution)/shard_map/ppermute | solution.py:257
  69.2 6.2 %collective-permute-start.36 = (bf16[8,6144]{1,0:T(8,128)(2,1)S(1)}, bf16[8,6144]{1,0:T(8,128)(2,1)S(1)}, u32[]{:S(2)}, u32[]{:S(2)}) collective-permute-start(bf16[8,6144]{1,0:T(8,128)(2,1)S(1)} %shard_map.105), channel_id=1, source_target_pairs={{0,2},{2,4},{4,6},{6,8},{8,10},{10,12},{12,14},{14,0},{1,3},{3,5},... | collective-permute-start | bytes 294920 | tf_op jit(solution)/shard_map/ppermute | solution.py:261
  69.4 6.2 %collective-permute-start.26 = (bf16[8,6144]{1,0:T(8,128)(2,1)S(1)}, bf16[8,6144]{1,0:T(8,128)(2,1)S(1)}, u32[]{:S(2)}, u32[]{:S(2)}) collective-permute-start(bf16[8,6144]{1,0:T(8,128)(2,1)S(1)} %shard_map.94), channel_id=1, source_target_pairs={{0,14},{2,0},{4,2},{6,4},{8,6},{10,8},{12,10},{14,12},{1,15},{3,1}... | collective-permute-start | bytes 294920 | tf_op jit(solution)/shard_map/ppermute | solution.py:261
  72.7 6.6 %collective-permute-start.33 = (bf16[8,6144]{1,0:T(8,128)(2,1)S(1)}, bf16[8,6144]{1,0:T(8,128)(2,1)S(1)}, u32[]{:S(2)}, u32[]{:S(2)}) collective-permute-start(bf16[8,6144]{1,0:T(8,128)(2,1)S(1)} %shard_map.102), channel_id=1, source_target_pairs={{0,14},{2,0},{4,2},{6,4},{8,6},{10,8},{12,10},{14,12},{1,15},{3,1}... | collective-permute-start | bytes 294920 | tf_op jit(solution)/shard_map/ppermute | solution.py:261
  75.5 6.4 %collective-permute-start.37 = (bf16[8,6144]{1,0:T(8,128)(2,1)S(1)}, bf16[8,6144]{1,0:T(8,128)(2,1)S(1)}, u32[]{:S(2)}, u32[]{:S(2)}) collective-permute-start(bf16[8,6144]{1,0:T(8,128)(2,1)S(1)} %shard_map.106), channel_id=1, source_target_pairs={{0,2},{2,4},{4,6},{6,8},{8,10},{10,12},{12,14},{14,0},{1,3},{3,5},... | collective-permute-start | bytes 294920 | tf_op jit(solution)/shard_map/ppermute | solution.py:261
  75.6 7.3 %collective-permute-start.30 = (bf16[8,6144]{1,0:T(8,128)(2,1)S(1)}, bf16[8,6144]{1,0:T(8,128)(2,1)S(1)}, u32[]{:S(2)}, u32[]{:S(2)}) collective-permute-start(bf16[8,6144]{1,0:T(8,128)(2,1)S(1)} %shard_map.98), channel_id=1, source_target_pairs={{0,2},{2,4},{4,6},{6,8},{8,10},{10,12},{12,14},{14,0},{1,3},{3,5},... | collective-permute-start | bytes 294920 | tf_op jit(solution)/shard_map/ppermute | solution.py:261
  76.0 7.0 %collective-permute-start.27 = (bf16[8,6144]{1,0:T(8,128)(2,1)S(1)}, bf16[8,6144]{1,0:T(8,128)(2,1)S(1)}, u32[]{:S(2)}, u32[]{:S(2)}) collective-permute-start(bf16[8,6144]{1,0:T(8,128)(2,1)S(1)} %shard_map.95), channel_id=1, source_target_pairs={{0,14},{2,0},{4,2},{6,4},{8,6},{10,8},{12,10},{14,12},{1,15},{3,1}... | collective-permute-start | bytes 294920 | tf_op jit(solution)/shard_map/ppermute | solution.py:261
  79.4 7.0 %collective-permute-start.34 = (bf16[8,6144]{1,0:T(8,128)(2,1)S(1)}, bf16[8,6144]{1,0:T(8,128)(2,1)S(1)}, u32[]{:S(2)}, u32[]{:S(2)}) collective-permute-start(bf16[8,6144]{1,0:T(8,128)(2,1)S(1)} %shard_map.103), channel_id=1, source_target_pairs={{0,14},{2,0},{4,2},{6,4},{8,6},{10,8},{12,10},{14,12},{1,15},{3,1}... | collective-permute-start | bytes 294920 | tf_op jit(solution)/shard_map/ppermute | solution.py:261
  82.9 9.5 %collective-permute-start.31 = (bf16[8,6144]{1,0:T(8,128)(2,1)S(1)}, bf16[8,6144]{1,0:T(8,128)(2,1)S(1)}, u32[]{:S(2)}, u32[]{:S(2)}) collective-permute-start(bf16[8,6144]{1,0:T(8,128)(2,1)S(1)} %shard_map.99), channel_id=1, source_target_pairs={{0,2},{2,4},{4,6},{6,8},{8,10},{10,12},{12,14},{14,0},{1,3},{3,5},... | collective-permute-start | bytes 294920 | tf_op jit(solution)/shard_map/ppermute | solution.py:261
  86.5 6.1 %collective-permute-start.35 = (bf16[8,6144]{1,0:T(8,128)(2,1)S(1)}, bf16[8,6144]{1,0:T(8,128)(2,1)S(1)}, u32[]{:S(2)}, u32[]{:S(2)}) collective-permute-start(bf16[8,6144]{1,0:T(8,128)(2,1)S(1)} %shard_map.104), channel_id=1, source_target_pairs={{0,14},{2,0},{4,2},{6,4},{8,6},{10,8},{12,10},{14,12},{1,15},{3,1}... | collective-permute-start | bytes 294920 | tf_op jit(solution)/shard_map/ppermute | solution.py:261
  87.9 6.6 %collective-permute-start.39 = (bf16[8,6144]{1,0:T(8,128)(2,1)S(1)}, bf16[8,6144]{1,0:T(8,128)(2,1)S(1)}, u32[]{:S(2)}, u32[]{:S(2)}) collective-permute-start(bf16[8,6144]{1,0:T(8,128)(2,1)S(1)} %shard_map.108), channel_id=1, source_target_pairs={{0,2},{2,4},{4,6},{6,8},{8,10},{10,12},{12,14},{14,0},{1,3},{3,5},... | collective-permute-start | bytes 294920 | tf_op jit(solution)/shard_map/ppermute | solution.py:261
  88.8 7.2 %collective-permute-start.29 = (bf16[8,6144]{1,0:T(8,128)(2,1)S(1)}, bf16[8,6144]{1,0:T(8,128)(2,1)S(1)}, u32[]{:S(2)}, u32[]{:S(2)}) collective-permute-start(bf16[8,6144]{1,0:T(8,128)(2,1)S(1)} %shard_map.97), channel_id=1, source_target_pairs={{0,14},{2,0},{4,2},{6,4},{8,6},{10,8},{12,10},{14,12},{1,15},{3,1}... | collective-permute-start | bytes 294920 | tf_op jit(solution)/shard_map/ppermute | solution.py:261
  99.3 8.7 %collective-permute-start.41 = (bf16[2,6144]{1,0:T(2,128)(2,1)S(1)}, bf16[2,6144]{1,0:T(2,128)(2,1)S(1)}, u32[]{:S(2)}, u32[]{:S(2)}) collective-permute-start(bf16[2,6144]{1,0:T(2,128)(2,1)S(1)} %get-tuple-element.40), channel_id=1, source_target_pairs={{0,96},{32,0},{64,32},{96,64},{1,97},{33,1},{65,33},{97,65},{2,98}... | collective-permute-start | bytes 73736 | tf_op jit(solution)/shard_map/ppermute | solution.py:253
  103.1 7.7 %collective-permute-start.42 = (bf16[2,6144]{1,0:T(2,128)(2,1)S(1)}, bf16[2,6144]{1,0:T(2,128)(2,1)S(1)}, u32[]{:S(2)}, u32[]{:S(2)}) collective-permute-start(bf16[2,6144]{1,0:T(2,128)(2,1)S(1)} %get-tuple-element.41), channel_id=1, source_target_pairs={{0,64},{32,96},{64,0},{96,32},{1,65},{33,97},{65,1},{97,33},{2,66}... | collective-permute-start | bytes 73736 | tf_op jit(solution)/shard_map/ppermute | solution.py:253
  (12 other events, 59.4 us)

commit v3 on v2

--- a/solution.py
+++ b/solution.py
@@ -58,10 +58,7 @@
     slots_hbm,
     tok_hbm,
     router_hbm,
-    own,
-    s1,
-    s2,
-    s3,
+    out,
     cw_ref,
     tok_ref,
     router_ref,
@@ -77,7 +74,6 @@
     ]
     for copy in copies:
         copy.start()
-    here = lax.axis_index("xo")
     count, width = tok_ref.shape
     for copy in copies:
         copy.wait()
@@ -116,8 +112,7 @@
     gates = [v / total for v in chosen]
     lane = lax.broadcasted_iota(jnp.int32, (count, LANES), 1)
     weights = jnp.zeros((count, LANES), F32)
-    for j, out in enumerate((own, s1, s2, s3)):
-        expert = lax.rem(here + j, EXPERTS)
+    for expert in range(EXPERTS):
         rows = []
         for s in range(CAP):
             row = jnp.zeros((1, width), F32)
@@ -131,20 +126,19 @@
             for k in range(2):
                 match = (ids[k] == expert) & (slots[k] == s)
                 column = jnp.where(match, gates[k], column)
-            weights = jnp.where(lane == j * CAP + s, column, weights)
-        out[:, :width] = jnp.concatenate(rows, axis=0).astype(BF16)
-        out[:, width:] = statistic
+            weights = jnp.where(lane == expert * CAP + s, column, weights)
+        rows = jnp.concatenate(rows, axis=0).astype(BF16)
+        for column in range(PAIR):
+            out[expert * PAIR + column, :, :width] = rows
+            out[expert * PAIR + column, :, width:] = statistic
     cw_ref[...] = weights
 
 
-def in_hbm(value):
-    return pltpu.with_memory_space_constraint(value, pltpu.HBM)
-
-
-def join_kernel(own, r1, r2, r3, unread, out):
-    out[...] = jnp.concatenate([ref[...].astype(F32) for ref in (own, r1, r2, r3)], axis=0).astype(
-        out.dtype
-    )
+def halves_kernel(rows_ref, unread, a_ref, b_ref):
+    half = rows_ref.shape[0] // 2
+    for n, out in enumerate((a_ref, b_ref)):
+        rows = [rows_ref[n * half + i].astype(F32) for i in range(half)]
+        out[...] = jnp.concatenate(rows, axis=0).astype(out.dtype)
 
 
 def stack_kernel(count, *refs):
@@ -227,19 +221,25 @@
     out[...] = value.astype(out.dtype)
 
 
-def part_kernel(a_ref, came_ref, own, s1, s2, s3):
-    total = a_ref[...] + came_ref[...].astype(F32)
-    for j, out in enumerate((own, s1, s2, s3)):
-        out[...] = total[j * CAP : (j + 1) * CAP].astype(out.dtype)
-
-
-def mix_kernel(cw_ref, own, r1, r2, r3, out):
+def last_kernel(kept_ref, crossed_ref, *refs):
+    out = refs[-1]
+    half = out.shape[0] // 2
+    size = half * CAP
+    for b in range(2):
+        at = slice(b * size, (b + 1) * size)
+        total = kept_ref[at, :] + crossed_ref[at, :].astype(F32)
+        total = total + refs[2 * b][...].astype(F32) + refs[2 * b + 1][...].astype(F32)
+        for n in range(half):
+            out[b * half + n] = total[n * CAP : (n + 1) * CAP].astype(out.dtype)
+
+
+def mix_kernel(cw_ref, rows_ref, out):
     weights = cw_ref[...]
     total = None
-    for j, ref in enumerate((own, r1, r2, r3)):
-        value = ref[...].astype(F32)
+    for expert in range(EXPERTS):
+        value = rows_ref[expert * PAIR].astype(F32) + rows_ref[expert * PAIR + 1].astype(F32)
         for s in range(CAP):
-            at = j * CAP + s
+            at = expert * CAP + s
             term = weights[:, at : at + 1] * value[s : s + 1, :]
             total = term if total is None else total + term
     out[...] = total.astype(out.dtype)
@@ -249,8 +249,8 @@
     return pltpu.with_memory_space_constraint(value, pltpu.HBM)
 
 
-def to_expert(value, step):
-    return lax.ppermute(value, "xo", [(i, (i + step) % EXPERTS) for i in range(EXPERTS)])
+def across(value):
+    return lax.all_to_all(value, ("xo", "xi"), split_axis=0, concat_axis=0, tiled=True)
 
 
 def swap(value, axis):
@@ -266,9 +266,13 @@
     count, width = tokens.shape
     wide = width + LANES
     hbm = pl.BlockSpec(memory_space=pltpu.HBM)
-    *sends, weights = call(
+    columns = EXPERTS * PAIR
+    packed, weights = call(
         pack_kernel,
-        [shape(CAP, wide, BF16)] * EXPERTS + [shape(count, LANES, F32)],
+        [
+            jax.ShapeDtypeStruct((columns, CAP, wide), BF16),
+            shape(count, LANES, F32),
+        ],
         [in_hbm(a) for a in (expert_ids.T, slots.T, tokens, router_weight.T)],
         in_specs=[hbm] * 4,
         scratch=[
@@ -279,16 +283,14 @@
             pltpu.SemaphoreType.DMA((4,)),
         ],
     )
-    arrived = [sends[0]] + [to_expert(sends[k], k) for k in range(1, EXPERTS)]
-    size = EXPERTS * CAP
-    gate_near, up_near, down_near = fetch([gate_weight, up_weight, down_weight], sends[0])
-    block_a = call(
-        join_kernel,
-        [shape(size, wide, BF16)],
-        (*arrived, gate_near),
-        in_specs=vmem(EXPERTS) + [pl.BlockSpec(memory_space=pl.ANY)],
-    )[0]
-    block_b = swap(block_a, "xi")
+    gate_near, up_near, down_near = fetch([gate_weight, up_weight, down_weight], packed)
+    size = columns * CAP // 2
+    block_a, block_b = call(
+        halves_kernel,
+        [shape(size, wide, BF16)] * 2,
+        (across(packed), gate_near),
+        in_specs=vmem(1) + [pl.BlockSpec(memory_space=pl.ANY)],
+    )
 
     got = {}
     for b, block in enumerate((block_a, block_b)):
@@ -348,20 +350,12 @@
                     [kept[group], crossed[group]] + came,
                 )[0]
                 moving[b, sign] = along(value, -sign)
-    sums = []
-    for b, dtype in ((1, BF16), (0, F32)):
-        sums += call(
-            functools.partial(add_kernel, b * size),
-            [shape(size, width, dtype)],
-            (kept[0], crossed[0], moving[b, 1], moving[b, -1]),
-        )
-    pieces = call(
-        part_kernel,
-        [shape(CAP, width, F32)] + [shape(CAP, width, BF16)] * 3,
-        (sums[1], swap(sums[0], "xi")),
-    )
-    returned = [pieces[0]] + [to_expert(pieces[k], -k) for k in range(1, EXPERTS)]
-    mixed_rows = call(mix_kernel, [shape(count, width, BF16)], (weights, *returned))[0]
+    sums = call(
+        last_kernel,
+        [jax.ShapeDtypeStruct((columns, CAP, width), BF16)],
+        (kept[0], crossed[0], *[moving[b, sign] for b in (0, 1) for sign in (1, -1)]),
+    )[0]
+    mixed_rows = call(mix_kernel, [shape(count, width, BF16)], (weights, across(sums)))[0]
     return (mixed_rows, balance)
 
 

time: 114 us -> 122 us (1.070)
  blocking collectives: 0 us -> 14.5 us
  starting transfers between devices: 75.7 us -> 67.7 us
  local copies, waits for them, and re-layouts: 0 us -> 3.34 us
  waiting for transfers between devices: 25.7 us -> 23 us
    all_to_all x0 -> x1, starting transfers between devices: none -> 22.7 us  [across(): lax.all_to_all(value, ('xo', 'xi'), split_axis=0, concat_axis=0, tiled=True)]
    ppermute x6 -> x0, starting transfers between devices: 18.1 us -> none  [to_expert(): lax.ppermute(value, 'xo', [(i, (i + step) % EXPERTS) for i in range(EXPER...]
    ppermute x10 -> x8, starting transfers between devices: 17.8 us -> 1.77 us  [swap(): return lax.ppermute(value, axis, [(0, 1), (1, 0)])]
    all_to_all x0 -> x1, blocking collectives: none -> 14.5 us  [across(): lax.all_to_all(value, ('xo', 'xi'), split_axis=0, concat_axis=0, tiled=True)]
    ppermute x6 -> x0, waiting for transfers between devices: 5.3 us -> none  [to_expert(): lax.ppermute(value, 'xo', [(i, (i + step) % EXPERTS) for i in range(EXPER...]
    ppermute x28, starting transfers between devices: 39.7 us -> 43.3 us  [along(): lax.ppermute(value, 'y', [(y, (y + step) % RING) for y in range(RING)])]
    unnamed x0 -> x8, local copies, waits for them, and re-layouts: none -> 3.34 us
    ppermute x28, waiting for transfers between devices: 15.1 us -> 18.1 us  [along(): lax.ppermute(value, 'y', [(y, (y + step) % RING) for y in range(RING)])]
  transfers between devices with their start and end apart: 44 -> 37, of which waited for: 15 -> 10; matrix products, arithmetic and copies ran while one was open for 0% -> 0% of each run, Pallas kernels for 4% -> 4%
where the time goes in v3:
time: 122 us
  starting transfers between devices  67.7 us (55%)
  waiting for transfers between devices  23 us (19%)
  blocking collectives  14.5 us (12%)
  Pallas kernels  12.6 us (10%)
  local copies, waits for them, and re-layouts  3.34 us (3%)
    ppermute x28, starting transfers between devices, along(): lax.ppermute(value, 'y', [(y, (y + step) % RING) for y in range(RING)])  43.3 us
    all_to_all x1, starting transfers between devices, across(): lax.all_to_all(value, ('xo', 'xi'), split_axis=0, concat_axis=0, tiled=True)  22.7 us
    ppermute x28, waiting for transfers between devices, along(): lax.ppermute(value, 'y', [(y, (y + step) % RING) for y in range(RING)])  18.1 us
    all_to_all x1, blocking collectives, across(): lax.all_to_all(value, ('xo', 'xi'), split_axis=0, concat_axis=0, tiled=True)  14.5 us
    pallas_call x1, Pallas kernels, local(): pl.pallas_call(functools.partial(expert_kernel, scale, groups), out_shape...  5.08 us
    ppermute x8, waiting for transfers between devices, swap(): return lax.ppermute(value, axis, [(0, 1), (1, 0)])  3.81 us
    pallas_call x22, Pallas kernels, call(): pl.pallas_call(kernel, out_shape=outs, in_specs=in_specs or vmem(len(args...  3.79 us
    pallas_call x1, Pallas kernels, fetch(): pl.pallas_call(fetch_kernel, out_shape=[pltpu.VMEM(w.shape, w.dtype) for...  3.78 us
  transfers between devices with their start and end apart: 37, of which 10 were waited for; matrix products, arithmetic and copies ran while one was open for 0% of the time, Pallas kernels for 4%

profile of v3, /device:TPU:514, one launch (start us, length us, event | category | flops | bytes accessed | tf_op | source)
XLA Modules:
  0.0 122.2 jit_solution(4137324822983296139)
XLA Ops:
  0.6 2.1 %shard_map.86 = (bf16[8,2,6272]{2,1,0:T(2,128)(2,1)}, f32[4,128]{1,0:T(4,128)S(1)}) custom-call(s32[2,4]{1,0:T(2,128)} %bitcast.5, s32[2,4]{1,0:T(2,128)} %bitcast.6, bf16[4,6144]{1,0:T(4,128)(2,1)} %tok_hbm.1, bf16[4,6144]{1,0:T(4,128)(2,1)} %bitcast.4), custom_call_target="tpu_custom_call" | custom-call | flops 200000 | bytes 1000000 | tf_op jit(solution)/shard_map/pallas_call | solution.py:33
  2.7 22.7 %all-to-all-start = ((bf16[8,2,6272]{2,1,0:T(2,128)(2,1)}), bf16[8,2,6272]{2,1,0:T(2,128)(2,1)S(1)}, u32[]{:S(2)}, u32[]{:S(2)}) async-start(bf16[8,2,6272]{2,1,0:T(2,128)(2,1)} %get-tuple-element.19.refs_3_), calls=%async_computation | async-start | bytes 401408 | tf_op jit(solution)/shard_map/all_to_all | solution.py:253
  25.4 3.8 %shard_map.87 = (bf16[6144,256]{1,0:T(8,128)(2,1)S(1)}, bf16[6144,256]{1,0:T(8,128)(2,1)S(1)}, bf16[256,6144]{1,0:T(8,128)(2,1)S(1)}) custom-call(bf16[6144,256]{1,0:T(8,128)(2,1)} %refs_0_.1, bf16[6144,256]{1,0:T(8,128)(2,1)} %refs_1_.1, bf16[256,6144]{1,0:T(8,128)(2,1)} %refs_2_.1, bf16[8,2,6272]{2,1,0:T(2,128)(2,1)} %get-tuple-element.19.refs_3_), custom_call_target="tpu_custom_call" | custom-call | flops 1000000 | bytes 18874368 | tf_op jit(solution)/shard_map/pallas_call | solution.py:199
  29.2 1.6 %copy-done = bf16[6144,256]{1,0:T(8,128)(2,1)} copy-done((bf16[6144,256]{1,0:T(8,128)(2,1)}, bf16[6144,256]{1,0:T(8,128)(2,1)S(1)}, u32[]{:S(2)}) %copy-start) | copy-done | bytes 3145752
  30.9 1.7 %copy-done.2 = bf16[256,6144]{1,0:T(8,128)(2,1)} copy-done((bf16[256,6144]{1,0:T(8,128)(2,1)}, bf16[256,6144]{1,0:T(8,128)(2,1)S(1)}, u32[]{:S(2)}) %copy-start.2) | copy-done | bytes 3145752
  32.6 1.1 all-to-all-done.rows_ref
  33.9 2.0 %collective-permute-start = (bf16[8,6272]{1,0:T(8,128)(2,1)S(1)}, bf16[8,6272]{1,0:T(8,128)(2,1)S(1)}, u32[]{:S(2)}, u32[]{:S(2)}) collective-permute-start(bf16[8,6272]{1,0:T(8,128)(2,1)S(1)} %get-tuple-element.21.refs_0_), channel_id=1, source_target_pairs={{0,2},{2,4},{4,6},{6,8},{8,10},{10,12},{12,14},{14,0},{1,3},{3,5},... | collective-permute-start | bytes 301064 | tf_op jit(solution)/shard_map/ppermute | solution.py:261
  35.9 1.4 %collective-permute-start.3 = (bf16[8,6272]{1,0:T(8,128)(2,1)S(1)}, bf16[8,6272]{1,0:T(8,128)(2,1)S(1)}, u32[]{:S(2)}, u32[]{:S(2)}) collective-permute-start(bf16[8,6272]{1,0:T(8,128)(2,1)S(1)} %get-tuple-element.22.refs_1_), channel_id=1, source_target_pairs={{0,14},{2,0},{4,2},{6,4},{8,6},{10,8},{12,10},{14,12},{1,15},{3,1}... | collective-permute-start | bytes 301064 | tf_op jit(solution)/shard_map/ppermute | solution.py:261
  37.9 1.4 %collective-permute-done.1.refs_3_ = bf16[8,6272]{1,0:T(8,128)(2,1)S(1)} collective-permute-done((bf16[8,6272]{1,0:T(8,128)(2,1)S(1)}, bf16[8,6272]{1,0:T(8,128)(2,1)S(1)}, u32[]{:S(2)}, u32[]{:S(2)}) %collective-permute-start.1) | collective-permute-done | bytes 100384 | tf_op jit(solution)/shard_map/ppermute | solution.py:261
  39.3 1.4 %collective-permute-start.5 = (bf16[8,6272]{1,0:T(8,128)(2,1)S(1)}, bf16[8,6272]{1,0:T(8,128)(2,1)S(1)}, u32[]{:S(2)}, u32[]{:S(2)}) collective-permute-start(bf16[8,6272]{1,0:T(8,128)(2,1)S(1)} %collective-permute-done.1.refs_3_), channel_id=1, source_target_pairs={{0,14},{2,0},{4,2},{6,4},{8,6},{10,8},{12,10},{14,12},{1,15},{3,1}... | collective-permute-start | bytes 301064 | tf_op jit(solution)/shard_map/ppermute | solution.py:261
  41.3 2.6 %collective-permute-start.7 = (bf16[8,6272]{1,0:T(8,128)(2,1)S(1)}, bf16[8,6272]{1,0:T(8,128)(2,1)S(1)}, u32[]{:S(2)}, u32[]{:S(2)}) collective-permute-start(bf16[8,6272]{1,0:T(8,128)(2,1)S(1)} %collective-permute-done.3.refs_5_), channel_id=1, source_target_pairs={{0,14},{2,0},{4,2},{6,4},{8,6},{10,8},{12,10},{14,12},{1,15},{3,1}... | collective-permute-start | bytes 301064 | tf_op jit(solution)/shard_map/ppermute | solution.py:261
  44.1 3.3 %collective-permute-start.9 = (bf16[8,6272]{1,0:T(8,128)(2,1)S(1)}, bf16[8,6272]{1,0:T(8,128)(2,1)S(1)}, u32[]{:S(2)}, u32[]{:S(2)}) collective-permute-start(bf16[8,6272]{1,0:T(8,128)(2,1)S(1)} %collective-permute-done.5.refs_1_), channel_id=1, source_target_pairs={{0,14},{2,0},{4,2},{6,4},{8,6},{10,8},{12,10},{14,12},{1,15},{3,1}... | collective-permute-start | bytes 301064 | tf_op jit(solution)/shard_map/ppermute | solution.py:261
  47.5 3.2 %collective-permute-start.11 = (bf16[8,6272]{1,0:T(8,128)(2,1)S(1)}, bf16[8,6272]{1,0:T(8,128)(2,1)S(1)}, u32[]{:S(2)}, u32[]{:S(2)}) collective-permute-start(bf16[8,6272]{1,0:T(8,128)(2,1)S(1)} %collective-permute-done.7.refs_3_), channel_id=1, source_target_pairs={{0,14},{2,0},{4,2},{6,4},{8,6},{10,8},{12,10},{14,12},{1,15},{3,1}... | collective-permute-start | bytes 301064 | tf_op jit(solution)/shard_map/ppermute | solution.py:261
  50.9 2.6 %collective-permute-done.8.refs_0_ = bf16[8,6272]{1,0:T(8,128)(2,1)S(1)} collective-permute-done((bf16[8,6272]{1,0:T(8,128)(2,1)S(1)}, bf16[8,6272]{1,0:T(8,128)(2,1)S(1)}, u32[]{:S(2)}, u32[]{:S(2)}) %collective-permute-start.8) | collective-permute-done | bytes 100384 | tf_op jit(solution)/shard_map/ppermute | solution.py:261
  53.5 3.1 %collective-permute-done.10.refs_2_ = bf16[8,6272]{1,0:T(8,128)(2,1)S(1)} collective-permute-done((bf16[8,6272]{1,0:T(8,128)(2,1)S(1)}, bf16[8,6272]{1,0:T(8,128)(2,1)S(1)}, u32[]{:S(2)}, u32[]{:S(2)}) %collective-permute-start.10) | collective-permute-done | bytes 100384 | tf_op jit(solution)/shard_map/ppermute | solution.py:261
  57.1 3.2 %collective-permute-start.13 = (bf16[8,6272]{1,0:T(8,128)(2,1)S(1)}, bf16[8,6272]{1,0:T(8,128)(2,1)S(1)}, u32[]{:S(2)}, u32[]{:S(2)}) collective-permute-start(bf16[8,6272]{1,0:T(8,128)(2,1)S(1)} %collective-permute-done.11.refs_3_), channel_id=1, source_target_pairs={{0,14},{2,0},{4,2},{6,4},{8,6},{10,8},{12,10},{14,12},{1,15},{3,1}... | collective-permute-start | bytes 301064 | tf_op jit(solution)/shard_map/ppermute | solution.py:261
  60.3 3.1 %collective-permute-done.12.refs_0_ = bf16[8,6272]{1,0:T(8,128)(2,1)S(1)} collective-permute-done((bf16[8,6272]{1,0:T(8,128)(2,1)S(1)}, bf16[8,6272]{1,0:T(8,128)(2,1)S(1)}, u32[]{:S(2)}, u32[]{:S(2)}) %collective-permute-start.12) | collective-permute-done | bytes 100384 | tf_op jit(solution)/shard_map/ppermute | solution.py:261
  63.5 1.4 %collective-permute-done.17.refs_7_ = bf16[16,6272]{1,0:T(8,128)(2,1)S(1)} collective-permute-done((bf16[16,6272]{1,0:T(8,128)(2,1)S(1)}, bf16[16,6272]{1,0:T(8,128)(2,1)S(1)}, u32[]{:S(2)}, u32[]{:S(2)}) %collective-permute-start.17) | collective-permute-done | bytes 200736 | tf_op jit(solution)/shard_map/ppermute | solution.py:257
  65.0 5.1 %shard_map.93 = (f32[48,6144]{1,0:T(8,128)S(1)}, f32[32,6144]{1,0:T(8,128)S(1)}, f32[32,6144]{1,0:T(8,128)S(1)}, f32[16,6144]{1,0:T(8,128)S(1)}, bf16[48,6144]{1...) custom-call(bf16[48,6272]{1,0:T(8,128)(2,1)S(1)} %shard_map.89.refs_, ...), custom_call_target="tpu_custom_call" | custom-call | flops 2415919104 | bytes 9000000 | tf_op jit(solution)/shard_map/pallas_call | solution.py:317
  71.1 2.4 %collective-permute-done.21.crossed_ref = bf16[16,6144]{1,0:T(8,128)(2,1)S(1)} collective-permute-done((bf16[16,6144]{1,0:T(8,128)(2,1)S(1)}, bf16[16,6144]{1,0:T(8,128)(2,1)S(1)}, u32[]{:S(2)}, u32[]{:S(2)}) %collective-permute-start.21) | collective-permute-done | bytes 196640 | tf_op jit(solution)/shard_map/ppermute | solution.py:257
  73.5 3.1 %collective-permute-start.22 = (bf16[8,6144]{1,0:T(8,128)(2,1)S(1)}, bf16[8,6144]{1,0:T(8,128)(2,1)S(1)}, u32[]{:S(2)}, u32[]{:S(2)}) collective-permute-start(bf16[8,6144]{1,0:T(8,128)(2,1)S(1)} %shard_map.94), channel_id=1, source_target_pairs={{0,14},{2,0},{4,2},{6,4},{8,6},{10,8},{12,10},{14,12},{1,15},{3,1}... | collective-permute-start | bytes 294920 | tf_op jit(solution)/shard_map/ppermute | solution.py:261
  76.7 2.2 %collective-permute-done.22.refs_0_ = bf16[8,6144]{1,0:T(8,128)(2,1)S(1)} collective-permute-done((bf16[8,6144]{1,0:T(8,128)(2,1)S(1)}, bf16[8,6144]{1,0:T(8,128)(2,1)S(1)}, u32[]{:S(2)}, u32[]{:S(2)}) %collective-permute-start.22) | collective-permute-done | bytes 98336 | tf_op jit(solution)/shard_map/ppermute | solution.py:261
  79.0 3.8 %collective-permute-start.23 = (bf16[8,6144]{1,0:T(8,128)(2,1)S(1)}, bf16[8,6144]{1,0:T(8,128)(2,1)S(1)}, u32[]{:S(2)}, u32[]{:S(2)}) collective-permute-start(bf16[8,6144]{1,0:T(8,128)(2,1)S(1)} %shard_map.95), channel_id=1, source_target_pairs={{0,14},{2,0},{4,2},{6,4},{8,6},{10,8},{12,10},{14,12},{1,15},{3,1}... | collective-permute-start | bytes 294920 | tf_op jit(solution)/shard_map/ppermute | solution.py:261
  83.0 3.3 %collective-permute-start.29 = (bf16[8,6144]{1,0:T(8,128)(2,1)S(1)}, bf16[8,6144]{1,0:T(8,128)(2,1)S(1)}, u32[]{:S(2)}, u32[]{:S(2)}) collective-permute-start(bf16[8,6144]{1,0:T(8,128)(2,1)S(1)} %shard_map.101), channel_id=1, source_target_pairs={{0,14},{2,0},{4,2},{6,4},{8,6},{10,8},{12,10},{14,12},{1,15},{3,1}... | collective-permute-start | bytes 294920 | tf_op jit(solution)/shard_map/ppermute | solution.py:261
  86.5 3.3 %collective-permute-start.24 = (bf16[8,6144]{1,0:T(8,128)(2,1)S(1)}, bf16[8,6144]{1,0:T(8,128)(2,1)S(1)}, u32[]{:S(2)}, u32[]{:S(2)}) collective-permute-start(bf16[8,6144]{1,0:T(8,128)(2,1)S(1)} %shard_map.96), channel_id=1, source_target_pairs={{0,14},{2,0},{4,2},{6,4},{8,6},{10,8},{12,10},{14,12},{1,15},{3,1}... | collective-permute-start | bytes 294920 | tf_op jit(solution)/shard_map/ppermute | solution.py:261
  90.3 3.3 %collective-permute-start.30 = (bf16[8,6144]{1,0:T(8,128)(2,1)S(1)}, bf16[8,6144]{1,0:T(8,128)(2,1)S(1)}, u32[]{:S(2)}, u32[]{:S(2)}) collective-permute-start(bf16[8,6144]{1,0:T(8,128)(2,1)S(1)} %shard_map.102), channel_id=1, source_target_pairs={{0,14},{2,0},{4,2},{6,4},{8,6},{10,8},{12,10},{14,12},{1,15},{3,1}... | collective-permute-start | bytes 294920 | tf_op jit(solution)/shard_map/ppermute | solution.py:261
  93.8 3.3 %collective-permute-start.25 = (bf16[8,6144]{1,0:T(8,128)(2,1)S(1)}, bf16[8,6144]{1,0:T(8,128)(2,1)S(1)}, u32[]{:S(2)}, u32[]{:S(2)}) collective-permute-start(bf16[8,6144]{1,0:T(8,128)(2,1)S(1)} %shard_map.97), channel_id=1, source_target_pairs={{0,14},{2,0},{4,2},{6,4},{8,6},{10,8},{12,10},{14,12},{1,15},{3,1}... | collective-permute-start | bytes 294920 | tf_op jit(solution)/shard_map/ppermute | solution.py:261
  97.4 3.3 %collective-permute-start.31 = (bf16[8,6144]{1,0:T(8,128)(2,1)S(1)}, bf16[8,6144]{1,0:T(8,128)(2,1)S(1)}, u32[]{:S(2)}, u32[]{:S(2)}) collective-permute-start(bf16[8,6144]{1,0:T(8,128)(2,1)S(1)} %shard_map.103), channel_id=1, source_target_pairs={{0,14},{2,0},{4,2},{6,4},{8,6},{10,8},{12,10},{14,12},{1,15},{3,1}... | collective-permute-start | bytes 294920 | tf_op jit(solution)/shard_map/ppermute | solution.py:261
  100.9 2.2 %collective-permute-done.28.refs_1_ = bf16[8,6144]{1,0:T(8,128)(2,1)S(1)} collective-permute-done((bf16[8,6144]{1,0:T(8,128)(2,1)S(1)}, bf16[8,6144]{1,0:T(8,128)(2,1)S(1)}, u32[]{:S(2)}, u32[]{:S(2)}) %collective-permute-start.28) | collective-permute-done | bytes 98336 | tf_op jit(solution)/shard_map/ppermute | solution.py:261
  103.1 3.5 %collective-permute-done.35.refs_3_ = bf16[8,6144]{1,0:T(8,128)(2,1)S(1)} collective-permute-done((bf16[8,6144]{1,0:T(8,128)(2,1)S(1)}, bf16[8,6144]{1,0:T(8,128)(2,1)S(1)}, u32[]{:S(2)}, u32[]{:S(2)}) %collective-permute-start.35) | collective-permute-done | bytes 98336 | tf_op jit(solution)/shard_map/ppermute | solution.py:261
  106.8 14.5 %all_to_all.10.rows_ref = bf16[8,2,6144]{2,1,0:T(2,128)(2,1)S(1)} all-to-all(bf16[8,2,6144]{2,1,0:T(2,128)(2,1)S(1)} %shard_map.108), channel_id=1, replica_groups=mesh['groups'=2,'xo'=4,'xi'=2,'y'=8,'core'=2] {'xo','xi'}, dimensions={0} | all-to-all | bytes 393216 | tf_op jit(solution)/shard_map/all_to_all | solution.py:253
  121.3 0.9 shard_map.109
  (75 shorter events, 5.4 us)
Async XLA Ops:
  2.7 30.9 %all-to-all-start = ((bf16[8,2,6272]{2,1,0:T(2,128)(2,1)}), bf16[8,2,6272]{2,1,0:T(2,128)(2,1)S(1)}, u32[]{:S(2)}, u32[]{:S(2)}) async-start(bf16[8,2,6272]{2,1,0:T(2,128)(2,1)} %get-tuple-element.19.refs_3_), calls=%async_computation | async-start | bytes 401408 | tf_op jit(solution)/shard_map/all_to_all | solution.py:253
  33.8 5.5 %collective-permute-start.1 = (bf16[8,6272]{1,0:T(8,128)(2,1)S(1)}, bf16[8,6272]{1,0:T(8,128)(2,1)S(1)}, u32[]{:S(2)}, u32[]{:S(2)}) collective-permute-start(bf16[8,6272]{1,0:T(8,128)(2,1)S(1)} %get-tuple-element.21.refs_0_), channel_id=1, source_target_pairs={{0,14},{2,0},{4,2},{6,4},{8,6},{10,8},{12,10},{14,12},{1,15},{3,1}... | collective-permute-start | bytes 301064 | tf_op jit(solution)/shard_map/ppermute | solution.py:261
  33.9 6.7 %collective-permute-start = (bf16[8,6272]{1,0:T(8,128)(2,1)S(1)}, bf16[8,6272]{1,0:T(8,128)(2,1)S(1)}, u32[]{:S(2)}, u32[]{:S(2)}) collective-permute-start(bf16[8,6272]{1,0:T(8,128)(2,1)S(1)} %get-tuple-element.21.refs_0_), channel_id=1, source_target_pairs={{0,2},{2,4},{4,6},{6,8},{8,10},{10,12},{12,14},{14,0},{1,3},{3,5},... | collective-permute-start | bytes 301064 | tf_op jit(solution)/shard_map/ppermute | solution.py:261
  37.3 6.6 %collective-permute-start.2 = (bf16[8,6272]{1,0:T(8,128)(2,1)S(1)}, bf16[8,6272]{1,0:T(8,128)(2,1)S(1)}, u32[]{:S(2)}, u32[]{:S(2)}) collective-permute-start(bf16[8,6272]{1,0:T(8,128)(2,1)S(1)} %get-tuple-element.22.refs_1_), channel_id=1, source_target_pairs={{0,2},{2,4},{4,6},{6,8},{8,10},{10,12},{12,14},{14,0},{1,3},{3,5},... | collective-permute-start | bytes 301064 | tf_op jit(solution)/shard_map/ppermute | solution.py:261
  40.7 6.8 %collective-permute-start.4 = (bf16[8,6272]{1,0:T(8,128)(2,1)S(1)}, bf16[8,6272]{1,0:T(8,128)(2,1)S(1)}, u32[]{:S(2)}, u32[]{:S(2)}) collective-permute-start(bf16[8,6272]{1,0:T(8,128)(2,1)S(1)} %collective-permute-done.refs_2_), channel_id=1, source_target_pairs={{0,2},{2,4},{4,6},{6,8},{8,10},{10,12},{12,14},{14,0},{1,3},{3,5},... | collective-permute-start | bytes 301064 | tf_op jit(solution)/shard_map/ppermute | solution.py:261
  41.3 6.1 %collective-permute-start.7 = (bf16[8,6272]{1,0:T(8,128)(2,1)S(1)}, bf16[8,6272]{1,0:T(8,128)(2,1)S(1)}, u32[]{:S(2)}, u32[]{:S(2)}) collective-permute-start(bf16[8,6272]{1,0:T(8,128)(2,1)S(1)} %collective-permute-done.3.refs_5_), channel_id=1, source_target_pairs={{0,14},{2,0},{4,2},{6,4},{8,6},{10,8},{12,10},{14,12},{1,15},{3,1}... | collective-permute-start | bytes 301064 | tf_op jit(solution)/shard_map/ppermute | solution.py:261
  43.9 6.8 %collective-permute-start.6 = (bf16[8,6272]{1,0:T(8,128)(2,1)S(1)}, bf16[8,6272]{1,0:T(8,128)(2,1)S(1)}, u32[]{:S(2)}, u32[]{:S(2)}) collective-permute-start(bf16[8,6272]{1,0:T(8,128)(2,1)S(1)} %collective-permute-done.2.refs_4_), channel_id=1, source_target_pairs={{0,2},{2,4},{4,6},{6,8},{8,10},{10,12},{12,14},{14,0},{1,3},{3,5},... | collective-permute-start | bytes 301064 | tf_op jit(solution)/shard_map/ppermute | solution.py:261
  43.9 21.0 %collective-permute-start.14 = (bf16[48,6272]{1,0:T(8,128)(2,1)S(1)}, bf16[48,6272]{1,0:T(8,128)(2,1)S(1)}, u32[]{:S(2)}, u32[]{:S(2)}) collective-permute-start(bf16[48,6272]{1,0:T(8,128)(2,1)S(1)} %shard_map.89.refs_0_), channel_id=1, source_target_pairs={{0,1},{1,0},{2,3},{3,2},{4,5},{5,4},{6,7},{7,6},{8,9},{9,8},{10,11... | collective-permute-start | bytes 1806344 | tf_op jit(solution)/shard_map/ppermute | solution.py:257
  44.1 6.6 %collective-permute-start.9 = (bf16[8,6272]{1,0:T(8,128)(2,1)S(1)}, bf16[8,6272]{1,0:T(8,128)(2,1)S(1)}, u32[]{:S(2)}, u32[]{:S(2)}) collective-permute-start(bf16[8,6272]{1,0:T(8,128)(2,1)S(1)} %collective-permute-done.5.refs_1_), channel_id=1, source_target_pairs={{0,14},{2,0},{4,2},{6,4},{8,6},{10,8},{12,10},{14,12},{1,15},{3,1}... | collective-permute-start | bytes 301064 | tf_op jit(solution)/shard_map/ppermute | solution.py:261
  47.5 6.0 %collective-permute-start.8 = (bf16[8,6272]{1,0:T(8,128)(2,1)S(1)}, bf16[8,6272]{1,0:T(8,128)(2,1)S(1)}, u32[]{:S(2)}, u32[]{:S(2)}) collective-permute-start(bf16[8,6272]{1,0:T(8,128)(2,1)S(1)} %collective-permute-done.4.refs_0_), channel_id=1, source_target_pairs={{0,2},{2,4},{4,6},{6,8},{8,10},{10,12},{12,14},{14,0},{1,3},{3,5},... | collective-permute-start | bytes 301064 | tf_op jit(solution)/shard_map/ppermute | solution.py:261
  47.5 6.0 %collective-permute-start.11 = (bf16[8,6272]{1,0:T(8,128)(2,1)S(1)}, bf16[8,6272]{1,0:T(8,128)(2,1)S(1)}, u32[]{:S(2)}, u32[]{:S(2)}) collective-permute-start(bf16[8,6272]{1,0:T(8,128)(2,1)S(1)} %collective-permute-done.7.refs_3_), channel_id=1, source_target_pairs={{0,14},{2,0},{4,2},{6,4},{8,6},{10,8},{12,10},{14,12},{1,15},{3,1}... | collective-permute-start | bytes 301064 | tf_op jit(solution)/shard_map/ppermute | solution.py:261
  50.7 5.8 %collective-permute-start.10 = (bf16[8,6272]{1,0:T(8,128)(2,1)S(1)}, bf16[8,6272]{1,0:T(8,128)(2,1)S(1)}, u32[]{:S(2)}, u32[]{:S(2)}) collective-permute-start(bf16[8,6272]{1,0:T(8,128)(2,1)S(1)} %collective-permute-done.6.refs_2_), channel_id=1, source_target_pairs={{0,2},{2,4},{4,6},{6,8},{8,10},{10,12},{12,14},{14,0},{1,3},{3,5},... | collective-permute-start | bytes 301064 | tf_op jit(solution)/shard_map/ppermute | solution.py:261
  50.7 12.8 %collective-permute-start.15 = (bf16[32,6272]{1,0:T(8,128)(2,1)S(1)}, bf16[32,6272]{1,0:T(8,128)(2,1)S(1)}, u32[]{:S(2)}, u32[]{:S(2)}) collective-permute-start(bf16[32,6272]{1,0:T(8,128)(2,1)S(1)} %shard_map.90.refs_1_), channel_id=1, source_target_pairs={{0,1},{1,0},{2,3},{3,2},{4,5},{5,4},{6,7},{7,6},{8,9},{9,8},{10,11... | collective-permute-start | bytes 1204232 | tf_op jit(solution)/shard_map/ppermute | solution.py:257
  56.6 8.4 %collective-permute-start.16 = (bf16[32,6272]{1,0:T(8,128)(2,1)S(1)}, bf16[32,6272]{1,0:T(8,128)(2,1)S(1)}, u32[]{:S(2)}, u32[]{:S(2)}) collective-permute-start(bf16[32,6272]{1,0:T(8,128)(2,1)S(1)} %shard_map.91.refs_2_), channel_id=1, source_target_pairs={{0,1},{1,0},{2,3},{3,2},{4,5},{5,4},{6,7},{7,6},{8,9},{9,8},{10,11... | collective-permute-start | bytes 1204232 | tf_op jit(solution)/shard_map/ppermute | solution.py:257
  56.9 6.4 %collective-permute-start.12 = (bf16[8,6272]{1,0:T(8,128)(2,1)S(1)}, bf16[8,6272]{1,0:T(8,128)(2,1)S(1)}, u32[]{:S(2)}, u32[]{:S(2)}) collective-permute-start(bf16[8,6272]{1,0:T(8,128)(2,1)S(1)} %collective-permute-done.8.refs_0_), channel_id=1, source_target_pairs={{0,2},{2,4},{4,6},{6,8},{8,10},{10,12},{12,14},{14,0},{1,3},{3,5},... | collective-permute-start | bytes 301064 | tf_op jit(solution)/shard_map/ppermute | solution.py:261
  57.1 6.3 %collective-permute-start.13 = (bf16[8,6272]{1,0:T(8,128)(2,1)S(1)}, bf16[8,6272]{1,0:T(8,128)(2,1)S(1)}, u32[]{:S(2)}, u32[]{:S(2)}) collective-permute-start(bf16[8,6272]{1,0:T(8,128)(2,1)S(1)} %collective-permute-done.11.refs_3_), channel_id=1, source_target_pairs={{0,14},{2,0},{4,2},{6,4},{8,6},{10,8},{12,10},{14,12},{1,15},{3,1}... | collective-permute-start | bytes 301064 | tf_op jit(solution)/shard_map/ppermute | solution.py:261
  70.0 8.9 %collective-permute-start.20 = (bf16[32,6144]{1,0:T(8,128)(2,1)S(1)}, bf16[32,6144]{1,0:T(8,128)(2,1)S(1)}, u32[]{:S(2)}, u32[]{:S(2)}) collective-permute-start(bf16[32,6144]{1,0:T(8,128)(2,1)S(1)} %get-tuple-element.30), channel_id=1, source_target_pairs={{0,1},{1,0},{2,3},{3,2},{4,5},{5,4},{6,7},{7,6},{8,9},{9,8},{10,11... | collective-permute-start | bytes 1179656 | tf_op jit(solution)/shard_map/ppermute | solution.py:257
  70.2 23.6 %collective-permute-start.18 = (bf16[48,6144]{1,0:T(8,128)(2,1)S(1)}, bf16[48,6144]{1,0:T(8,128)(2,1)S(1)}, u32[]{:S(2)}, u32[]{:S(2)}) collective-permute-start(bf16[48,6144]{1,0:T(8,128)(2,1)S(1)} %get-tuple-element.26), channel_id=1, source_target_pairs={{0,1},{1,0},{2,3},{3,2},{4,5},{5,4},{6,7},{7,6},{8,9},{9,8},{10,11... | collective-permute-start | bytes 1769480 | tf_op jit(solution)/shard_map/ppermute | solution.py:257
  70.6 15.8 %collective-permute-start.19 = (bf16[32,6144]{1,0:T(8,128)(2,1)S(1)}, bf16[32,6144]{1,0:T(8,128)(2,1)S(1)}, u32[]{:S(2)}, u32[]{:S(2)}) collective-permute-start(bf16[32,6144]{1,0:T(8,128)(2,1)S(1)} %get-tuple-element.28), channel_id=1, source_target_pairs={{0,1},{1,0},{2,3},{3,2},{4,5},{5,4},{6,7},{7,6},{8,9},{9,8},{10,11... | collective-permute-start | bytes 1179656 | tf_op jit(solution)/shard_map/ppermute | solution.py:257
  76.6 6.4 %collective-permute-start.32 = (bf16[8,6144]{1,0:T(8,128)(2,1)S(1)}, bf16[8,6144]{1,0:T(8,128)(2,1)S(1)}, u32[]{:S(2)}, u32[]{:S(2)}) collective-permute-start(bf16[8,6144]{1,0:T(8,128)(2,1)S(1)} %shard_map.104), channel_id=1, source_target_pairs={{0,2},{2,4},{4,6},{6,8},{8,10},{10,12},{12,14},{14,0},{1,3},{3,5},... | collective-permute-start | bytes 294920 | tf_op jit(solution)/shard_map/ppermute | solution.py:261
  79.0 7.5 %collective-permute-start.23 = (bf16[8,6144]{1,0:T(8,128)(2,1)S(1)}, bf16[8,6144]{1,0:T(8,128)(2,1)S(1)}, u32[]{:S(2)}, u32[]{:S(2)}) collective-permute-start(bf16[8,6144]{1,0:T(8,128)(2,1)S(1)} %shard_map.95), channel_id=1, source_target_pairs={{0,14},{2,0},{4,2},{6,4},{8,6},{10,8},{12,10},{14,12},{1,15},{3,1}... | collective-permute-start | bytes 294920 | tf_op jit(solution)/shard_map/ppermute | solution.py:261
  82.8 7.0 %collective-permute-start.26 = (bf16[8,6144]{1,0:T(8,128)(2,1)S(1)}, bf16[8,6144]{1,0:T(8,128)(2,1)S(1)}, u32[]{:S(2)}, u32[]{:S(2)}) collective-permute-start(bf16[8,6144]{1,0:T(8,128)(2,1)S(1)} %shard_map.98), channel_id=1, source_target_pairs={{0,2},{2,4},{4,6},{6,8},{8,10},{10,12},{12,14},{14,0},{1,3},{3,5},... | collective-permute-start | bytes 294920 | tf_op jit(solution)/shard_map/ppermute | solution.py:261
  83.0 7.3 %collective-permute-start.29 = (bf16[8,6144]{1,0:T(8,128)(2,1)S(1)}, bf16[8,6144]{1,0:T(8,128)(2,1)S(1)}, u32[]{:S(2)}, u32[]{:S(2)}) collective-permute-start(bf16[8,6144]{1,0:T(8,128)(2,1)S(1)} %shard_map.101), channel_id=1, source_target_pairs={{0,14},{2,0},{4,2},{6,4},{8,6},{10,8},{12,10},{14,12},{1,15},{3,1}... | collective-permute-start | bytes 294920 | tf_op jit(solution)/shard_map/ppermute | solution.py:261
  86.3 7.3 %collective-permute-start.33 = (bf16[8,6144]{1,0:T(8,128)(2,1)S(1)}, bf16[8,6144]{1,0:T(8,128)(2,1)S(1)}, u32[]{:S(2)}, u32[]{:S(2)}) collective-permute-start(bf16[8,6144]{1,0:T(8,128)(2,1)S(1)} %shard_map.105), channel_id=1, source_target_pairs={{0,2},{2,4},{4,6},{6,8},{8,10},{10,12},{12,14},{14,0},{1,3},{3,5},... | collective-permute-start | bytes 294920 | tf_op jit(solution)/shard_map/ppermute | solution.py:261
  86.5 7.3 %collective-permute-start.24 = (bf16[8,6144]{1,0:T(8,128)(2,1)S(1)}, bf16[8,6144]{1,0:T(8,128)(2,1)S(1)}, u32[]{:S(2)}, u32[]{:S(2)}) collective-permute-start(bf16[8,6144]{1,0:T(8,128)(2,1)S(1)} %shard_map.96), channel_id=1, source_target_pairs={{0,14},{2,0},{4,2},{6,4},{8,6},{10,8},{12,10},{14,12},{1,15},{3,1}... | collective-permute-start | bytes 294920 | tf_op jit(solution)/shard_map/ppermute | solution.py:261
  89.9 7.3 %collective-permute-start.27 = (bf16[8,6144]{1,0:T(8,128)(2,1)S(1)}, bf16[8,6144]{1,0:T(8,128)(2,1)S(1)}, u32[]{:S(2)}, u32[]{:S(2)}) collective-permute-start(bf16[8,6144]{1,0:T(8,128)(2,1)S(1)} %shard_map.99), channel_id=1, source_target_pairs={{0,2},{2,4},{4,6},{6,8},{8,10},{10,12},{12,14},{14,0},{1,3},{3,5},... | collective-permute-start | bytes 294920 | tf_op jit(solution)/shard_map/ppermute | solution.py:261
  90.3 7.0 %collective-permute-start.30 = (bf16[8,6144]{1,0:T(8,128)(2,1)S(1)}, bf16[8,6144]{1,0:T(8,128)(2,1)S(1)}, u32[]{:S(2)}, u32[]{:S(2)}) collective-permute-start(bf16[8,6144]{1,0:T(8,128)(2,1)S(1)} %shard_map.102), channel_id=1, source_target_pairs={{0,14},{2,0},{4,2},{6,4},{8,6},{10,8},{12,10},{14,12},{1,15},{3,1}... | collective-permute-start | bytes 294920 | tf_op jit(solution)/shard_map/ppermute | solution.py:261
  93.6 7.1 %collective-permute-start.34 = (bf16[8,6144]{1,0:T(8,128)(2,1)S(1)}, bf16[8,6144]{1,0:T(8,128)(2,1)S(1)}, u32[]{:S(2)}, u32[]{:S(2)}) collective-permute-start(bf16[8,6144]{1,0:T(8,128)(2,1)S(1)} %shard_map.106), channel_id=1, source_target_pairs={{0,2},{2,4},{4,6},{6,8},{8,10},{10,12},{12,14},{14,0},{1,3},{3,5},... | collective-permute-start | bytes 294920 | tf_op jit(solution)/shard_map/ppermute | solution.py:261
  93.8 7.0 %collective-permute-start.25 = (bf16[8,6144]{1,0:T(8,128)(2,1)S(1)}, bf16[8,6144]{1,0:T(8,128)(2,1)S(1)}, u32[]{:S(2)}, u32[]{:S(2)}) collective-permute-start(bf16[8,6144]{1,0:T(8,128)(2,1)S(1)} %shard_map.97), channel_id=1, source_target_pairs={{0,14},{2,0},{4,2},{6,4},{8,6},{10,8},{12,10},{14,12},{1,15},{3,1}... | collective-permute-start | bytes 294920 | tf_op jit(solution)/shard_map/ppermute | solution.py:261
  97.2 5.9 %collective-permute-start.28 = (bf16[8,6144]{1,0:T(8,128)(2,1)S(1)}, bf16[8,6144]{1,0:T(8,128)(2,1)S(1)}, u32[]{:S(2)}, u32[]{:S(2)}) collective-permute-start(bf16[8,6144]{1,0:T(8,128)(2,1)S(1)} %shard_map.100), channel_id=1, source_target_pairs={{0,2},{2,4},{4,6},{6,8},{8,10},{10,12},{12,14},{14,0},{1,3},{3,5},... | collective-permute-start | bytes 294920 | tf_op jit(solution)/shard_map/ppermute | solution.py:261
  97.4 5.8 %collective-permute-start.31 = (bf16[8,6144]{1,0:T(8,128)(2,1)S(1)}, bf16[8,6144]{1,0:T(8,128)(2,1)S(1)}, u32[]{:S(2)}, u32[]{:S(2)}) collective-permute-start(bf16[8,6144]{1,0:T(8,128)(2,1)S(1)} %shard_map.103), channel_id=1, source_target_pairs={{0,14},{2,0},{4,2},{6,4},{8,6},{10,8},{12,10},{14,12},{1,15},{3,1}... | collective-permute-start | bytes 294920 | tf_op jit(solution)/shard_map/ppermute | solution.py:261
  100.7 5.9 %collective-permute-start.35 = (bf16[8,6144]{1,0:T(8,128)(2,1)S(1)}, bf16[8,6144]{1,0:T(8,128)(2,1)S(1)}, u32[]{:S(2)}, u32[]{:S(2)}) collective-permute-start(bf16[8,6144]{1,0:T(8,128)(2,1)S(1)} %shard_map.107), channel_id=1, source_target_pairs={{0,2},{2,4},{4,6},{6,8},{8,10},{10,12},{12,14},{14,0},{1,3},{3,5},... | collective-permute-start | bytes 294920 | tf_op jit(solution)/shard_map/ppermute | solution.py:261
  (9 other events, 86.0 us)

commit v4 on v3

--- a/solution.py
+++ b/solution.py
@@ -283,7 +283,7 @@
             pltpu.SemaphoreType.DMA((4,)),
         ],
     )
-    gate_near, up_near, down_near = fetch([gate_weight, up_weight, down_weight], packed)
+    gate_near = fetch([gate_weight], packed)[0]
     size = columns * CAP // 2
     block_a, block_b = call(
         halves_kernel,
@@ -304,8 +304,15 @@
     rows = [size * len(part) for part in parts]
     near, far = [], []
     for group, part in enumerate(parts):
+        behind = []
+        if group == len(parts) - 1:
+            up_near, down_near = fetch([up_weight, down_weight], near[-1])
+            behind = [up_near]
         near += call(
-            functools.partial(stack_kernel, len(part)), [shape(rows[group], wide, BF16)], part
+            functools.partial(stack_kernel, len(part)),
+            [shape(rows[group], wide, BF16)],
+            part + behind,
+            in_specs=vmem(len(part)) + [pl.BlockSpec(memory_space=pl.ANY)] * len(behind),
         )
         far.append(swap(near[group], "core"))
 

time: 122 us -> 120 us (0.984)
  local copies, waits for them, and re-layouts: 3.34 us -> 0 us
  waiting for transfers between devices: 23 us -> 25.4 us
  blocking collectives: 14.5 us -> 12.3 us
    all_to_all x1, waiting for transfers between devices: 1.07 us -> 6.29 us  [across(): lax.all_to_all(value, ('xo', 'xi'), split_axis=0, concat_axis=0, tiled=True)]
    unnamed x8 -> x0, local copies, waits for them, and re-layouts: 3.34 us -> none
    ppermute x28, waiting for transfers between devices: 18.1 us -> 15.3 us  [along(): lax.ppermute(value, 'y', [(y, (y + step) % RING) for y in range(RING)])]
    all_to_all x1, blocking collectives: 14.5 us -> 12.3 us  [across(): lax.all_to_all(value, ('xo', 'xi'), split_axis=0, concat_axis=0, tiled=True)]
    pallas_call x1 -> x2, Pallas kernels: 3.78 us -> 4.76 us  [fetch(): pl.pallas_call(fetch_kernel, out_shape=[pltpu.VMEM(w.shape, w.dtype) for...]
where the time goes in v4:
time: 120 us
  starting transfers between devices  67.7 us (56%)
  waiting for transfers between devices  25.4 us (21%)
  Pallas kernels  13.6 us (11%)
  blocking collectives  12.3 us (10%)
    ppermute x28, starting transfers between devices, along(): lax.ppermute(value, 'y', [(y, (y + step) % RING) for y in range(RING)])  43.2 us
    all_to_all x1, starting transfers between devices, across(): lax.all_to_all(value, ('xo', 'xi'), split_axis=0, concat_axis=0, tiled=True)  22.7 us
    ppermute x28, waiting for transfers between devices, along(): lax.ppermute(value, 'y', [(y, (y + step) % RING) for y in range(RING)])  15.3 us
    all_to_all x1, blocking collectives, across(): lax.all_to_all(value, ('xo', 'xi'), split_axis=0, concat_axis=0, tiled=True)  12.3 us
    all_to_all x1, waiting for transfers between devices, across(): lax.all_to_all(value, ('xo', 'xi'), split_axis=0, concat_axis=0, tiled=True)  6.29 us
    pallas_call x1, Pallas kernels, local(): pl.pallas_call(functools.partial(expert_kernel, scale, groups), out_shape...  5.08 us
    pallas_call x2, Pallas kernels, fetch(): pl.pallas_call(fetch_kernel, out_shape=[pltpu.VMEM(w.shape, w.dtype) for...  4.76 us
    ppermute x8, waiting for transfers between devices, swap(): return lax.ppermute(value, axis, [(0, 1), (1, 0)])  3.81 us
  transfers between devices with their start and end apart: 37, of which 10 were waited for; matrix products, arithmetic and copies ran while one was open for 0% of the time, Pallas kernels for 4%

profile of v4, /device:TPU:514, one launch (start us, length us, event | category | flops | bytes accessed | tf_op | source)
XLA Modules:
  0.0 120.0 jit_solution(5001041491809996662)
XLA Ops:
  0.6 2.1 %shard_map.86 = (bf16[8,2,6272]{2,1,0:T(2,128)(2,1)}, f32[4,128]{1,0:T(4,128)S(1)}) custom-call(s32[2,4]{1,0:T(2,128)} %bitcast.5, s32[2,4]{1,0:T(2,128)} %bitcast.6, bf16[4,6144]{1,0:T(4,128)(2,1)} %tok_hbm.1, bf16[4,6144]{1,0:T(4,128)(2,1)} %bitcast.4), custom_call_target="tpu_custom_call" | custom-call | flops 200000 | bytes 1000000 | tf_op jit(solution)/shard_map/pallas_call | solution.py:33
  2.7 22.7 %all-to-all-start = ((bf16[8,2,6272]{2,1,0:T(2,128)(2,1)}), bf16[8,2,6272]{2,1,0:T(2,128)(2,1)S(1)}, u32[]{:S(2)}, u32[]{:S(2)}) async-start(bf16[8,2,6272]{2,1,0:T(2,128)(2,1)} %get-tuple-element.18.refs_1_), calls=%async_computation | async-start | bytes 401408 | tf_op jit(solution)/shard_map/all_to_all | solution.py:253
  25.4 1.9 %shard_map.87.unread.refs_8_ = bf16[6144,256]{1,0:T(8,128)(2,1)S(1)} custom-call(bf16[6144,256]{1,0:T(8,128)(2,1)} %refs_0_.2, bf16[8,2,6272]{2,1,0:T(2,128)(2,1)} %get-tuple-element.18.refs_1_), custom_call_target="tpu_custom_call" | custom-call | flops 1000000 | bytes 6291456 | tf_op jit(solution)/shard_map/pallas_call | solution.py:199
  27.3 6.3 %all-to-all-done.rows_ref = bf16[8,2,6272]{2,1,0:T(2,128)(2,1)S(1)} async-done(((bf16[8,2,6272]{2,1,0:T(2,128)(2,1)}), bf16[8,2,6272]{2,1,0:T(2,128)(2,1)S(1)}, u32[]{:S(2)}, u32[]{:S(2)}) %all-to-all-start) | async-done | bytes 200736 | tf_op jit(solution)/shard_map/all_to_all | solution.py:253
  33.9 2.0 %collective-permute-start = (bf16[8,6272]{1,0:T(8,128)(2,1)S(1)}, bf16[8,6272]{1,0:T(8,128)(2,1)S(1)}, u32[]{:S(2)}, u32[]{:S(2)}) collective-permute-start(bf16[8,6272]{1,0:T(8,128)(2,1)S(1)} %get-tuple-element.19.refs_0_), channel_id=1, source_target_pairs={{0,2},{2,4},{4,6},{6,8},{8,10},{10,12},{12,14},{14,0},{1,3},{3,5},... | collective-permute-start | bytes 301064 | tf_op jit(solution)/shard_map/ppermute | solution.py:261
  35.9 1.4 %collective-permute-start.3 = (bf16[8,6272]{1,0:T(8,128)(2,1)S(1)}, bf16[8,6272]{1,0:T(8,128)(2,1)S(1)}, u32[]{:S(2)}, u32[]{:S(2)}) collective-permute-start(bf16[8,6272]{1,0:T(8,128)(2,1)S(1)} %get-tuple-element.20.refs_1_), channel_id=1, source_target_pairs={{0,14},{2,0},{4,2},{6,4},{8,6},{10,8},{12,10},{14,12},{1,15},{3,1}... | collective-permute-start | bytes 301064 | tf_op jit(solution)/shard_map/ppermute | solution.py:261
  37.3 0.7 collective-permute-start.2
  37.9 1.4 %collective-permute-done.1.refs_3_ = bf16[8,6272]{1,0:T(8,128)(2,1)S(1)} collective-permute-done((bf16[8,6272]{1,0:T(8,128)(2,1)S(1)}, bf16[8,6272]{1,0:T(8,128)(2,1)S(1)}, u32[]{:S(2)}, u32[]{:S(2)}) %collective-permute-start.1) | collective-permute-done | bytes 100384 | tf_op jit(solution)/shard_map/ppermute | solution.py:261
  39.3 1.4 %collective-permute-start.5 = (bf16[8,6272]{1,0:T(8,128)(2,1)S(1)}, bf16[8,6272]{1,0:T(8,128)(2,1)S(1)}, u32[]{:S(2)}, u32[]{:S(2)}) collective-permute-start(bf16[8,6272]{1,0:T(8,128)(2,1)S(1)} %collective-permute-done.1.refs_3_), channel_id=1, source_target_pairs={{0,14},{2,0},{4,2},{6,4},{8,6},{10,8},{12,10},{14,12},{1,15},{3,1}... | collective-permute-start | bytes 301064 | tf_op jit(solution)/shard_map/ppermute | solution.py:261
  40.7 0.7 collective-permute-start.4
  41.3 2.6 %collective-permute-start.7 = (bf16[8,6272]{1,0:T(8,128)(2,1)S(1)}, bf16[8,6272]{1,0:T(8,128)(2,1)S(1)}, u32[]{:S(2)}, u32[]{:S(2)}) collective-permute-start(bf16[8,6272]{1,0:T(8,128)(2,1)S(1)} %collective-permute-done.3.refs_5_), channel_id=1, source_target_pairs={{0,14},{2,0},{4,2},{6,4},{8,6},{10,8},{12,10},{14,12},{1,15},{3,1}... | collective-permute-start | bytes 301064 | tf_op jit(solution)/shard_map/ppermute | solution.py:261
  44.1 3.3 %collective-permute-start.9 = (bf16[8,6272]{1,0:T(8,128)(2,1)S(1)}, bf16[8,6272]{1,0:T(8,128)(2,1)S(1)}, u32[]{:S(2)}, u32[]{:S(2)}) collective-permute-start(bf16[8,6272]{1,0:T(8,128)(2,1)S(1)} %collective-permute-done.5.refs_1_), channel_id=1, source_target_pairs={{0,14},{2,0},{4,2},{6,4},{8,6},{10,8},{12,10},{14,12},{1,15},{3,1}... | collective-permute-start | bytes 301064 | tf_op jit(solution)/shard_map/ppermute | solution.py:261
  47.5 3.2 %collective-permute-start.11 = (bf16[8,6272]{1,0:T(8,128)(2,1)S(1)}, bf16[8,6272]{1,0:T(8,128)(2,1)S(1)}, u32[]{:S(2)}, u32[]{:S(2)}) collective-permute-start(bf16[8,6272]{1,0:T(8,128)(2,1)S(1)} %collective-permute-done.7.refs_3_), channel_id=1, source_target_pairs={{0,14},{2,0},{4,2},{6,4},{8,6},{10,8},{12,10},{14,12},{1,15},{3,1}... | collective-permute-start | bytes 301064 | tf_op jit(solution)/shard_map/ppermute | solution.py:261
  50.9 2.6 %collective-permute-done.8.refs_0_ = bf16[8,6272]{1,0:T(8,128)(2,1)S(1)} collective-permute-done((bf16[8,6272]{1,0:T(8,128)(2,1)S(1)}, bf16[8,6272]{1,0:T(8,128)(2,1)S(1)}, u32[]{:S(2)}, u32[]{:S(2)}) %collective-permute-start.8) | collective-permute-done | bytes 100384 | tf_op jit(solution)/shard_map/ppermute | solution.py:261
  53.5 3.1 %collective-permute-done.10.refs_2_ = bf16[8,6272]{1,0:T(8,128)(2,1)S(1)} collective-permute-done((bf16[8,6272]{1,0:T(8,128)(2,1)S(1)}, bf16[8,6272]{1,0:T(8,128)(2,1)S(1)}, u32[]{:S(2)}, u32[]{:S(2)}) %collective-permute-start.10) | collective-permute-done | bytes 100384 | tf_op jit(solution)/shard_map/ppermute | solution.py:261
  57.1 3.2 %collective-permute-start.13 = (bf16[8,6272]{1,0:T(8,128)(2,1)S(1)}, bf16[8,6272]{1,0:T(8,128)(2,1)S(1)}, u32[]{:S(2)}, u32[]{:S(2)}) collective-permute-start(bf16[8,6272]{1,0:T(8,128)(2,1)S(1)} %collective-permute-done.11.refs_3_), channel_id=1, source_target_pairs={{0,14},{2,0},{4,2},{6,4},{8,6},{10,8},{12,10},{14,12},{1,15},{3,1}... | collective-permute-start | bytes 301064 | tf_op jit(solution)/shard_map/ppermute | solution.py:261
  60.3 2.9 %shard_map.92 = (bf16[6144,256]{1,0:T(8,128)(2,1)S(1)}, bf16[256,6144]{1,0:T(8,128)(2,1)S(1)}) custom-call(bf16[6144,256]{1,0:T(8,128)(2,1)} %refs_0_.3, bf16[256,6144]{1,0:T(8,128)(2,1)} %refs_1_.1, bf16[32,6272]{1,0:T(8,128)(2,1)S(1)} %shard_map.91.refs_2_), custom_call_target="tpu_custom_call" | custom-call | flops 1000000 | bytes 12582912 | tf_op jit(solution)/shard_map/pallas_call | solution.py:199
  63.5 1.4 %collective-permute-done.17.refs_7_ = bf16[16,6272]{1,0:T(8,128)(2,1)S(1)} collective-permute-done((bf16[16,6272]{1,0:T(8,128)(2,1)S(1)}, bf16[16,6272]{1,0:T(8,128)(2,1)S(1)}, u32[]{:S(2)}, u32[]{:S(2)}) %collective-permute-start.17) | collective-permute-done | bytes 200736 | tf_op jit(solution)/shard_map/ppermute | solution.py:257
  65.0 5.1 %shard_map.94 = (f32[48,6144]{1,0:T(8,128)S(1)}, f32[32,6144]{1,0:T(8,128)S(1)}, f32[32,6144]{1,0:T(8,128)S(1)}, f32[16,6144]{1,0:T(8,128)S(1)}, bf16[48,6144]{1...) custom-call(bf16[48,6272]{1,0:T(8,128)(2,1)S(1)} %shard_map.89.refs_, ...), custom_call_target="tpu_custom_call" | custom-call | flops 2415919104 | bytes 9000000 | tf_op jit(solution)/shard_map/pallas_call | solution.py:324
  71.1 2.4 %collective-permute-done.21.crossed_ref = bf16[16,6144]{1,0:T(8,128)(2,1)S(1)} collective-permute-done((bf16[16,6144]{1,0:T(8,128)(2,1)S(1)}, bf16[16,6144]{1,0:T(8,128)(2,1)S(1)}, u32[]{:S(2)}, u32[]{:S(2)}) %collective-permute-start.21) | collective-permute-done | bytes 196640 | tf_op jit(solution)/shard_map/ppermute | solution.py:257
  73.5 3.1 %collective-permute-start.22 = (bf16[8,6144]{1,0:T(8,128)(2,1)S(1)}, bf16[8,6144]{1,0:T(8,128)(2,1)S(1)}, u32[]{:S(2)}, u32[]{:S(2)}) collective-permute-start(bf16[8,6144]{1,0:T(8,128)(2,1)S(1)} %shard_map.95), channel_id=1, source_target_pairs={{0,14},{2,0},{4,2},{6,4},{8,6},{10,8},{12,10},{14,12},{1,15},{3,1}... | collective-permute-start | bytes 294920 | tf_op jit(solution)/shard_map/ppermute | solution.py:261
  76.7 2.2 %collective-permute-done.22.refs_0_ = bf16[8,6144]{1,0:T(8,128)(2,1)S(1)} collective-permute-done((bf16[8,6144]{1,0:T(8,128)(2,1)S(1)}, bf16[8,6144]{1,0:T(8,128)(2,1)S(1)}, u32[]{:S(2)}, u32[]{:S(2)}) %collective-permute-start.22) | collective-permute-done | bytes 98336 | tf_op jit(solution)/shard_map/ppermute | solution.py:261
  79.0 3.8 %collective-permute-start.23 = (bf16[8,6144]{1,0:T(8,128)(2,1)S(1)}, bf16[8,6144]{1,0:T(8,128)(2,1)S(1)}, u32[]{:S(2)}, u32[]{:S(2)}) collective-permute-start(bf16[8,6144]{1,0:T(8,128)(2,1)S(1)} %shard_map.96), channel_id=1, source_target_pairs={{0,14},{2,0},{4,2},{6,4},{8,6},{10,8},{12,10},{14,12},{1,15},{3,1}... | collective-permute-start | bytes 294920 | tf_op jit(solution)/shard_map/ppermute | solution.py:261
  83.0 3.3 %collective-permute-start.29 = (bf16[8,6144]{1,0:T(8,128)(2,1)S(1)}, bf16[8,6144]{1,0:T(8,128)(2,1)S(1)}, u32[]{:S(2)}, u32[]{:S(2)}) collective-permute-start(bf16[8,6144]{1,0:T(8,128)(2,1)S(1)} %shard_map.102), channel_id=1, source_target_pairs={{0,14},{2,0},{4,2},{6,4},{8,6},{10,8},{12,10},{14,12},{1,15},{3,1}... | collective-permute-start | bytes 294920 | tf_op jit(solution)/shard_map/ppermute | solution.py:261
  86.5 3.3 %collective-permute-start.24 = (bf16[8,6144]{1,0:T(8,128)(2,1)S(1)}, bf16[8,6144]{1,0:T(8,128)(2,1)S(1)}, u32[]{:S(2)}, u32[]{:S(2)}) collective-permute-start(bf16[8,6144]{1,0:T(8,128)(2,1)S(1)} %shard_map.97), channel_id=1, source_target_pairs={{0,14},{2,0},{4,2},{6,4},{8,6},{10,8},{12,10},{14,12},{1,15},{3,1}... | collective-permute-start | bytes 294920 | tf_op jit(solution)/shard_map/ppermute | solution.py:261
  90.3 3.3 %collective-permute-start.30 = (bf16[8,6144]{1,0:T(8,128)(2,1)S(1)}, bf16[8,6144]{1,0:T(8,128)(2,1)S(1)}, u32[]{:S(2)}, u32[]{:S(2)}) collective-permute-start(bf16[8,6144]{1,0:T(8,128)(2,1)S(1)} %shard_map.103), channel_id=1, source_target_pairs={{0,14},{2,0},{4,2},{6,4},{8,6},{10,8},{12,10},{14,12},{1,15},{3,1}... | collective-permute-start | bytes 294920 | tf_op jit(solution)/shard_map/ppermute | solution.py:261
  93.8 3.3 %collective-permute-start.25 = (bf16[8,6144]{1,0:T(8,128)(2,1)S(1)}, bf16[8,6144]{1,0:T(8,128)(2,1)S(1)}, u32[]{:S(2)}, u32[]{:S(2)}) collective-permute-start(bf16[8,6144]{1,0:T(8,128)(2,1)S(1)} %shard_map.98), channel_id=1, source_target_pairs={{0,14},{2,0},{4,2},{6,4},{8,6},{10,8},{12,10},{14,12},{1,15},{3,1}... | collective-permute-start | bytes 294920 | tf_op jit(solution)/shard_map/ppermute | solution.py:261
  97.4 3.3 %collective-permute-start.31 = (bf16[8,6144]{1,0:T(8,128)(2,1)S(1)}, bf16[8,6144]{1,0:T(8,128)(2,1)S(1)}, u32[]{:S(2)}, u32[]{:S(2)}) collective-permute-start(bf16[8,6144]{1,0:T(8,128)(2,1)S(1)} %shard_map.104), channel_id=1, source_target_pairs={{0,14},{2,0},{4,2},{6,4},{8,6},{10,8},{12,10},{14,12},{1,15},{3,1}... | collective-permute-start | bytes 294920 | tf_op jit(solution)/shard_map/ppermute | solution.py:261
  100.9 2.2 %collective-permute-done.28.refs_1_ = bf16[8,6144]{1,0:T(8,128)(2,1)S(1)} collective-permute-done((bf16[8,6144]{1,0:T(8,128)(2,1)S(1)}, bf16[8,6144]{1,0:T(8,128)(2,1)S(1)}, u32[]{:S(2)}, u32[]{:S(2)}) %collective-permute-start.28) | collective-permute-done | bytes 98336 | tf_op jit(solution)/shard_map/ppermute | solution.py:261
  103.1 3.5 %collective-permute-done.35.refs_3_ = bf16[8,6144]{1,0:T(8,128)(2,1)S(1)} collective-permute-done((bf16[8,6144]{1,0:T(8,128)(2,1)S(1)}, bf16[8,6144]{1,0:T(8,128)(2,1)S(1)}, u32[]{:S(2)}, u32[]{:S(2)}) %collective-permute-start.35) | collective-permute-done | bytes 98336 | tf_op jit(solution)/shard_map/ppermute | solution.py:261
  106.8 12.3 %all_to_all.10.rows_ref = bf16[8,2,6144]{2,1,0:T(2,128)(2,1)S(1)} all-to-all(bf16[8,2,6144]{2,1,0:T(2,128)(2,1)S(1)} %shard_map.109), channel_id=1, replica_groups=mesh['groups'=2,'xo'=4,'xi'=2,'y'=8,'core'=2] {'xo','xi'}, dimensions={0} | all-to-all | bytes 393216 | tf_op jit(solution)/shard_map/all_to_all | solution.py:253
  119.0 0.9 shard_map.110
  (68 shorter events, 4.2 us)
Async XLA Ops:
  2.7 30.9 %all-to-all-start = ((bf16[8,2,6272]{2,1,0:T(2,128)(2,1)}), bf16[8,2,6272]{2,1,0:T(2,128)(2,1)S(1)}, u32[]{:S(2)}, u32[]{:S(2)}) async-start(bf16[8,2,6272]{2,1,0:T(2,128)(2,1)} %get-tuple-element.18.refs_1_), calls=%async_computation | async-start | bytes 401408 | tf_op jit(solution)/shard_map/all_to_all | solution.py:253
  33.8 5.5 %collective-permute-start.1 = (bf16[8,6272]{1,0:T(8,128)(2,1)S(1)}, bf16[8,6272]{1,0:T(8,128)(2,1)S(1)}, u32[]{:S(2)}, u32[]{:S(2)}) collective-permute-start(bf16[8,6272]{1,0:T(8,128)(2,1)S(1)} %get-tuple-element.19.refs_0_), channel_id=1, source_target_pairs={{0,14},{2,0},{4,2},{6,4},{8,6},{10,8},{12,10},{14,12},{1,15},{3,1}... | collective-permute-start | bytes 301064 | tf_op jit(solution)/shard_map/ppermute | solution.py:261
  33.9 6.7 %collective-permute-start = (bf16[8,6272]{1,0:T(8,128)(2,1)S(1)}, bf16[8,6272]{1,0:T(8,128)(2,1)S(1)}, u32[]{:S(2)}, u32[]{:S(2)}) collective-permute-start(bf16[8,6272]{1,0:T(8,128)(2,1)S(1)} %get-tuple-element.19.refs_0_), channel_id=1, source_target_pairs={{0,2},{2,4},{4,6},{6,8},{8,10},{10,12},{12,14},{14,0},{1,3},{3,5},... | collective-permute-start | bytes 301064 | tf_op jit(solution)/shard_map/ppermute | solution.py:261
  37.3 6.6 %collective-permute-start.2 = (bf16[8,6272]{1,0:T(8,128)(2,1)S(1)}, bf16[8,6272]{1,0:T(8,128)(2,1)S(1)}, u32[]{:S(2)}, u32[]{:S(2)}) collective-permute-start(bf16[8,6272]{1,0:T(8,128)(2,1)S(1)} %get-tuple-element.20.refs_1_), channel_id=1, source_target_pairs={{0,2},{2,4},{4,6},{6,8},{8,10},{10,12},{12,14},{14,0},{1,3},{3,5},... | collective-permute-start | bytes 301064 | tf_op jit(solution)/shard_map/ppermute | solution.py:261
  40.7 6.8 %collective-permute-start.4 = (bf16[8,6272]{1,0:T(8,128)(2,1)S(1)}, bf16[8,6272]{1,0:T(8,128)(2,1)S(1)}, u32[]{:S(2)}, u32[]{:S(2)}) collective-permute-start(bf16[8,6272]{1,0:T(8,128)(2,1)S(1)} %collective-permute-done.refs_2_), channel_id=1, source_target_pairs={{0,2},{2,4},{4,6},{6,8},{8,10},{10,12},{12,14},{14,0},{1,3},{3,5},... | collective-permute-start | bytes 301064 | tf_op jit(solution)/shard_map/ppermute | solution.py:261
  41.3 6.1 %collective-permute-start.7 = (bf16[8,6272]{1,0:T(8,128)(2,1)S(1)}, bf16[8,6272]{1,0:T(8,128)(2,1)S(1)}, u32[]{:S(2)}, u32[]{:S(2)}) collective-permute-start(bf16[8,6272]{1,0:T(8,128)(2,1)S(1)} %collective-permute-done.3.refs_5_), channel_id=1, source_target_pairs={{0,14},{2,0},{4,2},{6,4},{8,6},{10,8},{12,10},{14,12},{1,15},{3,1}... | collective-permute-start | bytes 301064 | tf_op jit(solution)/shard_map/ppermute | solution.py:261
  43.9 6.8 %collective-permute-start.6 = (bf16[8,6272]{1,0:T(8,128)(2,1)S(1)}, bf16[8,6272]{1,0:T(8,128)(2,1)S(1)}, u32[]{:S(2)}, u32[]{:S(2)}) collective-permute-start(bf16[8,6272]{1,0:T(8,128)(2,1)S(1)} %collective-permute-done.2.refs_4_), channel_id=1, source_target_pairs={{0,2},{2,4},{4,6},{6,8},{8,10},{10,12},{12,14},{14,0},{1,3},{3,5},... | collective-permute-start | bytes 301064 | tf_op jit(solution)/shard_map/ppermute | solution.py:261
  44.0 21.0 %collective-permute-start.14 = (bf16[48,6272]{1,0:T(8,128)(2,1)S(1)}, bf16[48,6272]{1,0:T(8,128)(2,1)S(1)}, u32[]{:S(2)}, u32[]{:S(2)}) collective-permute-start(bf16[48,6272]{1,0:T(8,128)(2,1)S(1)} %shard_map.89.refs_0_), channel_id=1, source_target_pairs={{0,1},{1,0},{2,3},{3,2},{4,5},{5,4},{6,7},{7,6},{8,9},{9,8},{10,11... | collective-permute-start | bytes 1806344 | tf_op jit(solution)/shard_map/ppermute | solution.py:257
  44.1 6.6 %collective-permute-start.9 = (bf16[8,6272]{1,0:T(8,128)(2,1)S(1)}, bf16[8,6272]{1,0:T(8,128)(2,1)S(1)}, u32[]{:S(2)}, u32[]{:S(2)}) collective-permute-start(bf16[8,6272]{1,0:T(8,128)(2,1)S(1)} %collective-permute-done.5.refs_1_), channel_id=1, source_target_pairs={{0,14},{2,0},{4,2},{6,4},{8,6},{10,8},{12,10},{14,12},{1,15},{3,1}... | collective-permute-start | bytes 301064 | tf_op jit(solution)/shard_map/ppermute | solution.py:261
  47.5 6.0 %collective-permute-start.8 = (bf16[8,6272]{1,0:T(8,128)(2,1)S(1)}, bf16[8,6272]{1,0:T(8,128)(2,1)S(1)}, u32[]{:S(2)}, u32[]{:S(2)}) collective-permute-start(bf16[8,6272]{1,0:T(8,128)(2,1)S(1)} %collective-permute-done.4.refs_0_), channel_id=1, source_target_pairs={{0,2},{2,4},{4,6},{6,8},{8,10},{10,12},{12,14},{14,0},{1,3},{3,5},... | collective-permute-start | bytes 301064 | tf_op jit(solution)/shard_map/ppermute | solution.py:261
  47.5 6.0 %collective-permute-start.11 = (bf16[8,6272]{1,0:T(8,128)(2,1)S(1)}, bf16[8,6272]{1,0:T(8,128)(2,1)S(1)}, u32[]{:S(2)}, u32[]{:S(2)}) collective-permute-start(bf16[8,6272]{1,0:T(8,128)(2,1)S(1)} %collective-permute-done.7.refs_3_), channel_id=1, source_target_pairs={{0,14},{2,0},{4,2},{6,4},{8,6},{10,8},{12,10},{14,12},{1,15},{3,1}... | collective-permute-start | bytes 301064 | tf_op jit(solution)/shard_map/ppermute | solution.py:261
  50.7 5.8 %collective-permute-start.10 = (bf16[8,6272]{1,0:T(8,128)(2,1)S(1)}, bf16[8,6272]{1,0:T(8,128)(2,1)S(1)}, u32[]{:S(2)}, u32[]{:S(2)}) collective-permute-start(bf16[8,6272]{1,0:T(8,128)(2,1)S(1)} %collective-permute-done.6.refs_2_), channel_id=1, source_target_pairs={{0,2},{2,4},{4,6},{6,8},{8,10},{10,12},{12,14},{14,0},{1,3},{3,5},... | collective-permute-start | bytes 301064 | tf_op jit(solution)/shard_map/ppermute | solution.py:261
  50.8 12.8 %collective-permute-start.15 = (bf16[32,6272]{1,0:T(8,128)(2,1)S(1)}, bf16[32,6272]{1,0:T(8,128)(2,1)S(1)}, u32[]{:S(2)}, u32[]{:S(2)}) collective-permute-start(bf16[32,6272]{1,0:T(8,128)(2,1)S(1)} %shard_map.90.refs_1_), channel_id=1, source_target_pairs={{0,1},{1,0},{2,3},{3,2},{4,5},{5,4},{6,7},{7,6},{8,9},{9,8},{10,11... | collective-permute-start | bytes 1204232 | tf_op jit(solution)/shard_map/ppermute | solution.py:257
  56.6 8.4 %collective-permute-start.16 = (bf16[32,6272]{1,0:T(8,128)(2,1)S(1)}, bf16[32,6272]{1,0:T(8,128)(2,1)S(1)}, u32[]{:S(2)}, u32[]{:S(2)}) collective-permute-start(bf16[32,6272]{1,0:T(8,128)(2,1)S(1)} %shard_map.91.refs_2_), channel_id=1, source_target_pairs={{0,1},{1,0},{2,3},{3,2},{4,5},{5,4},{6,7},{7,6},{8,9},{9,8},{10,11... | collective-permute-start | bytes 1204232 | tf_op jit(solution)/shard_map/ppermute | solution.py:257
  56.9 6.4 %collective-permute-start.12 = (bf16[8,6272]{1,0:T(8,128)(2,1)S(1)}, bf16[8,6272]{1,0:T(8,128)(2,1)S(1)}, u32[]{:S(2)}, u32[]{:S(2)}) collective-permute-start(bf16[8,6272]{1,0:T(8,128)(2,1)S(1)} %collective-permute-done.8.refs_0_), channel_id=1, source_target_pairs={{0,2},{2,4},{4,6},{6,8},{8,10},{10,12},{12,14},{14,0},{1,3},{3,5},... | collective-permute-start | bytes 301064 | tf_op jit(solution)/shard_map/ppermute | solution.py:261
  57.1 6.3 %collective-permute-start.13 = (bf16[8,6272]{1,0:T(8,128)(2,1)S(1)}, bf16[8,6272]{1,0:T(8,128)(2,1)S(1)}, u32[]{:S(2)}, u32[]{:S(2)}) collective-permute-start(bf16[8,6272]{1,0:T(8,128)(2,1)S(1)} %collective-permute-done.11.refs_3_), channel_id=1, source_target_pairs={{0,14},{2,0},{4,2},{6,4},{8,6},{10,8},{12,10},{14,12},{1,15},{3,1}... | collective-permute-start | bytes 301064 | tf_op jit(solution)/shard_map/ppermute | solution.py:261
  70.0 8.9 %collective-permute-start.20 = (bf16[32,6144]{1,0:T(8,128)(2,1)S(1)}, bf16[32,6144]{1,0:T(8,128)(2,1)S(1)}, u32[]{:S(2)}, u32[]{:S(2)}) collective-permute-start(bf16[32,6144]{1,0:T(8,128)(2,1)S(1)} %get-tuple-element.28), channel_id=1, source_target_pairs={{0,1},{1,0},{2,3},{3,2},{4,5},{5,4},{6,7},{7,6},{8,9},{9,8},{10,11... | collective-permute-start | bytes 1179656 | tf_op jit(solution)/shard_map/ppermute | solution.py:257
  70.2 23.6 %collective-permute-start.18 = (bf16[48,6144]{1,0:T(8,128)(2,1)S(1)}, bf16[48,6144]{1,0:T(8,128)(2,1)S(1)}, u32[]{:S(2)}, u32[]{:S(2)}) collective-permute-start(bf16[48,6144]{1,0:T(8,128)(2,1)S(1)} %get-tuple-element.24), channel_id=1, source_target_pairs={{0,1},{1,0},{2,3},{3,2},{4,5},{5,4},{6,7},{7,6},{8,9},{9,8},{10,11... | collective-permute-start | bytes 1769480 | tf_op jit(solution)/shard_map/ppermute | solution.py:257
  70.5 15.8 %collective-permute-start.19 = (bf16[32,6144]{1,0:T(8,128)(2,1)S(1)}, bf16[32,6144]{1,0:T(8,128)(2,1)S(1)}, u32[]{:S(2)}, u32[]{:S(2)}) collective-permute-start(bf16[32,6144]{1,0:T(8,128)(2,1)S(1)} %get-tuple-element.26), channel_id=1, source_target_pairs={{0,1},{1,0},{2,3},{3,2},{4,5},{5,4},{6,7},{7,6},{8,9},{9,8},{10,11... | collective-permute-start | bytes 1179656 | tf_op jit(solution)/shard_map/ppermute | solution.py:257
  76.5 6.4 %collective-permute-start.32 = (bf16[8,6144]{1,0:T(8,128)(2,1)S(1)}, bf16[8,6144]{1,0:T(8,128)(2,1)S(1)}, u32[]{:S(2)}, u32[]{:S(2)}) collective-permute-start(bf16[8,6144]{1,0:T(8,128)(2,1)S(1)} %shard_map.105), channel_id=1, source_target_pairs={{0,2},{2,4},{4,6},{6,8},{8,10},{10,12},{12,14},{14,0},{1,3},{3,5},... | collective-permute-start | bytes 294920 | tf_op jit(solution)/shard_map/ppermute | solution.py:261
  79.0 7.5 %collective-permute-start.23 = (bf16[8,6144]{1,0:T(8,128)(2,1)S(1)}, bf16[8,6144]{1,0:T(8,128)(2,1)S(1)}, u32[]{:S(2)}, u32[]{:S(2)}) collective-permute-start(bf16[8,6144]{1,0:T(8,128)(2,1)S(1)} %shard_map.96), channel_id=1, source_target_pairs={{0,14},{2,0},{4,2},{6,4},{8,6},{10,8},{12,10},{14,12},{1,15},{3,1}... | collective-permute-start | bytes 294920 | tf_op jit(solution)/shard_map/ppermute | solution.py:261
  82.8 7.0 %collective-permute-start.26 = (bf16[8,6144]{1,0:T(8,128)(2,1)S(1)}, bf16[8,6144]{1,0:T(8,128)(2,1)S(1)}, u32[]{:S(2)}, u32[]{:S(2)}) collective-permute-start(bf16[8,6144]{1,0:T(8,128)(2,1)S(1)} %shard_map.99), channel_id=1, source_target_pairs={{0,2},{2,4},{4,6},{6,8},{8,10},{10,12},{12,14},{14,0},{1,3},{3,5},... | collective-permute-start | bytes 294920 | tf_op jit(solution)/shard_map/ppermute | solution.py:261
  83.0 7.3 %collective-permute-start.29 = (bf16[8,6144]{1,0:T(8,128)(2,1)S(1)}, bf16[8,6144]{1,0:T(8,128)(2,1)S(1)}, u32[]{:S(2)}, u32[]{:S(2)}) collective-permute-start(bf16[8,6144]{1,0:T(8,128)(2,1)S(1)} %shard_map.102), channel_id=1, source_target_pairs={{0,14},{2,0},{4,2},{6,4},{8,6},{10,8},{12,10},{14,12},{1,15},{3,1}... | collective-permute-start | bytes 294920 | tf_op jit(solution)/shard_map/ppermute | solution.py:261
  86.3 7.3 %collective-permute-start.33 = (bf16[8,6144]{1,0:T(8,128)(2,1)S(1)}, bf16[8,6144]{1,0:T(8,128)(2,1)S(1)}, u32[]{:S(2)}, u32[]{:S(2)}) collective-permute-start(bf16[8,6144]{1,0:T(8,128)(2,1)S(1)} %shard_map.106), channel_id=1, source_target_pairs={{0,2},{2,4},{4,6},{6,8},{8,10},{10,12},{12,14},{14,0},{1,3},{3,5},... | collective-permute-start | bytes 294920 | tf_op jit(solution)/shard_map/ppermute | solution.py:261
  86.5 7.3 %collective-permute-start.24 = (bf16[8,6144]{1,0:T(8,128)(2,1)S(1)}, bf16[8,6144]{1,0:T(8,128)(2,1)S(1)}, u32[]{:S(2)}, u32[]{:S(2)}) collective-permute-start(bf16[8,6144]{1,0:T(8,128)(2,1)S(1)} %shard_map.97), channel_id=1, source_target_pairs={{0,14},{2,0},{4,2},{6,4},{8,6},{10,8},{12,10},{14,12},{1,15},{3,1}... | collective-permute-start | bytes 294920 | tf_op jit(solution)/shard_map/ppermute | solution.py:261
  89.9 7.3 %collective-permute-start.27 = (bf16[8,6144]{1,0:T(8,128)(2,1)S(1)}, bf16[8,6144]{1,0:T(8,128)(2,1)S(1)}, u32[]{:S(2)}, u32[]{:S(2)}) collective-permute-start(bf16[8,6144]{1,0:T(8,128)(2,1)S(1)} %shard_map.100), channel_id=1, source_target_pairs={{0,2},{2,4},{4,6},{6,8},{8,10},{10,12},{12,14},{14,0},{1,3},{3,5},... | collective-permute-start | bytes 294920 | tf_op jit(solution)/shard_map/ppermute | solution.py:261
  90.3 7.0 %collective-permute-start.30 = (bf16[8,6144]{1,0:T(8,128)(2,1)S(1)}, bf16[8,6144]{1,0:T(8,128)(2,1)S(1)}, u32[]{:S(2)}, u32[]{:S(2)}) collective-permute-start(bf16[8,6144]{1,0:T(8,128)(2,1)S(1)} %shard_map.103), channel_id=1, source_target_pairs={{0,14},{2,0},{4,2},{6,4},{8,6},{10,8},{12,10},{14,12},{1,15},{3,1}... | collective-permute-start | bytes 294920 | tf_op jit(solution)/shard_map/ppermute | solution.py:261
  93.6 7.1 %collective-permute-start.34 = (bf16[8,6144]{1,0:T(8,128)(2,1)S(1)}, bf16[8,6144]{1,0:T(8,128)(2,1)S(1)}, u32[]{:S(2)}, u32[]{:S(2)}) collective-permute-start(bf16[8,6144]{1,0:T(8,128)(2,1)S(1)} %shard_map.107), channel_id=1, source_target_pairs={{0,2},{2,4},{4,6},{6,8},{8,10},{10,12},{12,14},{14,0},{1,3},{3,5},... | collective-permute-start | bytes 294920 | tf_op jit(solution)/shard_map/ppermute | solution.py:261
  93.8 7.0 %collective-permute-start.25 = (bf16[8,6144]{1,0:T(8,128)(2,1)S(1)}, bf16[8,6144]{1,0:T(8,128)(2,1)S(1)}, u32[]{:S(2)}, u32[]{:S(2)}) collective-permute-start(bf16[8,6144]{1,0:T(8,128)(2,1)S(1)} %shard_map.98), channel_id=1, source_target_pairs={{0,14},{2,0},{4,2},{6,4},{8,6},{10,8},{12,10},{14,12},{1,15},{3,1}... | collective-permute-start | bytes 294920 | tf_op jit(solution)/shard_map/ppermute | solution.py:261
  97.2 5.9 %collective-permute-start.28 = (bf16[8,6144]{1,0:T(8,128)(2,1)S(1)}, bf16[8,6144]{1,0:T(8,128)(2,1)S(1)}, u32[]{:S(2)}, u32[]{:S(2)}) collective-permute-start(bf16[8,6144]{1,0:T(8,128)(2,1)S(1)} %shard_map.101), channel_id=1, source_target_pairs={{0,2},{2,4},{4,6},{6,8},{8,10},{10,12},{12,14},{14,0},{1,3},{3,5},... | collective-permute-start | bytes 294920 | tf_op jit(solution)/shard_map/ppermute | solution.py:261
  97.4 5.8 %collective-permute-start.31 = (bf16[8,6144]{1,0:T(8,128)(2,1)S(1)}, bf16[8,6144]{1,0:T(8,128)(2,1)S(1)}, u32[]{:S(2)}, u32[]{:S(2)}) collective-permute-start(bf16[8,6144]{1,0:T(8,128)(2,1)S(1)} %shard_map.104), channel_id=1, source_target_pairs={{0,14},{2,0},{4,2},{6,4},{8,6},{10,8},{12,10},{14,12},{1,15},{3,1}... | collective-permute-start | bytes 294920 | tf_op jit(solution)/shard_map/ppermute | solution.py:261
  100.7 5.9 %collective-permute-start.35 = (bf16[8,6144]{1,0:T(8,128)(2,1)S(1)}, bf16[8,6144]{1,0:T(8,128)(2,1)S(1)}, u32[]{:S(2)}, u32[]{:S(2)}) collective-permute-start(bf16[8,6144]{1,0:T(8,128)(2,1)S(1)} %shard_map.108), channel_id=1, source_target_pairs={{0,2},{2,4},{4,6},{6,8},{8,10},{10,12},{12,14},{14,0},{1,3},{3,5},... | collective-permute-start | bytes 294920 | tf_op jit(solution)/shard_map/ppermute | solution.py:261
  (5 other events, 20.0 us)

commit v5 on v2

--- a/solution.py
+++ b/solution.py
@@ -131,14 +131,10 @@
             for k in range(2):
                 match = (ids[k] == expert) & (slots[k] == s)
                 column = jnp.where(match, gates[k], column)
-            weights = jnp.where(lane == j * CAP + s, column, weights)
+            weights = jnp.where(lane == expert * CAP + s, column, weights)
         out[:, :width] = jnp.concatenate(rows, axis=0).astype(BF16)
         out[:, width:] = statistic
     cw_ref[...] = weights
-
-
-def in_hbm(value):
-    return pltpu.with_memory_space_constraint(value, pltpu.HBM)
 
 
 def join_kernel(own, r1, r2, r3, unread, out):
@@ -227,19 +223,27 @@
     out[...] = value.astype(out.dtype)
 
 
-def part_kernel(a_ref, came_ref, own, s1, s2, s3):
-    total = a_ref[...] + came_ref[...].astype(F32)
-    for j, out in enumerate((own, s1, s2, s3)):
-        out[...] = total[j * CAP : (j + 1) * CAP].astype(out.dtype)
-
-
-def mix_kernel(cw_ref, own, r1, r2, r3, out):
+def last_kernel(kept_ref, crossed_ref, *refs):
+    out = refs[-1]
+    here, column = lax.axis_index("xo"), lax.axis_index("xi")
+    size = EXPERTS * CAP
+    for b in range(PAIR):
+        at = slice(b * size, (b + 1) * size)
+        total = kept_ref[at, :] + crossed_ref[at, :].astype(F32)
+        total = total + refs[2 * b][...].astype(F32) + refs[2 * b + 1][...].astype(F32)
+        owner = column if b == 0 else 1 - column
+        for j in range(EXPERTS):
+            entry = lax.rem(here + EXPERTS - j, EXPERTS) * PAIR + owner
+            out[entry] = total[j * CAP : (j + 1) * CAP].astype(out.dtype)
+
+
+def mix_kernel(cw_ref, rows_ref, out):
     weights = cw_ref[...]
     total = None
-    for j, ref in enumerate((own, r1, r2, r3)):
-        value = ref[...].astype(F32)
+    for expert in range(EXPERTS):
+        value = rows_ref[expert * PAIR].astype(F32) + rows_ref[expert * PAIR + 1].astype(F32)
         for s in range(CAP):
-            at = j * CAP + s
+            at = expert * CAP + s
             term = weights[:, at : at + 1] * value[s : s + 1, :]
             total = term if total is None else total + term
     out[...] = total.astype(out.dtype)
@@ -251,6 +255,10 @@
 
 def to_expert(value, step):
     return lax.ppermute(value, "xo", [(i, (i + step) % EXPERTS) for i in range(EXPERTS)])
+
+
+def across(value):
+    return lax.all_to_all(value, ("xo", "xi"), split_axis=0, concat_axis=0, tiled=True)
 
 
 def swap(value, axis):
@@ -348,20 +356,12 @@
                     [kept[group], crossed[group]] + came,
                 )[0]
                 moving[b, sign] = along(value, -sign)
-    sums = []
-    for b, dtype in ((1, BF16), (0, F32)):
-        sums += call(
-            functools.partial(add_kernel, b * size),
-            [shape(size, width, dtype)],
-            (kept[0], crossed[0], moving[b, 1], moving[b, -1]),
-        )
-    pieces = call(
-        part_kernel,
-        [shape(CAP, width, F32)] + [shape(CAP, width, BF16)] * 3,
-        (sums[1], swap(sums[0], "xi")),
-    )
-    returned = [pieces[0]] + [to_expert(pieces[k], -k) for k in range(1, EXPERTS)]
-    mixed_rows = call(mix_kernel, [shape(count, width, BF16)], (weights, *returned))[0]
+    sums = call(
+        last_kernel,
+        [jax.ShapeDtypeStruct((EXPERTS * PAIR, CAP, width), BF16)],
+        (kept[0], crossed[0], *[moving[b, sign] for b in (0, 1) for sign in (1, -1)]),
+    )[0]
+    mixed_rows = call(mix_kernel, [shape(count, width, BF16)], (weights, across(sums)))[0]
     return (mixed_rows, balance)
 
 

time: 114 us -> 120 us (1.053)
  blocking collectives: 0 us -> 16.4 us
  starting transfers between devices: 75.7 us -> 69.3 us
  waiting for transfers between devices: 25.7 us -> 21.2 us
    all_to_all x0 -> x1, blocking collectives: none -> 16.4 us  [across(): lax.all_to_all(value, ('xo', 'xi'), split_axis=0, concat_axis=0, tiled=True)]
    ppermute x6 -> x3, starting transfers between devices: 18.1 us -> 9.38 us  [to_expert(): lax.ppermute(value, 'xo', [(i, (i + step) % EXPERTS) for i in range(EXPER...]
    ppermute x6 -> x3, waiting for transfers between devices: 5.3 us -> 0.01 us  [to_expert(): lax.ppermute(value, 'xo', [(i, (i + step) % EXPERTS) for i in range(EXPER...]
    ppermute x28, starting transfers between devices: 39.7 us -> 43.6 us  [along(): lax.ppermute(value, 'y', [(y, (y + step) % RING) for y in range(RING)])]
    ppermute x28, waiting for transfers between devices: 15.1 us -> 16.8 us  [along(): lax.ppermute(value, 'y', [(y, (y + step) % RING) for y in range(RING)])]
    ppermute x10 -> x9, starting transfers between devices: 17.8 us -> 16.3 us  [swap(): return lax.ppermute(value, axis, [(0, 1), (1, 0)])]
    ppermute x10 -> x9, waiting for transfers between devices: 5.24 us -> 4.43 us  [swap(): return lax.ppermute(value, axis, [(0, 1), (1, 0)])]
    pallas_call x24 -> x22, Pallas kernels: 3.05 us -> 3.07 us  [call(): pl.pallas_call(kernel, out_shape=outs, in_specs=in_specs or vmem(len(args...]
  transfers between devices with their start and end apart: 44 -> 40, of which waited for: 15 -> 9; matrix products, arithmetic and copies ran while one was open for 0% -> 0% of each run, Pallas kernels for 4% -> 4%
where the time goes in v5:
time: 120 us
  starting transfers between devices  69.3 us (58%)
  waiting for transfers between devices  21.2 us (18%)
  blocking collectives  16.4 us (14%)
  Pallas kernels  11.9 us (10%)
    ppermute x28, starting transfers between devices, along(): lax.ppermute(value, 'y', [(y, (y + step) % RING) for y in range(RING)])  43.6 us
    ppermute x28, waiting for transfers between devices, along(): lax.ppermute(value, 'y', [(y, (y + step) % RING) for y in range(RING)])  16.8 us
    all_to_all x1, blocking collectives, across(): lax.all_to_all(value, ('xo', 'xi'), split_axis=0, concat_axis=0, tiled=True)  16.4 us
    ppermute x9, starting transfers between devices, swap(): return lax.ppermute(value, axis, [(0, 1), (1, 0)])  16.3 us
    ppermute x3, starting transfers between devices, to_expert(): lax.ppermute(value, 'xo', [(i, (i + step) % EXPERTS) for i in range(EXPER...  9.38 us
    pallas_call x1, Pallas kernels, local(): pl.pallas_call(functools.partial(expert_kernel, scale, groups), out_shape...  5.1 us
    ppermute x9, waiting for transfers between devices, swap(): return lax.ppermute(value, axis, [(0, 1), (1, 0)])  4.43 us
    pallas_call x1, Pallas kernels, fetch(): pl.pallas_call(fetch_kernel, out_shape=[pltpu.VMEM(w.shape, w.dtype) for...  3.78 us
  transfers between devices with their start and end apart: 40, of which 9 were waited for; matrix products, arithmetic and copies ran while one was open for 0% of the time, Pallas kernels for 4%

profile of v5, /device:TPU:514, one launch (start us, length us, event | category | flops | bytes accessed | tf_op | source)
XLA Modules:
  0.0 119.9 jit_solution(13767258032357087793)
XLA Ops:
  0.6 1.4 %shard_map.86 = (bf16[2,6272]{1,0:T(2,128)(2,1)S(1)}, bf16[2,6272]{1,0:T(2,128)(2,1)S(1)}, bf16[2,6272]{1,0:T(2,128)(2,1)S(1)}, bf16[2,6272]{1,0:T(2,128)(2,1)S(1)}, f32[4,128]{1,0:T(4,128)S(1)}) custom-call(s32[2,4]{1,0:T(2,128)} %bitcast.5, s32[2,4]{1,0:T(2,128)} %bitcast.6, bf16[4,6144]{1,0:T(4,128)(2,1)} %tok_hbm.1, bf16[4,6144]{1,0:T(4,128)(2,1)} %bitcast.4), custom_call_target="tpu_custom_call" | custom-call | flops 200000 | bytes 1000000 | tf_op jit(solution)/shard_map/pallas_call | solution.py:33
  2.1 2.8 %collective-permute-start = (bf16[2,6272]{1,0:T(2,128)(2,1)S(1)}, bf16[2,6272]{1,0:T(2,128)(2,1)S(1)}, u32[]{:S(2)}, u32[]{:S(2)}) collective-permute-start(bf16[2,6272]{1,0:T(2,128)(2,1)S(1)} %get-tuple-element.21), channel_id=1, source_target_pairs={{0,32},{32,64},{64,96},{96,0},{1,33},{33,65},{65,97},{97,1},{2,34}... | collective-permute-start | bytes 75272 | tf_op jit(solution)/shard_map/ppermute | solution.py:257
  4.9 3.3 %collective-permute-start.1 = (bf16[2,6272]{1,0:T(2,128)(2,1)S(1)}, bf16[2,6272]{1,0:T(2,128)(2,1)S(1)}, u32[]{:S(2)}, u32[]{:S(2)}) collective-permute-start(bf16[2,6272]{1,0:T(2,128)(2,1)S(1)} %get-tuple-element.22), channel_id=1, source_target_pairs={{0,64},{32,96},{64,0},{96,32},{1,65},{33,97},{65,1},{97,33},{2,66}... | collective-permute-start | bytes 75272 | tf_op jit(solution)/shard_map/ppermute | solution.py:257
  8.2 3.2 %collective-permute-start.2 = (bf16[2,6272]{1,0:T(2,128)(2,1)S(1)}, bf16[2,6272]{1,0:T(2,128)(2,1)S(1)}, u32[]{:S(2)}, u32[]{:S(2)}) collective-permute-start(bf16[2,6272]{1,0:T(2,128)(2,1)S(1)} %get-tuple-element.23), channel_id=1, source_target_pairs={{0,96},{32,0},{64,32},{96,64},{1,97},{33,1},{65,33},{97,65},{2,98}... | collective-permute-start | bytes 75272 | tf_op jit(solution)/shard_map/ppermute | solution.py:257
  11.4 3.8 %shard_map.87 = (bf16[6144,256]{1,0:T(8,128)(2,1)S(1)}, bf16[6144,256]{1,0:T(8,128)(2,1)S(1)}, bf16[256,6144]{1,0:T(8,128)(2,1)S(1)}) custom-call(bf16[6144,256]{1,0:T(8,128)(2,1)} %refs_0_.1, bf16[6144,256]{1,0:T(8,128)(2,1)} %refs_1_.1, bf16[256,6144]{1,0:T(8,128)(2,1)} %refs_2_.1, bf16[2,6272]{1,0:T(2,128)(2,1)S(1)} %get-tuple-element.20.refs_3_.own), custom_call_target="tpu_custom_call" | custom-call | flops 1000000 | bytes 18874368 | tf_op jit(solution)/shard_map/pallas_call | solution.py:201
  15.3 14.7 %collective-permute-start.3 = (bf16[8,6272]{1,0:T(8,128)(2,1)S(1)}, bf16[8,6272]{1,0:T(8,128)(2,1)S(1)}, u32[]{:S(2)}, u32[]{:S(2)}) collective-permute-start(bf16[8,6272]{1,0:T(8,128)(2,1)S(1)} %shard_map.88.refs_0_), channel_id=1, source_target_pairs={{0,16},{16,0},{1,17},{17,1},{2,18},{18,2},{3,19},{19,3},{4,20},{20... | collective-permute-start | bytes 301064 | tf_op jit(solution)/shard_map/ppermute | solution.py:265
  30.1 2.0 %collective-permute-start.4 = (bf16[8,6272]{1,0:T(8,128)(2,1)S(1)}, bf16[8,6272]{1,0:T(8,128)(2,1)S(1)}, u32[]{:S(2)}, u32[]{:S(2)}) collective-permute-start(bf16[8,6272]{1,0:T(8,128)(2,1)S(1)} %shard_map.88.refs_0_), channel_id=1, source_target_pairs={{0,2},{2,4},{4,6},{6,8},{8,10},{10,12},{12,14},{14,0},{1,3},{3,5},... | collective-permute-start | bytes 301064 | tf_op jit(solution)/shard_map/ppermute | solution.py:269
  33.3 1.4 %collective-permute-start.6 = (bf16[8,6272]{1,0:T(8,128)(2,1)S(1)}, bf16[8,6272]{1,0:T(8,128)(2,1)S(1)}, u32[]{:S(2)}, u32[]{:S(2)}) collective-permute-start(bf16[8,6272]{1,0:T(8,128)(2,1)S(1)} %collective-permute-done.3.refs_1_), channel_id=1, source_target_pairs={{0,2},{2,4},{4,6},{6,8},{8,10},{10,12},{12,14},{14,0},{1,3},{3,5},... | collective-permute-start | bytes 301064 | tf_op jit(solution)/shard_map/ppermute | solution.py:269
  34.7 1.8 %collective-permute-start.9 = (bf16[8,6272]{1,0:T(8,128)(2,1)S(1)}, bf16[8,6272]{1,0:T(8,128)(2,1)S(1)}, u32[]{:S(2)}, u32[]{:S(2)}) collective-permute-start(bf16[8,6272]{1,0:T(8,128)(2,1)S(1)} %collective-permute-done.5.refs_3_), channel_id=1, source_target_pairs={{0,14},{2,0},{4,2},{6,4},{8,6},{10,8},{12,10},{14,12},{1,15},{3,1}... | collective-permute-start | bytes 301064 | tf_op jit(solution)/shard_map/ppermute | solution.py:269
  36.6 1.0 collective-permute-start.8
  37.5 2.3 %collective-permute-start.11 = (bf16[8,6272]{1,0:T(8,128)(2,1)S(1)}, bf16[8,6272]{1,0:T(8,128)(2,1)S(1)}, u32[]{:S(2)}, u32[]{:S(2)}) collective-permute-start(bf16[8,6272]{1,0:T(8,128)(2,1)S(1)} %collective-permute-done.7.refs_5_), channel_id=1, source_target_pairs={{0,14},{2,0},{4,2},{6,4},{8,6},{10,8},{12,10},{14,12},{1,15},{3,1}... | collective-permute-start | bytes 301064 | tf_op jit(solution)/shard_map/ppermute | solution.py:269
  40.4 2.9 %collective-permute-start.13 = (bf16[8,6272]{1,0:T(8,128)(2,1)S(1)}, bf16[8,6272]{1,0:T(8,128)(2,1)S(1)}, u32[]{:S(2)}, u32[]{:S(2)}) collective-permute-start(bf16[8,6272]{1,0:T(8,128)(2,1)S(1)} %collective-permute-done.9.refs_1_), channel_id=1, source_target_pairs={{0,14},{2,0},{4,2},{6,4},{8,6},{10,8},{12,10},{14,12},{1,15},{3,1}... | collective-permute-start | bytes 301064 | tf_op jit(solution)/shard_map/ppermute | solution.py:269
  43.4 3.2 %collective-permute-start.15 = (bf16[8,6272]{1,0:T(8,128)(2,1)S(1)}, bf16[8,6272]{1,0:T(8,128)(2,1)S(1)}, u32[]{:S(2)}, u32[]{:S(2)}) collective-permute-start(bf16[8,6272]{1,0:T(8,128)(2,1)S(1)} %collective-permute-done.11.refs_3_), channel_id=1, source_target_pairs={{0,14},{2,0},{4,2},{6,4},{8,6},{10,8},{12,10},{14,12},{1,15},{3,1}... | collective-permute-start | bytes 301064 | tf_op jit(solution)/shard_map/ppermute | solution.py:269
  46.8 2.6 %collective-permute-done.12.refs_0_ = bf16[8,6272]{1,0:T(8,128)(2,1)S(1)} collective-permute-done((bf16[8,6272]{1,0:T(8,128)(2,1)S(1)}, bf16[8,6272]{1,0:T(8,128)(2,1)S(1)}, u32[]{:S(2)}, u32[]{:S(2)}) %collective-permute-start.12) | collective-permute-done | bytes 100384 | tf_op jit(solution)/shard_map/ppermute | solution.py:269
  49.4 3.1 %collective-permute-done.14.refs_2_ = bf16[8,6272]{1,0:T(8,128)(2,1)S(1)} collective-permute-done((bf16[8,6272]{1,0:T(8,128)(2,1)S(1)}, bf16[8,6272]{1,0:T(8,128)(2,1)S(1)}, u32[]{:S(2)}, u32[]{:S(2)}) %collective-permute-start.14) | collective-permute-done | bytes 100384 | tf_op jit(solution)/shard_map/ppermute | solution.py:269
  52.8 3.2 %collective-permute-start.17 = (bf16[8,6272]{1,0:T(8,128)(2,1)S(1)}, bf16[8,6272]{1,0:T(8,128)(2,1)S(1)}, u32[]{:S(2)}, u32[]{:S(2)}) collective-permute-start(bf16[8,6272]{1,0:T(8,128)(2,1)S(1)} %collective-permute-done.15.refs_3_), channel_id=1, source_target_pairs={{0,14},{2,0},{4,2},{6,4},{8,6},{10,8},{12,10},{14,12},{1,15},{3,1}... | collective-permute-start | bytes 301064 | tf_op jit(solution)/shard_map/ppermute | solution.py:269
  56.0 3.1 %collective-permute-done.16.refs_0_ = bf16[8,6272]{1,0:T(8,128)(2,1)S(1)} collective-permute-done((bf16[8,6272]{1,0:T(8,128)(2,1)S(1)}, bf16[8,6272]{1,0:T(8,128)(2,1)S(1)}, u32[]{:S(2)}, u32[]{:S(2)}) %collective-permute-start.16) | collective-permute-done | bytes 100384 | tf_op jit(solution)/shard_map/ppermute | solution.py:269
  59.2 1.4 %collective-permute-done.21.refs_7_ = bf16[16,6272]{1,0:T(8,128)(2,1)S(1)} collective-permute-done((bf16[16,6272]{1,0:T(8,128)(2,1)S(1)}, bf16[16,6272]{1,0:T(8,128)(2,1)S(1)}, u32[]{:S(2)}, u32[]{:S(2)}) %collective-permute-start.21) | collective-permute-done | bytes 200736 | tf_op jit(solution)/shard_map/ppermute | solution.py:265
  60.7 5.1 %shard_map.93 = (f32[48,6144]{1,0:T(8,128)S(1)}, f32[32,6144]{1,0:T(8,128)S(1)}, f32[32,6144]{1,0:T(8,128)S(1)}, f32[16,6144]{1,0:T(8,128)S(1)}, bf16[48,6144]{1...) custom-call(bf16[48,6272]{1,0:T(8,128)(2,1)S(1)} %shard_map.89.refs_, ...), custom_call_target="tpu_custom_call" | custom-call | flops 2415919104 | bytes 9000000 | tf_op jit(solution)/shard_map/pallas_call | solution.py:323
  66.8 2.4 %collective-permute-done.25.crossed_ref = bf16[16,6144]{1,0:T(8,128)(2,1)S(1)} collective-permute-done((bf16[16,6144]{1,0:T(8,128)(2,1)S(1)}, bf16[16,6144]{1,0:T(8,128)(2,1)S(1)}, u32[]{:S(2)}, u32[]{:S(2)}) %collective-permute-start.25) | collective-permute-done | bytes 196640 | tf_op jit(solution)/shard_map/ppermute | solution.py:265
  69.2 3.1 %collective-permute-start.26 = (bf16[8,6144]{1,0:T(8,128)(2,1)S(1)}, bf16[8,6144]{1,0:T(8,128)(2,1)S(1)}, u32[]{:S(2)}, u32[]{:S(2)}) collective-permute-start(bf16[8,6144]{1,0:T(8,128)(2,1)S(1)} %shard_map.94), channel_id=1, source_target_pairs={{0,14},{2,0},{4,2},{6,4},{8,6},{10,8},{12,10},{14,12},{1,15},{3,1}... | collective-permute-start | bytes 294920 | tf_op jit(solution)/shard_map/ppermute | solution.py:269
  72.4 2.2 %collective-permute-done.26.refs_0_ = bf16[8,6144]{1,0:T(8,128)(2,1)S(1)} collective-permute-done((bf16[8,6144]{1,0:T(8,128)(2,1)S(1)}, bf16[8,6144]{1,0:T(8,128)(2,1)S(1)}, u32[]{:S(2)}, u32[]{:S(2)}) %collective-permute-start.26) | collective-permute-done | bytes 98336 | tf_op jit(solution)/shard_map/ppermute | solution.py:269
  74.7 3.8 %collective-permute-start.27 = (bf16[8,6144]{1,0:T(8,128)(2,1)S(1)}, bf16[8,6144]{1,0:T(8,128)(2,1)S(1)}, u32[]{:S(2)}, u32[]{:S(2)}) collective-permute-start(bf16[8,6144]{1,0:T(8,128)(2,1)S(1)} %shard_map.95), channel_id=1, source_target_pairs={{0,14},{2,0},{4,2},{6,4},{8,6},{10,8},{12,10},{14,12},{1,15},{3,1}... | collective-permute-start | bytes 294920 | tf_op jit(solution)/shard_map/ppermute | solution.py:269
  78.7 3.5 %collective-permute-start.33 = (bf16[8,6144]{1,0:T(8,128)(2,1)S(1)}, bf16[8,6144]{1,0:T(8,128)(2,1)S(1)}, u32[]{:S(2)}, u32[]{:S(2)}) collective-permute-start(bf16[8,6144]{1,0:T(8,128)(2,1)S(1)} %shard_map.101), channel_id=1, source_target_pairs={{0,14},{2,0},{4,2},{6,4},{8,6},{10,8},{12,10},{14,12},{1,15},{3,1}... | collective-permute-start | bytes 294920 | tf_op jit(solution)/shard_map/ppermute | solution.py:269
  82.5 3.3 %collective-permute-start.28 = (bf16[8,6144]{1,0:T(8,128)(2,1)S(1)}, bf16[8,6144]{1,0:T(8,128)(2,1)S(1)}, u32[]{:S(2)}, u32[]{:S(2)}) collective-permute-start(bf16[8,6144]{1,0:T(8,128)(2,1)S(1)} %shard_map.96), channel_id=1, source_target_pairs={{0,14},{2,0},{4,2},{6,4},{8,6},{10,8},{12,10},{14,12},{1,15},{3,1}... | collective-permute-start | bytes 294920 | tf_op jit(solution)/shard_map/ppermute | solution.py:269
  86.0 3.3 %collective-permute-start.34 = (bf16[8,6144]{1,0:T(8,128)(2,1)S(1)}, bf16[8,6144]{1,0:T(8,128)(2,1)S(1)}, u32[]{:S(2)}, u32[]{:S(2)}) collective-permute-start(bf16[8,6144]{1,0:T(8,128)(2,1)S(1)} %shard_map.102), channel_id=1, source_target_pairs={{0,14},{2,0},{4,2},{6,4},{8,6},{10,8},{12,10},{14,12},{1,15},{3,1}... | collective-permute-start | bytes 294920 | tf_op jit(solution)/shard_map/ppermute | solution.py:269
  89.5 3.3 %collective-permute-start.29 = (bf16[8,6144]{1,0:T(8,128)(2,1)S(1)}, bf16[8,6144]{1,0:T(8,128)(2,1)S(1)}, u32[]{:S(2)}, u32[]{:S(2)}) collective-permute-start(bf16[8,6144]{1,0:T(8,128)(2,1)S(1)} %shard_map.97), channel_id=1, source_target_pairs={{0,14},{2,0},{4,2},{6,4},{8,6},{10,8},{12,10},{14,12},{1,15},{3,1}... | collective-permute-start | bytes 294920 | tf_op jit(solution)/shard_map/ppermute | solution.py:269
  93.1 3.3 %collective-permute-start.35 = (bf16[8,6144]{1,0:T(8,128)(2,1)S(1)}, bf16[8,6144]{1,0:T(8,128)(2,1)S(1)}, u32[]{:S(2)}, u32[]{:S(2)}) collective-permute-start(bf16[8,6144]{1,0:T(8,128)(2,1)S(1)} %shard_map.103), channel_id=1, source_target_pairs={{0,14},{2,0},{4,2},{6,4},{8,6},{10,8},{12,10},{14,12},{1,15},{3,1}... | collective-permute-start | bytes 294920 | tf_op jit(solution)/shard_map/ppermute | solution.py:269
  96.6 2.2 %collective-permute-done.32.refs_1_ = bf16[8,6144]{1,0:T(8,128)(2,1)S(1)} collective-permute-done((bf16[8,6144]{1,0:T(8,128)(2,1)S(1)}, bf16[8,6144]{1,0:T(8,128)(2,1)S(1)}, u32[]{:S(2)}, u32[]{:S(2)}) %collective-permute-start.32) | collective-permute-done | bytes 98336 | tf_op jit(solution)/shard_map/ppermute | solution.py:269
  98.8 3.5 %collective-permute-done.39.refs_3_ = bf16[8,6144]{1,0:T(8,128)(2,1)S(1)} collective-permute-done((bf16[8,6144]{1,0:T(8,128)(2,1)S(1)}, bf16[8,6144]{1,0:T(8,128)(2,1)S(1)}, u32[]{:S(2)}, u32[]{:S(2)}) %collective-permute-start.39) | collective-permute-done | bytes 98336 | tf_op jit(solution)/shard_map/ppermute | solution.py:269
  102.5 16.4 %all_to_all.5.rows_ref = bf16[8,2,6144]{2,1,0:T(2,128)(2,1)S(1)} all-to-all(bf16[8,2,6144]{2,1,0:T(2,128)(2,1)S(1)} %shard_map.108), channel_id=1, replica_groups=mesh['groups'=2,'xo'=4,'xi'=2,'y'=8,'core'=2] {'xo','xi'}, dimensions={0} | all-to-all | bytes 393216 | tf_op jit(solution)/shard_map/all_to_all | solution.py:261
  118.9 0.9 shard_map.109
  (73 shorter events, 5.1 us)
Async XLA Ops:
  2.1 13.2 %collective-permute-start = (bf16[2,6272]{1,0:T(2,128)(2,1)S(1)}, bf16[2,6272]{1,0:T(2,128)(2,1)S(1)}, u32[]{:S(2)}, u32[]{:S(2)}) collective-permute-start(bf16[2,6272]{1,0:T(2,128)(2,1)S(1)} %get-tuple-element.21), channel_id=1, source_target_pairs={{0,32},{32,64},{64,96},{96,0},{1,33},{33,65},{65,97},{97,1},{2,34}... | collective-permute-start | bytes 75272 | tf_op jit(solution)/shard_map/ppermute | solution.py:257
  4.9 10.4 %collective-permute-start.1 = (bf16[2,6272]{1,0:T(2,128)(2,1)S(1)}, bf16[2,6272]{1,0:T(2,128)(2,1)S(1)}, u32[]{:S(2)}, u32[]{:S(2)}) collective-permute-start(bf16[2,6272]{1,0:T(2,128)(2,1)S(1)} %get-tuple-element.22), channel_id=1, source_target_pairs={{0,64},{32,96},{64,0},{96,32},{1,65},{33,97},{65,1},{97,33},{2,66}... | collective-permute-start | bytes 75272 | tf_op jit(solution)/shard_map/ppermute | solution.py:257
  8.2 7.1 %collective-permute-start.2 = (bf16[2,6272]{1,0:T(2,128)(2,1)S(1)}, bf16[2,6272]{1,0:T(2,128)(2,1)S(1)}, u32[]{:S(2)}, u32[]{:S(2)}) collective-permute-start(bf16[2,6272]{1,0:T(2,128)(2,1)S(1)} %get-tuple-element.23), channel_id=1, source_target_pairs={{0,96},{32,0},{64,32},{96,64},{1,97},{33,1},{65,33},{97,65},{2,98}... | collective-permute-start | bytes 75272 | tf_op jit(solution)/shard_map/ppermute | solution.py:257
  15.3 17.4 %collective-permute-start.3 = (bf16[8,6272]{1,0:T(8,128)(2,1)S(1)}, bf16[8,6272]{1,0:T(8,128)(2,1)S(1)}, u32[]{:S(2)}, u32[]{:S(2)}) collective-permute-start(bf16[8,6272]{1,0:T(8,128)(2,1)S(1)} %shard_map.88.refs_0_), channel_id=1, source_target_pairs={{0,16},{16,0},{1,17},{17,1},{2,18},{18,2},{3,19},{19,3},{4,20},{20... | collective-permute-start | bytes 301064 | tf_op jit(solution)/shard_map/ppermute | solution.py:265
  30.1 6.5 %collective-permute-start.4 = (bf16[8,6272]{1,0:T(8,128)(2,1)S(1)}, bf16[8,6272]{1,0:T(8,128)(2,1)S(1)}, u32[]{:S(2)}, u32[]{:S(2)}) collective-permute-start(bf16[8,6272]{1,0:T(8,128)(2,1)S(1)} %shard_map.88.refs_0_), channel_id=1, source_target_pairs={{0,2},{2,4},{4,6},{6,8},{8,10},{10,12},{12,14},{14,0},{1,3},{3,5},... | collective-permute-start | bytes 301064 | tf_op jit(solution)/shard_map/ppermute | solution.py:269
  33.3 6.5 %collective-permute-start.6 = (bf16[8,6272]{1,0:T(8,128)(2,1)S(1)}, bf16[8,6272]{1,0:T(8,128)(2,1)S(1)}, u32[]{:S(2)}, u32[]{:S(2)}) collective-permute-start(bf16[8,6272]{1,0:T(8,128)(2,1)S(1)} %collective-permute-done.3.refs_1_), channel_id=1, source_target_pairs={{0,2},{2,4},{4,6},{6,8},{8,10},{10,12},{12,14},{14,0},{1,3},{3,5},... | collective-permute-start | bytes 301064 | tf_op jit(solution)/shard_map/ppermute | solution.py:269
  36.6 6.8 %collective-permute-start.8 = (bf16[8,6272]{1,0:T(8,128)(2,1)S(1)}, bf16[8,6272]{1,0:T(8,128)(2,1)S(1)}, u32[]{:S(2)}, u32[]{:S(2)}) collective-permute-start(bf16[8,6272]{1,0:T(8,128)(2,1)S(1)} %collective-permute-done.4.refs_2_), channel_id=1, source_target_pairs={{0,2},{2,4},{4,6},{6,8},{8,10},{10,12},{12,14},{14,0},{1,3},{3,5},... | collective-permute-start | bytes 301064 | tf_op jit(solution)/shard_map/ppermute | solution.py:269
  39.8 6.8 %collective-permute-start.10 = (bf16[8,6272]{1,0:T(8,128)(2,1)S(1)}, bf16[8,6272]{1,0:T(8,128)(2,1)S(1)}, u32[]{:S(2)}, u32[]{:S(2)}) collective-permute-start(bf16[8,6272]{1,0:T(8,128)(2,1)S(1)} %collective-permute-done.6.refs_4_), channel_id=1, source_target_pairs={{0,2},{2,4},{4,6},{6,8},{8,10},{10,12},{12,14},{14,0},{1,3},{3,5},... | collective-permute-start | bytes 301064 | tf_op jit(solution)/shard_map/ppermute | solution.py:269
  40.3 20.4 %collective-permute-start.18 = (bf16[48,6272]{1,0:T(8,128)(2,1)S(1)}, bf16[48,6272]{1,0:T(8,128)(2,1)S(1)}, u32[]{:S(2)}, u32[]{:S(2)}) collective-permute-start(bf16[48,6272]{1,0:T(8,128)(2,1)S(1)} %shard_map.89.refs_0_), channel_id=1, source_target_pairs={{0,1},{1,0},{2,3},{3,2},{4,5},{5,4},{6,7},{7,6},{8,9},{9,8},{10,11... | collective-permute-start | bytes 1806344 | tf_op jit(solution)/shard_map/ppermute | solution.py:265
  40.4 6.2 %collective-permute-start.13 = (bf16[8,6272]{1,0:T(8,128)(2,1)S(1)}, bf16[8,6272]{1,0:T(8,128)(2,1)S(1)}, u32[]{:S(2)}, u32[]{:S(2)}) collective-permute-start(bf16[8,6272]{1,0:T(8,128)(2,1)S(1)} %collective-permute-done.9.refs_1_), channel_id=1, source_target_pairs={{0,14},{2,0},{4,2},{6,4},{8,6},{10,8},{12,10},{14,12},{1,15},{3,1}... | collective-permute-start | bytes 301064 | tf_op jit(solution)/shard_map/ppermute | solution.py:269
  43.4 6.0 %collective-permute-start.12 = (bf16[8,6272]{1,0:T(8,128)(2,1)S(1)}, bf16[8,6272]{1,0:T(8,128)(2,1)S(1)}, u32[]{:S(2)}, u32[]{:S(2)}) collective-permute-start(bf16[8,6272]{1,0:T(8,128)(2,1)S(1)} %collective-permute-done.8.refs_0_), channel_id=1, source_target_pairs={{0,2},{2,4},{4,6},{6,8},{8,10},{10,12},{12,14},{14,0},{1,3},{3,5},... | collective-permute-start | bytes 301064 | tf_op jit(solution)/shard_map/ppermute | solution.py:269
  43.4 6.0 %collective-permute-start.15 = (bf16[8,6272]{1,0:T(8,128)(2,1)S(1)}, bf16[8,6272]{1,0:T(8,128)(2,1)S(1)}, u32[]{:S(2)}, u32[]{:S(2)}) collective-permute-start(bf16[8,6272]{1,0:T(8,128)(2,1)S(1)} %collective-permute-done.11.refs_3_), channel_id=1, source_target_pairs={{0,14},{2,0},{4,2},{6,4},{8,6},{10,8},{12,10},{14,12},{1,15},{3,1}... | collective-permute-start | bytes 301064 | tf_op jit(solution)/shard_map/ppermute | solution.py:269
  46.6 5.8 %collective-permute-start.14 = (bf16[8,6272]{1,0:T(8,128)(2,1)S(1)}, bf16[8,6272]{1,0:T(8,128)(2,1)S(1)}, u32[]{:S(2)}, u32[]{:S(2)}) collective-permute-start(bf16[8,6272]{1,0:T(8,128)(2,1)S(1)} %collective-permute-done.10.refs_2_), channel_id=1, source_target_pairs={{0,2},{2,4},{4,6},{6,8},{8,10},{10,12},{12,14},{14,0},{1,3},{3,5},... | collective-permute-start | bytes 301064 | tf_op jit(solution)/shard_map/ppermute | solution.py:269
  46.6 14.0 %collective-permute-start.19 = (bf16[32,6272]{1,0:T(8,128)(2,1)S(1)}, bf16[32,6272]{1,0:T(8,128)(2,1)S(1)}, u32[]{:S(2)}, u32[]{:S(2)}) collective-permute-start(bf16[32,6272]{1,0:T(8,128)(2,1)S(1)} %shard_map.90.refs_1_), channel_id=1, source_target_pairs={{0,1},{1,0},{2,3},{3,2},{4,5},{5,4},{6,7},{7,6},{8,9},{9,8},{10,11... | collective-permute-start | bytes 1204232 | tf_op jit(solution)/shard_map/ppermute | solution.py:265
  52.5 8.2 %collective-permute-start.20 = (bf16[32,6272]{1,0:T(8,128)(2,1)S(1)}, bf16[32,6272]{1,0:T(8,128)(2,1)S(1)}, u32[]{:S(2)}, u32[]{:S(2)}) collective-permute-start(bf16[32,6272]{1,0:T(8,128)(2,1)S(1)} %shard_map.91.refs_2_), channel_id=1, source_target_pairs={{0,1},{1,0},{2,3},{3,2},{4,5},{5,4},{6,7},{7,6},{8,9},{9,8},{10,11... | collective-permute-start | bytes 1204232 | tf_op jit(solution)/shard_map/ppermute | solution.py:265
  52.6 6.4 %collective-permute-start.16 = (bf16[8,6272]{1,0:T(8,128)(2,1)S(1)}, bf16[8,6272]{1,0:T(8,128)(2,1)S(1)}, u32[]{:S(2)}, u32[]{:S(2)}) collective-permute-start(bf16[8,6272]{1,0:T(8,128)(2,1)S(1)} %collective-permute-done.12.refs_0_), channel_id=1, source_target_pairs={{0,2},{2,4},{4,6},{6,8},{8,10},{10,12},{12,14},{14,0},{1,3},{3,5},... | collective-permute-start | bytes 301064 | tf_op jit(solution)/shard_map/ppermute | solution.py:269
  52.8 6.3 %collective-permute-start.17 = (bf16[8,6272]{1,0:T(8,128)(2,1)S(1)}, bf16[8,6272]{1,0:T(8,128)(2,1)S(1)}, u32[]{:S(2)}, u32[]{:S(2)}) collective-permute-start(bf16[8,6272]{1,0:T(8,128)(2,1)S(1)} %collective-permute-done.15.refs_3_), channel_id=1, source_target_pairs={{0,14},{2,0},{4,2},{6,4},{8,6},{10,8},{12,10},{14,12},{1,15},{3,1}... | collective-permute-start | bytes 301064 | tf_op jit(solution)/shard_map/ppermute | solution.py:269
  65.8 8.9 %collective-permute-start.24 = (bf16[32,6144]{1,0:T(8,128)(2,1)S(1)}, bf16[32,6144]{1,0:T(8,128)(2,1)S(1)}, u32[]{:S(2)}, u32[]{:S(2)}) collective-permute-start(bf16[32,6144]{1,0:T(8,128)(2,1)S(1)} %get-tuple-element.32), channel_id=1, source_target_pairs={{0,1},{1,0},{2,3},{3,2},{4,5},{5,4},{6,7},{7,6},{8,9},{9,8},{10,11... | collective-permute-start | bytes 1179656 | tf_op jit(solution)/shard_map/ppermute | solution.py:265
  65.9 23.6 %collective-permute-start.22 = (bf16[48,6144]{1,0:T(8,128)(2,1)S(1)}, bf16[48,6144]{1,0:T(8,128)(2,1)S(1)}, u32[]{:S(2)}, u32[]{:S(2)}) collective-permute-start(bf16[48,6144]{1,0:T(8,128)(2,1)S(1)} %get-tuple-element.28), channel_id=1, source_target_pairs={{0,1},{1,0},{2,3},{3,2},{4,5},{5,4},{6,7},{7,6},{8,9},{9,8},{10,11... | collective-permute-start | bytes 1769480 | tf_op jit(solution)/shard_map/ppermute | solution.py:265
  66.3 16.0 %collective-permute-start.23 = (bf16[32,6144]{1,0:T(8,128)(2,1)S(1)}, bf16[32,6144]{1,0:T(8,128)(2,1)S(1)}, u32[]{:S(2)}, u32[]{:S(2)}) collective-permute-start(bf16[32,6144]{1,0:T(8,128)(2,1)S(1)} %get-tuple-element.30), channel_id=1, source_target_pairs={{0,1},{1,0},{2,3},{3,2},{4,5},{5,4},{6,7},{7,6},{8,9},{9,8},{10,11... | collective-permute-start | bytes 1179656 | tf_op jit(solution)/shard_map/ppermute | solution.py:265
  72.3 6.4 %collective-permute-start.36 = (bf16[8,6144]{1,0:T(8,128)(2,1)S(1)}, bf16[8,6144]{1,0:T(8,128)(2,1)S(1)}, u32[]{:S(2)}, u32[]{:S(2)}) collective-permute-start(bf16[8,6144]{1,0:T(8,128)(2,1)S(1)} %shard_map.104), channel_id=1, source_target_pairs={{0,2},{2,4},{4,6},{6,8},{8,10},{10,12},{12,14},{14,0},{1,3},{3,5},... | collective-permute-start | bytes 294920 | tf_op jit(solution)/shard_map/ppermute | solution.py:269
  74.7 7.7 %collective-permute-start.27 = (bf16[8,6144]{1,0:T(8,128)(2,1)S(1)}, bf16[8,6144]{1,0:T(8,128)(2,1)S(1)}, u32[]{:S(2)}, u32[]{:S(2)}) collective-permute-start(bf16[8,6144]{1,0:T(8,128)(2,1)S(1)} %shard_map.95), channel_id=1, source_target_pairs={{0,14},{2,0},{4,2},{6,4},{8,6},{10,8},{12,10},{14,12},{1,15},{3,1}... | collective-permute-start | bytes 294920 | tf_op jit(solution)/shard_map/ppermute | solution.py:269
  78.5 7.3 %collective-permute-start.30 = (bf16[8,6144]{1,0:T(8,128)(2,1)S(1)}, bf16[8,6144]{1,0:T(8,128)(2,1)S(1)}, u32[]{:S(2)}, u32[]{:S(2)}) collective-permute-start(bf16[8,6144]{1,0:T(8,128)(2,1)S(1)} %shard_map.98), channel_id=1, source_target_pairs={{0,2},{2,4},{4,6},{6,8},{8,10},{10,12},{12,14},{14,0},{1,3},{3,5},... | collective-permute-start | bytes 294920 | tf_op jit(solution)/shard_map/ppermute | solution.py:269
  78.7 7.3 %collective-permute-start.33 = (bf16[8,6144]{1,0:T(8,128)(2,1)S(1)}, bf16[8,6144]{1,0:T(8,128)(2,1)S(1)}, u32[]{:S(2)}, u32[]{:S(2)}) collective-permute-start(bf16[8,6144]{1,0:T(8,128)(2,1)S(1)} %shard_map.101), channel_id=1, source_target_pairs={{0,14},{2,0},{4,2},{6,4},{8,6},{10,8},{12,10},{14,12},{1,15},{3,1}... | collective-permute-start | bytes 294920 | tf_op jit(solution)/shard_map/ppermute | solution.py:269
  82.3 7.0 %collective-permute-start.37 = (bf16[8,6144]{1,0:T(8,128)(2,1)S(1)}, bf16[8,6144]{1,0:T(8,128)(2,1)S(1)}, u32[]{:S(2)}, u32[]{:S(2)}) collective-permute-start(bf16[8,6144]{1,0:T(8,128)(2,1)S(1)} %shard_map.105), channel_id=1, source_target_pairs={{0,2},{2,4},{4,6},{6,8},{8,10},{10,12},{12,14},{14,0},{1,3},{3,5},... | collective-permute-start | bytes 294920 | tf_op jit(solution)/shard_map/ppermute | solution.py:269
  82.5 7.0 %collective-permute-start.28 = (bf16[8,6144]{1,0:T(8,128)(2,1)S(1)}, bf16[8,6144]{1,0:T(8,128)(2,1)S(1)}, u32[]{:S(2)}, u32[]{:S(2)}) collective-permute-start(bf16[8,6144]{1,0:T(8,128)(2,1)S(1)} %shard_map.96), channel_id=1, source_target_pairs={{0,14},{2,0},{4,2},{6,4},{8,6},{10,8},{12,10},{14,12},{1,15},{3,1}... | collective-permute-start | bytes 294920 | tf_op jit(solution)/shard_map/ppermute | solution.py:269
  85.8 7.1 %collective-permute-start.31 = (bf16[8,6144]{1,0:T(8,128)(2,1)S(1)}, bf16[8,6144]{1,0:T(8,128)(2,1)S(1)}, u32[]{:S(2)}, u32[]{:S(2)}) collective-permute-start(bf16[8,6144]{1,0:T(8,128)(2,1)S(1)} %shard_map.99), channel_id=1, source_target_pairs={{0,2},{2,4},{4,6},{6,8},{8,10},{10,12},{12,14},{14,0},{1,3},{3,5},... | collective-permute-start | bytes 294920 | tf_op jit(solution)/shard_map/ppermute | solution.py:269
  86.0 7.0 %collective-permute-start.34 = (bf16[8,6144]{1,0:T(8,128)(2,1)S(1)}, bf16[8,6144]{1,0:T(8,128)(2,1)S(1)}, u32[]{:S(2)}, u32[]{:S(2)}) collective-permute-start(bf16[8,6144]{1,0:T(8,128)(2,1)S(1)} %shard_map.102), channel_id=1, source_target_pairs={{0,14},{2,0},{4,2},{6,4},{8,6},{10,8},{12,10},{14,12},{1,15},{3,1}... | collective-permute-start | bytes 294920 | tf_op jit(solution)/shard_map/ppermute | solution.py:269
  89.3 7.1 %collective-permute-start.38 = (bf16[8,6144]{1,0:T(8,128)(2,1)S(1)}, bf16[8,6144]{1,0:T(8,128)(2,1)S(1)}, u32[]{:S(2)}, u32[]{:S(2)}) collective-permute-start(bf16[8,6144]{1,0:T(8,128)(2,1)S(1)} %shard_map.106), channel_id=1, source_target_pairs={{0,2},{2,4},{4,6},{6,8},{8,10},{10,12},{12,14},{14,0},{1,3},{3,5},... | collective-permute-start | bytes 294920 | tf_op jit(solution)/shard_map/ppermute | solution.py:269
  89.5 7.0 %collective-permute-start.29 = (bf16[8,6144]{1,0:T(8,128)(2,1)S(1)}, bf16[8,6144]{1,0:T(8,128)(2,1)S(1)}, u32[]{:S(2)}, u32[]{:S(2)}) collective-permute-start(bf16[8,6144]{1,0:T(8,128)(2,1)S(1)} %shard_map.97), channel_id=1, source_target_pairs={{0,14},{2,0},{4,2},{6,4},{8,6},{10,8},{12,10},{14,12},{1,15},{3,1}... | collective-permute-start | bytes 294920 | tf_op jit(solution)/shard_map/ppermute | solution.py:269
  92.9 5.9 %collective-permute-start.32 = (bf16[8,6144]{1,0:T(8,128)(2,1)S(1)}, bf16[8,6144]{1,0:T(8,128)(2,1)S(1)}, u32[]{:S(2)}, u32[]{:S(2)}) collective-permute-start(bf16[8,6144]{1,0:T(8,128)(2,1)S(1)} %shard_map.100), channel_id=1, source_target_pairs={{0,2},{2,4},{4,6},{6,8},{8,10},{10,12},{12,14},{14,0},{1,3},{3,5},... | collective-permute-start | bytes 294920 | tf_op jit(solution)/shard_map/ppermute | solution.py:269
  96.4 5.9 %collective-permute-start.39 = (bf16[8,6144]{1,0:T(8,128)(2,1)S(1)}, bf16[8,6144]{1,0:T(8,128)(2,1)S(1)}, u32[]{:S(2)}, u32[]{:S(2)}) collective-permute-start(bf16[8,6144]{1,0:T(8,128)(2,1)S(1)} %shard_map.107), channel_id=1, source_target_pairs={{0,2},{2,4},{4,6},{6,8},{8,10},{10,12},{12,14},{14,0},{1,3},{3,5},... | collective-permute-start | bytes 294920 | tf_op jit(solution)/shard_map/ppermute | solution.py:269
  (8 other events, 36.5 us)

commit v6 on v2

--- a/solution.py
+++ b/solution.py
@@ -137,10 +137,6 @@
     cw_ref[...] = weights
 
 
-def in_hbm(value):
-    return pltpu.with_memory_space_constraint(value, pltpu.HBM)
-
-
 def join_kernel(own, r1, r2, r3, unread, out):
     out[...] = jnp.concatenate([ref[...].astype(F32) for ref in (own, r1, r2, r3)], axis=0).astype(
         out.dtype
@@ -281,7 +277,7 @@
     )
     arrived = [sends[0]] + [to_expert(sends[k], k) for k in range(1, EXPERTS)]
     size = EXPERTS * CAP
-    gate_near, up_near, down_near = fetch([gate_weight, up_weight, down_weight], sends[0])
+    gate_near = fetch([gate_weight], sends[0])[0]
     block_a = call(
         join_kernel,
         [shape(size, wide, BF16)],
@@ -302,8 +298,15 @@
     rows = [size * len(part) for part in parts]
     near, far = [], []
     for group, part in enumerate(parts):
+        behind = []
+        if group == len(parts) - 1:
+            up_near, down_near = fetch([up_weight, down_weight], near[-1])
+            behind = [up_near]
         near += call(
-            functools.partial(stack_kernel, len(part)), [shape(rows[group], wide, BF16)], part
+            functools.partial(stack_kernel, len(part)),
+            [shape(rows[group], wide, BF16)],
+            part + behind,
+            in_specs=vmem(len(part)) + [pl.BlockSpec(memory_space=pl.ANY)] * len(behind),
         )
         far.append(swap(near[group], "core"))
 

time: 114 us -> 115 us (level)
  waiting for transfers between devices: 25.7 us -> 24.5 us
    ppermute x28, waiting for transfers between devices: 15.1 us -> 13.3 us  [along(): lax.ppermute(value, 'y', [(y, (y + step) % RING) for y in range(RING)])]
    ppermute x10, starting transfers between devices: 17.8 us -> 19.4 us  [swap(): return lax.ppermute(value, axis, [(0, 1), (1, 0)])]
    pallas_call x1 -> x2, Pallas kernels: 3.78 us -> 4.76 us  [fetch(): pl.pallas_call(fetch_kernel, out_shape=[pltpu.VMEM(w.shape, w.dtype) for...]
  transfers between devices with their start and end apart: 44 -> 44, of which waited for: 15 -> 16; matrix products, arithmetic and copies ran while one was open for 0% -> 0% of each run, Pallas kernels for 4% -> 5%
where the time goes in v6:
time: 115 us; the launch traced here: 114 us
  starting transfers between devices  76.1 us (66%)
  waiting for transfers between devices  24.5 us (21%)
  Pallas kernels  12.9 us (11%)
    ppermute x28, starting transfers between devices, along(): lax.ppermute(value, 'y', [(y, (y + step) % RING) for y in range(RING)])  39.2 us
    ppermute x10, starting transfers between devices, swap(): return lax.ppermute(value, axis, [(0, 1), (1, 0)])  19.4 us
    ppermute x6, starting transfers between devices, to_expert(): lax.ppermute(value, 'xo', [(i, (i + step) % EXPERTS) for i in range(EXPER...  17.5 us
    ppermute x28, waiting for transfers between devices, along(): lax.ppermute(value, 'y', [(y, (y + step) % RING) for y in range(RING)])  13.3 us
    ppermute x6, waiting for transfers between devices, to_expert(): lax.ppermute(value, 'xo', [(i, (i + step) % EXPERTS) for i in range(EXPER...  5.94 us
    ppermute x10, waiting for transfers between devices, swap(): return lax.ppermute(value, axis, [(0, 1), (1, 0)])  5.24 us
    pallas_call x1, Pallas kernels, local(): pl.pallas_call(functools.partial(expert_kernel, scale, groups), out_shape...  5.08 us
    pallas_call x2, Pallas kernels, fetch(): pl.pallas_call(fetch_kernel, out_shape=[pltpu.VMEM(w.shape, w.dtype) for...  4.76 us
  transfers between devices with their start and end apart: 44, of which 16 were waited for; matrix products, arithmetic and copies ran while one was open for 0% of the time, Pallas kernels for 5%

profile of v6, /device:TPU:514, one launch (start us, length us, event | category | flops | bytes accessed | tf_op | source)
XLA Modules:
  0.0 114.5 jit_solution(6890732929734966431)
XLA Ops:
  0.6 1.4 %shard_map.86 = (bf16[2,6272]{1,0:T(2,128)(2,1)S(1)}, bf16[2,6272]{1,0:T(2,128)(2,1)S(1)}, bf16[2,6272]{1,0:T(2,128)(2,1)S(1)}, bf16[2,6272]{1,0:T(2,128)(2,1)S(1)}, f32[4,128]{1,0:T(4,128)S(1)}) custom-call(s32[2,4]{1,0:T(2,128)} %bitcast.5, s32[2,4]{1,0:T(2,128)} %bitcast.6, bf16[4,6144]{1,0:T(4,128)(2,1)} %tok_hbm.1, bf16[4,6144]{1,0:T(4,128)(2,1)} %bitcast.4), custom_call_target="tpu_custom_call" | custom-call | flops 200000 | bytes 1000000 | tf_op jit(solution)/shard_map/pallas_call | solution.py:33
  2.1 2.8 %collective-permute-start = (bf16[2,6272]{1,0:T(2,128)(2,1)S(1)}, bf16[2,6272]{1,0:T(2,128)(2,1)S(1)}, u32[]{:S(2)}, u32[]{:S(2)}) collective-permute-start(bf16[2,6272]{1,0:T(2,128)(2,1)S(1)} %get-tuple-element.24), channel_id=1, source_target_pairs={{0,32},{32,64},{64,96},{96,0},{1,33},{33,65},{65,97},{97,1},{2,34}... | collective-permute-start | bytes 75272 | tf_op jit(solution)/shard_map/ppermute | solution.py:249
  4.9 3.3 %collective-permute-start.1 = (bf16[2,6272]{1,0:T(2,128)(2,1)S(1)}, bf16[2,6272]{1,0:T(2,128)(2,1)S(1)}, u32[]{:S(2)}, u32[]{:S(2)}) collective-permute-start(bf16[2,6272]{1,0:T(2,128)(2,1)S(1)} %get-tuple-element.25), channel_id=1, source_target_pairs={{0,64},{32,96},{64,0},{96,32},{1,65},{33,97},{65,1},{97,33},{2,66}... | collective-permute-start | bytes 75272 | tf_op jit(solution)/shard_map/ppermute | solution.py:249
  8.2 3.2 %collective-permute-start.2 = (bf16[2,6272]{1,0:T(2,128)(2,1)S(1)}, bf16[2,6272]{1,0:T(2,128)(2,1)S(1)}, u32[]{:S(2)}, u32[]{:S(2)}) collective-permute-start(bf16[2,6272]{1,0:T(2,128)(2,1)S(1)} %get-tuple-element.26), channel_id=1, source_target_pairs={{0,96},{32,0},{64,32},{96,64},{1,97},{33,1},{65,33},{97,65},{2,98}... | collective-permute-start | bytes 75272 | tf_op jit(solution)/shard_map/ppermute | solution.py:249
  11.4 1.9 %shard_map.87.unread.refs_8_ = bf16[6144,256]{1,0:T(8,128)(2,1)S(1)} custom-call(bf16[6144,256]{1,0:T(8,128)(2,1)} %refs_0_.2, bf16[2,6272]{1,0:T(2,128)(2,1)S(1)} %get-tuple-element.23.refs_1_.own), custom_call_target="tpu_custom_call" | custom-call | flops 1000000 | bytes 6291456 | tf_op jit(solution)/shard_map/pallas_call | solution.py:201
  13.4 16.6 %collective-permute-start.3 = (bf16[8,6272]{1,0:T(8,128)(2,1)S(1)}, bf16[8,6272]{1,0:T(8,128)(2,1)S(1)}, u32[]{:S(2)}, u32[]{:S(2)}) collective-permute-start(bf16[8,6272]{1,0:T(8,128)(2,1)S(1)} %shard_map.88.refs_0_), channel_id=1, source_target_pairs={{0,16},{16,0},{1,17},{17,1},{2,18},{18,2},{3,19},{19,3},{4,20},{20... | collective-permute-start | bytes 301064 | tf_op jit(solution)/shard_map/ppermute | solution.py:253
  30.1 2.0 %collective-permute-start.4 = (bf16[8,6272]{1,0:T(8,128)(2,1)S(1)}, bf16[8,6272]{1,0:T(8,128)(2,1)S(1)}, u32[]{:S(2)}, u32[]{:S(2)}) collective-permute-start(bf16[8,6272]{1,0:T(8,128)(2,1)S(1)} %shard_map.88.refs_0_), channel_id=1, source_target_pairs={{0,2},{2,4},{4,6},{6,8},{8,10},{10,12},{12,14},{14,0},{1,3},{3,5},... | collective-permute-start | bytes 301064 | tf_op jit(solution)/shard_map/ppermute | solution.py:257
  33.3 1.4 %collective-permute-start.6 = (bf16[8,6272]{1,0:T(8,128)(2,1)S(1)}, bf16[8,6272]{1,0:T(8,128)(2,1)S(1)}, u32[]{:S(2)}, u32[]{:S(2)}) collective-permute-start(bf16[8,6272]{1,0:T(8,128)(2,1)S(1)} %collective-permute-done.3.refs_1_), channel_id=1, source_target_pairs={{0,2},{2,4},{4,6},{6,8},{8,10},{10,12},{12,14},{14,0},{1,3},{3,5},... | collective-permute-start | bytes 301064 | tf_op jit(solution)/shard_map/ppermute | solution.py:257
  35.5 1.4 %collective-permute-start.9 = (bf16[8,6272]{1,0:T(8,128)(2,1)S(1)}, bf16[8,6272]{1,0:T(8,128)(2,1)S(1)}, u32[]{:S(2)}, u32[]{:S(2)}) collective-permute-start(bf16[8,6272]{1,0:T(8,128)(2,1)S(1)} %collective-permute-done.5.refs_3_), channel_id=1, source_target_pairs={{0,14},{2,0},{4,2},{6,4},{8,6},{10,8},{12,10},{14,12},{1,15},{3,1}... | collective-permute-start | bytes 301064 | tf_op jit(solution)/shard_map/ppermute | solution.py:257
  37.5 2.6 %collective-permute-start.11 = (bf16[8,6272]{1,0:T(8,128)(2,1)S(1)}, bf16[8,6272]{1,0:T(8,128)(2,1)S(1)}, u32[]{:S(2)}, u32[]{:S(2)}) collective-permute-start(bf16[8,6272]{1,0:T(8,128)(2,1)S(1)} %collective-permute-done.7.refs_5_), channel_id=1, source_target_pairs={{0,14},{2,0},{4,2},{6,4},{8,6},{10,8},{12,10},{14,12},{1,15},{3,1}... | collective-permute-start | bytes 301064 | tf_op jit(solution)/shard_map/ppermute | solution.py:257
  40.3 3.3 %collective-permute-start.13 = (bf16[8,6272]{1,0:T(8,128)(2,1)S(1)}, bf16[8,6272]{1,0:T(8,128)(2,1)S(1)}, u32[]{:S(2)}, u32[]{:S(2)}) collective-permute-start(bf16[8,6272]{1,0:T(8,128)(2,1)S(1)} %collective-permute-done.9.refs_1_), channel_id=1, source_target_pairs={{0,14},{2,0},{4,2},{6,4},{8,6},{10,8},{12,10},{14,12},{1,15},{3,1}... | collective-permute-start | bytes 301064 | tf_op jit(solution)/shard_map/ppermute | solution.py:257
  43.7 3.2 %collective-permute-start.15 = (bf16[8,6272]{1,0:T(8,128)(2,1)S(1)}, bf16[8,6272]{1,0:T(8,128)(2,1)S(1)}, u32[]{:S(2)}, u32[]{:S(2)}) collective-permute-start(bf16[8,6272]{1,0:T(8,128)(2,1)S(1)} %collective-permute-done.11.refs_3_), channel_id=1, source_target_pairs={{0,14},{2,0},{4,2},{6,4},{8,6},{10,8},{12,10},{14,12},{1,15},{3,1}... | collective-permute-start | bytes 301064 | tf_op jit(solution)/shard_map/ppermute | solution.py:257
  47.1 2.6 %collective-permute-done.12.refs_0_ = bf16[8,6272]{1,0:T(8,128)(2,1)S(1)} collective-permute-done((bf16[8,6272]{1,0:T(8,128)(2,1)S(1)}, bf16[8,6272]{1,0:T(8,128)(2,1)S(1)}, u32[]{:S(2)}, u32[]{:S(2)}) %collective-permute-start.12) | collective-permute-done | bytes 100384 | tf_op jit(solution)/shard_map/ppermute | solution.py:257
  49.7 3.1 %collective-permute-done.14.refs_2_ = bf16[8,6272]{1,0:T(8,128)(2,1)S(1)} collective-permute-done((bf16[8,6272]{1,0:T(8,128)(2,1)S(1)}, bf16[8,6272]{1,0:T(8,128)(2,1)S(1)}, u32[]{:S(2)}, u32[]{:S(2)}) %collective-permute-start.14) | collective-permute-done | bytes 100384 | tf_op jit(solution)/shard_map/ppermute | solution.py:257
  53.1 3.2 %collective-permute-start.17 = (bf16[8,6272]{1,0:T(8,128)(2,1)S(1)}, bf16[8,6272]{1,0:T(8,128)(2,1)S(1)}, u32[]{:S(2)}, u32[]{:S(2)}) collective-permute-start(bf16[8,6272]{1,0:T(8,128)(2,1)S(1)} %collective-permute-done.15.refs_3_), channel_id=1, source_target_pairs={{0,14},{2,0},{4,2},{6,4},{8,6},{10,8},{12,10},{14,12},{1,15},{3,1}... | collective-permute-start | bytes 301064 | tf_op jit(solution)/shard_map/ppermute | solution.py:257
  56.3 2.9 %shard_map.92 = (bf16[6144,256]{1,0:T(8,128)(2,1)S(1)}, bf16[256,6144]{1,0:T(8,128)(2,1)S(1)}) custom-call(bf16[6144,256]{1,0:T(8,128)(2,1)} %refs_0_.3, bf16[256,6144]{1,0:T(8,128)(2,1)} %refs_1_.1, bf16[32,6272]{1,0:T(8,128)(2,1)S(1)} %shard_map.91.refs_2_), custom_call_target="tpu_custom_call" | custom-call | flops 1000000 | bytes 12582912 | tf_op jit(solution)/shard_map/pallas_call | solution.py:201
  59.5 1.4 %collective-permute-done.21.refs_7_ = bf16[16,6272]{1,0:T(8,128)(2,1)S(1)} collective-permute-done((bf16[16,6272]{1,0:T(8,128)(2,1)S(1)}, bf16[16,6272]{1,0:T(8,128)(2,1)S(1)}, u32[]{:S(2)}, u32[]{:S(2)}) %collective-permute-start.21) | collective-permute-done | bytes 200736 | tf_op jit(solution)/shard_map/ppermute | solution.py:253
  61.0 5.1 %shard_map.94 = (f32[48,6144]{1,0:T(8,128)S(1)}, f32[32,6144]{1,0:T(8,128)S(1)}, f32[32,6144]{1,0:T(8,128)S(1)}, f32[16,6144]{1,0:T(8,128)S(1)}, bf16[48,6144]{1...) custom-call(bf16[48,6272]{1,0:T(8,128)(2,1)S(1)} %shard_map.89.refs_, ...), custom_call_target="tpu_custom_call" | custom-call | flops 2415919104 | bytes 9000000 | tf_op jit(solution)/shard_map/pallas_call | solution.py:318
  67.1 2.4 %collective-permute-done.25.crossed_ref = bf16[16,6144]{1,0:T(8,128)(2,1)S(1)} collective-permute-done((bf16[16,6144]{1,0:T(8,128)(2,1)S(1)}, bf16[16,6144]{1,0:T(8,128)(2,1)S(1)}, u32[]{:S(2)}, u32[]{:S(2)}) %collective-permute-start.25) | collective-permute-done | bytes 196640 | tf_op jit(solution)/shard_map/ppermute | solution.py:253
  69.6 3.3 %collective-permute-start.26 = (bf16[8,6144]{1,0:T(8,128)(2,1)S(1)}, bf16[8,6144]{1,0:T(8,128)(2,1)S(1)}, u32[]{:S(2)}, u32[]{:S(2)}) collective-permute-start(bf16[8,6144]{1,0:T(8,128)(2,1)S(1)} %shard_map.95), channel_id=1, source_target_pairs={{0,14},{2,0},{4,2},{6,4},{8,6},{10,8},{12,10},{14,12},{1,15},{3,1}... | collective-permute-start | bytes 294920 | tf_op jit(solution)/shard_map/ppermute | solution.py:257
  73.0 1.8 %collective-permute-start.33 = (bf16[8,6144]{1,0:T(8,128)(2,1)S(1)}, bf16[8,6144]{1,0:T(8,128)(2,1)S(1)}, u32[]{:S(2)}, u32[]{:S(2)}) collective-permute-start(bf16[8,6144]{1,0:T(8,128)(2,1)S(1)} %shard_map.103), channel_id=1, source_target_pairs={{0,14},{2,0},{4,2},{6,4},{8,6},{10,8},{12,10},{14,12},{1,15},{3,1}... | collective-permute-start | bytes 294920 | tf_op jit(solution)/shard_map/ppermute | solution.py:257
  76.3 3.3 %collective-permute-start.27 = (bf16[8,6144]{1,0:T(8,128)(2,1)S(1)}, bf16[8,6144]{1,0:T(8,128)(2,1)S(1)}, u32[]{:S(2)}, u32[]{:S(2)}) collective-permute-start(bf16[8,6144]{1,0:T(8,128)(2,1)S(1)} %shard_map.96), channel_id=1, source_target_pairs={{0,14},{2,0},{4,2},{6,4},{8,6},{10,8},{12,10},{14,12},{1,15},{3,1}... | collective-permute-start | bytes 294920 | tf_op jit(solution)/shard_map/ppermute | solution.py:257
  79.7 2.1 %collective-permute-start.34 = (bf16[8,6144]{1,0:T(8,128)(2,1)S(1)}, bf16[8,6144]{1,0:T(8,128)(2,1)S(1)}, u32[]{:S(2)}, u32[]{:S(2)}) collective-permute-start(bf16[8,6144]{1,0:T(8,128)(2,1)S(1)} %shard_map.104), channel_id=1, source_target_pairs={{0,14},{2,0},{4,2},{6,4},{8,6},{10,8},{12,10},{14,12},{1,15},{3,1}... | collective-permute-start | bytes 294920 | tf_op jit(solution)/shard_map/ppermute | solution.py:257
  83.4 3.3 %collective-permute-start.28 = (bf16[8,6144]{1,0:T(8,128)(2,1)S(1)}, bf16[8,6144]{1,0:T(8,128)(2,1)S(1)}, u32[]{:S(2)}, u32[]{:S(2)}) collective-permute-start(bf16[8,6144]{1,0:T(8,128)(2,1)S(1)} %shard_map.97), channel_id=1, source_target_pairs={{0,14},{2,0},{4,2},{6,4},{8,6},{10,8},{12,10},{14,12},{1,15},{3,1}... | collective-permute-start | bytes 294920 | tf_op jit(solution)/shard_map/ppermute | solution.py:257
  86.7 1.2 %collective-permute-start.35 = (bf16[8,6144]{1,0:T(8,128)(2,1)S(1)}, bf16[8,6144]{1,0:T(8,128)(2,1)S(1)}, u32[]{:S(2)}, u32[]{:S(2)}) collective-permute-start(bf16[8,6144]{1,0:T(8,128)(2,1)S(1)} %shard_map.105), channel_id=1, source_target_pairs={{0,14},{2,0},{4,2},{6,4},{8,6},{10,8},{12,10},{14,12},{1,15},{3,1}... | collective-permute-start | bytes 294920 | tf_op jit(solution)/shard_map/ppermute | solution.py:257
  89.1 3.6 %collective-permute-start.29 = (bf16[8,6144]{1,0:T(8,128)(2,1)S(1)}, bf16[8,6144]{1,0:T(8,128)(2,1)S(1)}, u32[]{:S(2)}, u32[]{:S(2)}) collective-permute-start(bf16[8,6144]{1,0:T(8,128)(2,1)S(1)} %shard_map.98), channel_id=1, source_target_pairs={{0,14},{2,0},{4,2},{6,4},{8,6},{10,8},{12,10},{14,12},{1,15},{3,1}... | collective-permute-start | bytes 294920 | tf_op jit(solution)/shard_map/ppermute | solution.py:257
  92.9 1.9 %collective-permute-done.39.refs_1_ = bf16[8,6144]{1,0:T(8,128)(2,1)S(1)} collective-permute-done((bf16[8,6144]{1,0:T(8,128)(2,1)S(1)}, bf16[8,6144]{1,0:T(8,128)(2,1)S(1)}, u32[]{:S(2)}, u32[]{:S(2)}) %collective-permute-start.39) | collective-permute-done | bytes 98336 | tf_op jit(solution)/shard_map/ppermute | solution.py:257
  96.0 2.6 %collective-permute-done.32.refs_1_ = bf16[8,6144]{1,0:T(8,128)(2,1)S(1)} collective-permute-done((bf16[8,6144]{1,0:T(8,128)(2,1)S(1)}, bf16[8,6144]{1,0:T(8,128)(2,1)S(1)}, u32[]{:S(2)}, u32[]{:S(2)}) %collective-permute-start.32) | collective-permute-done | bytes 98336 | tf_op jit(solution)/shard_map/ppermute | solution.py:257
  99.6 3.5 %collective-permute-start.41 = (bf16[2,6144]{1,0:T(2,128)(2,1)S(1)}, bf16[2,6144]{1,0:T(2,128)(2,1)S(1)}, u32[]{:S(2)}, u32[]{:S(2)}) collective-permute-start(bf16[2,6144]{1,0:T(2,128)(2,1)S(1)} %get-tuple-element.38), channel_id=1, source_target_pairs={{0,96},{32,0},{64,32},{96,64},{1,97},{33,1},{65,33},{97,65},{2,98}... | collective-permute-start | bytes 73736 | tf_op jit(solution)/shard_map/ppermute | solution.py:249
  103.0 4.6 %collective-permute-start.42 = (bf16[2,6144]{1,0:T(2,128)(2,1)S(1)}, bf16[2,6144]{1,0:T(2,128)(2,1)S(1)}, u32[]{:S(2)}, u32[]{:S(2)}) collective-permute-start(bf16[2,6144]{1,0:T(2,128)(2,1)S(1)} %get-tuple-element.39), channel_id=1, source_target_pairs={{0,64},{32,96},{64,0},{96,32},{1,65},{33,97},{65,1},{97,33},{2,66}... | collective-permute-start | bytes 73736 | tf_op jit(solution)/shard_map/ppermute | solution.py:249
  107.6 3.1 %collective-permute-done.42.r2 = bf16[2,6144]{1,0:T(2,128)(2,1)S(1)} collective-permute-done((bf16[2,6144]{1,0:T(2,128)(2,1)S(1)}, bf16[2,6144]{1,0:T(2,128)(2,1)S(1)}, u32[]{:S(2)}, u32[]{:S(2)}) %collective-permute-start.42) | collective-permute-done | bytes 24608 | tf_op jit(solution)/shard_map/ppermute | solution.py:249
  110.8 2.8 %collective-permute-done.43.r3 = bf16[2,6144]{1,0:T(2,128)(2,1)S(1)} collective-permute-done((bf16[2,6144]{1,0:T(2,128)(2,1)S(1)}, bf16[2,6144]{1,0:T(2,128)(2,1)S(1)}, u32[]{:S(2)}, u32[]{:S(2)}) %collective-permute-start.43) | collective-permute-done | bytes 24608 | tf_op jit(solution)/shard_map/ppermute | solution.py:249
  (83 shorter events, 12.4 us)
Async XLA Ops:
  2.1 11.3 %collective-permute-start = (bf16[2,6272]{1,0:T(2,128)(2,1)S(1)}, bf16[2,6272]{1,0:T(2,128)(2,1)S(1)}, u32[]{:S(2)}, u32[]{:S(2)}) collective-permute-start(bf16[2,6272]{1,0:T(2,128)(2,1)S(1)} %get-tuple-element.24), channel_id=1, source_target_pairs={{0,32},{32,64},{64,96},{96,0},{1,33},{33,65},{65,97},{97,1},{2,34}... | collective-permute-start | bytes 75272 | tf_op jit(solution)/shard_map/ppermute | solution.py:249
  4.9 8.5 %collective-permute-start.1 = (bf16[2,6272]{1,0:T(2,128)(2,1)S(1)}, bf16[2,6272]{1,0:T(2,128)(2,1)S(1)}, u32[]{:S(2)}, u32[]{:S(2)}) collective-permute-start(bf16[2,6272]{1,0:T(2,128)(2,1)S(1)} %get-tuple-element.25), channel_id=1, source_target_pairs={{0,64},{32,96},{64,0},{96,32},{1,65},{33,97},{65,1},{97,33},{2,66}... | collective-permute-start | bytes 75272 | tf_op jit(solution)/shard_map/ppermute | solution.py:249
  13.4 19.2 %collective-permute-start.3 = (bf16[8,6272]{1,0:T(8,128)(2,1)S(1)}, bf16[8,6272]{1,0:T(8,128)(2,1)S(1)}, u32[]{:S(2)}, u32[]{:S(2)}) collective-permute-start(bf16[8,6272]{1,0:T(8,128)(2,1)S(1)} %shard_map.88.refs_0_), channel_id=1, source_target_pairs={{0,16},{16,0},{1,17},{17,1},{2,18},{18,2},{3,19},{19,3},{4,20},{20... | collective-permute-start | bytes 301064 | tf_op jit(solution)/shard_map/ppermute | solution.py:253
  30.1 6.8 %collective-permute-start.4 = (bf16[8,6272]{1,0:T(8,128)(2,1)S(1)}, bf16[8,6272]{1,0:T(8,128)(2,1)S(1)}, u32[]{:S(2)}, u32[]{:S(2)}) collective-permute-start(bf16[8,6272]{1,0:T(8,128)(2,1)S(1)} %shard_map.88.refs_0_), channel_id=1, source_target_pairs={{0,2},{2,4},{4,6},{6,8},{8,10},{10,12},{12,14},{14,0},{1,3},{3,5},... | collective-permute-start | bytes 301064 | tf_op jit(solution)/shard_map/ppermute | solution.py:257
  33.3 6.8 %collective-permute-start.6 = (bf16[8,6272]{1,0:T(8,128)(2,1)S(1)}, bf16[8,6272]{1,0:T(8,128)(2,1)S(1)}, u32[]{:S(2)}, u32[]{:S(2)}) collective-permute-start(bf16[8,6272]{1,0:T(8,128)(2,1)S(1)} %collective-permute-done.3.refs_1_), channel_id=1, source_target_pairs={{0,2},{2,4},{4,6},{6,8},{8,10},{10,12},{12,14},{14,0},{1,3},{3,5},... | collective-permute-start | bytes 301064 | tf_op jit(solution)/shard_map/ppermute | solution.py:257
  36.8 6.8 %collective-permute-start.8 = (bf16[8,6272]{1,0:T(8,128)(2,1)S(1)}, bf16[8,6272]{1,0:T(8,128)(2,1)S(1)}, u32[]{:S(2)}, u32[]{:S(2)}) collective-permute-start(bf16[8,6272]{1,0:T(8,128)(2,1)S(1)} %collective-permute-done.4.refs_2_), channel_id=1, source_target_pairs={{0,2},{2,4},{4,6},{6,8},{8,10},{10,12},{12,14},{14,0},{1,3},{3,5},... | collective-permute-start | bytes 301064 | tf_op jit(solution)/shard_map/ppermute | solution.py:257
  37.5 6.1 %collective-permute-start.11 = (bf16[8,6272]{1,0:T(8,128)(2,1)S(1)}, bf16[8,6272]{1,0:T(8,128)(2,1)S(1)}, u32[]{:S(2)}, u32[]{:S(2)}) collective-permute-start(bf16[8,6272]{1,0:T(8,128)(2,1)S(1)} %collective-permute-done.7.refs_5_), channel_id=1, source_target_pairs={{0,14},{2,0},{4,2},{6,4},{8,6},{10,8},{12,10},{14,12},{1,15},{3,1}... | collective-permute-start | bytes 301064 | tf_op jit(solution)/shard_map/ppermute | solution.py:257
  40.1 6.8 %collective-permute-start.10 = (bf16[8,6272]{1,0:T(8,128)(2,1)S(1)}, bf16[8,6272]{1,0:T(8,128)(2,1)S(1)}, u32[]{:S(2)}, u32[]{:S(2)}) collective-permute-start(bf16[8,6272]{1,0:T(8,128)(2,1)S(1)} %collective-permute-done.6.refs_4_), channel_id=1, source_target_pairs={{0,2},{2,4},{4,6},{6,8},{8,10},{10,12},{12,14},{14,0},{1,3},{3,5},... | collective-permute-start | bytes 301064 | tf_op jit(solution)/shard_map/ppermute | solution.py:257
  40.1 20.8 %collective-permute-start.18 = (bf16[48,6272]{1,0:T(8,128)(2,1)S(1)}, bf16[48,6272]{1,0:T(8,128)(2,1)S(1)}, u32[]{:S(2)}, u32[]{:S(2)}) collective-permute-start(bf16[48,6272]{1,0:T(8,128)(2,1)S(1)} %shard_map.89.refs_0_), channel_id=1, source_target_pairs={{0,1},{1,0},{2,3},{3,2},{4,5},{5,4},{6,7},{7,6},{8,9},{9,8},{10,11... | collective-permute-start | bytes 1806344 | tf_op jit(solution)/shard_map/ppermute | solution.py:253
  40.3 6.6 %collective-permute-start.13 = (bf16[8,6272]{1,0:T(8,128)(2,1)S(1)}, bf16[8,6272]{1,0:T(8,128)(2,1)S(1)}, u32[]{:S(2)}, u32[]{:S(2)}) collective-permute-start(bf16[8,6272]{1,0:T(8,128)(2,1)S(1)} %collective-permute-done.9.refs_1_), channel_id=1, source_target_pairs={{0,14},{2,0},{4,2},{6,4},{8,6},{10,8},{12,10},{14,12},{1,15},{3,1}... | collective-permute-start | bytes 301064 | tf_op jit(solution)/shard_map/ppermute | solution.py:257
  43.6 6.0 %collective-permute-start.12 = (bf16[8,6272]{1,0:T(8,128)(2,1)S(1)}, bf16[8,6272]{1,0:T(8,128)(2,1)S(1)}, u32[]{:S(2)}, u32[]{:S(2)}) collective-permute-start(bf16[8,6272]{1,0:T(8,128)(2,1)S(1)} %collective-permute-done.8.refs_0_), channel_id=1, source_target_pairs={{0,2},{2,4},{4,6},{6,8},{8,10},{10,12},{12,14},{14,0},{1,3},{3,5},... | collective-permute-start | bytes 301064 | tf_op jit(solution)/shard_map/ppermute | solution.py:257
  43.7 6.0 %collective-permute-start.15 = (bf16[8,6272]{1,0:T(8,128)(2,1)S(1)}, bf16[8,6272]{1,0:T(8,128)(2,1)S(1)}, u32[]{:S(2)}, u32[]{:S(2)}) collective-permute-start(bf16[8,6272]{1,0:T(8,128)(2,1)S(1)} %collective-permute-done.11.refs_3_), channel_id=1, source_target_pairs={{0,14},{2,0},{4,2},{6,4},{8,6},{10,8},{12,10},{14,12},{1,15},{3,1}... | collective-permute-start | bytes 301064 | tf_op jit(solution)/shard_map/ppermute | solution.py:257
  46.9 12.6 %collective-permute-start.19 = (bf16[32,6272]{1,0:T(8,128)(2,1)S(1)}, bf16[32,6272]{1,0:T(8,128)(2,1)S(1)}, u32[]{:S(2)}, u32[]{:S(2)}) collective-permute-start(bf16[32,6272]{1,0:T(8,128)(2,1)S(1)} %shard_map.90.refs_1_), channel_id=1, source_target_pairs={{0,1},{1,0},{2,3},{3,2},{4,5},{5,4},{6,7},{7,6},{8,9},{9,8},{10,11... | collective-permute-start | bytes 1204232 | tf_op jit(solution)/shard_map/ppermute | solution.py:253
  52.8 8.2 %collective-permute-start.20 = (bf16[32,6272]{1,0:T(8,128)(2,1)S(1)}, bf16[32,6272]{1,0:T(8,128)(2,1)S(1)}, u32[]{:S(2)}, u32[]{:S(2)}) collective-permute-start(bf16[32,6272]{1,0:T(8,128)(2,1)S(1)} %shard_map.91.refs_2_), channel_id=1, source_target_pairs={{0,1},{1,0},{2,3},{3,2},{4,5},{5,4},{6,7},{7,6},{8,9},{9,8},{10,11... | collective-permute-start | bytes 1204232 | tf_op jit(solution)/shard_map/ppermute | solution.py:253
  52.9 6.4 %collective-permute-start.16 = (bf16[8,6272]{1,0:T(8,128)(2,1)S(1)}, bf16[8,6272]{1,0:T(8,128)(2,1)S(1)}, u32[]{:S(2)}, u32[]{:S(2)}) collective-permute-start(bf16[8,6272]{1,0:T(8,128)(2,1)S(1)} %collective-permute-done.12.refs_0_), channel_id=1, source_target_pairs={{0,2},{2,4},{4,6},{6,8},{8,10},{10,12},{12,14},{14,0},{1,3},{3,5},... | collective-permute-start | bytes 301064 | tf_op jit(solution)/shard_map/ppermute | solution.py:257
  53.1 6.3 %collective-permute-start.17 = (bf16[8,6272]{1,0:T(8,128)(2,1)S(1)}, bf16[8,6272]{1,0:T(8,128)(2,1)S(1)}, u32[]{:S(2)}, u32[]{:S(2)}) collective-permute-start(bf16[8,6272]{1,0:T(8,128)(2,1)S(1)} %collective-permute-done.15.refs_3_), channel_id=1, source_target_pairs={{0,14},{2,0},{4,2},{6,4},{8,6},{10,8},{12,10},{14,12},{1,15},{3,1}... | collective-permute-start | bytes 301064 | tf_op jit(solution)/shard_map/ppermute | solution.py:257
  66.0 6.9 %collective-permute-start.24 = (bf16[32,6144]{1,0:T(8,128)(2,1)S(1)}, bf16[32,6144]{1,0:T(8,128)(2,1)S(1)}, u32[]{:S(2)}, u32[]{:S(2)}) collective-permute-start(bf16[32,6144]{1,0:T(8,128)(2,1)S(1)} %get-tuple-element.34), channel_id=1, source_target_pairs={{0,1},{1,0},{2,3},{3,2},{4,5},{5,4},{6,7},{7,6},{8,9},{9,8},{10,11... | collective-permute-start | bytes 1179656 | tf_op jit(solution)/shard_map/ppermute | solution.py:253
  66.2 20.5 %collective-permute-start.22 = (bf16[48,6144]{1,0:T(8,128)(2,1)S(1)}, bf16[48,6144]{1,0:T(8,128)(2,1)S(1)}, u32[]{:S(2)}, u32[]{:S(2)}) collective-permute-start(bf16[48,6144]{1,0:T(8,128)(2,1)S(1)} %get-tuple-element.30), channel_id=1, source_target_pairs={{0,1},{1,0},{2,3},{3,2},{4,5},{5,4},{6,7},{7,6},{8,9},{9,8},{10,11... | collective-permute-start | bytes 1769480 | tf_op jit(solution)/shard_map/ppermute | solution.py:253
  66.5 9.7 %collective-permute-start.23 = (bf16[32,6144]{1,0:T(8,128)(2,1)S(1)}, bf16[32,6144]{1,0:T(8,128)(2,1)S(1)}, u32[]{:S(2)}, u32[]{:S(2)}) collective-permute-start(bf16[32,6144]{1,0:T(8,128)(2,1)S(1)} %get-tuple-element.32), channel_id=1, source_target_pairs={{0,1},{1,0},{2,3},{3,2},{4,5},{5,4},{6,7},{7,6},{8,9},{9,8},{10,11... | collective-permute-start | bytes 1179656 | tf_op jit(solution)/shard_map/ppermute | solution.py:253
  69.5 6.2 %collective-permute-start.36 = (bf16[8,6144]{1,0:T(8,128)(2,1)S(1)}, bf16[8,6144]{1,0:T(8,128)(2,1)S(1)}, u32[]{:S(2)}, u32[]{:S(2)}) collective-permute-start(bf16[8,6144]{1,0:T(8,128)(2,1)S(1)} %shard_map.106), channel_id=1, source_target_pairs={{0,2},{2,4},{4,6},{6,8},{8,10},{10,12},{12,14},{14,0},{1,3},{3,5},... | collective-permute-start | bytes 294920 | tf_op jit(solution)/shard_map/ppermute | solution.py:257
  69.6 6.2 %collective-permute-start.26 = (bf16[8,6144]{1,0:T(8,128)(2,1)S(1)}, bf16[8,6144]{1,0:T(8,128)(2,1)S(1)}, u32[]{:S(2)}, u32[]{:S(2)}) collective-permute-start(bf16[8,6144]{1,0:T(8,128)(2,1)S(1)} %shard_map.95), channel_id=1, source_target_pairs={{0,14},{2,0},{4,2},{6,4},{8,6},{10,8},{12,10},{14,12},{1,15},{3,1}... | collective-permute-start | bytes 294920 | tf_op jit(solution)/shard_map/ppermute | solution.py:257
  73.0 6.6 %collective-permute-start.33 = (bf16[8,6144]{1,0:T(8,128)(2,1)S(1)}, bf16[8,6144]{1,0:T(8,128)(2,1)S(1)}, u32[]{:S(2)}, u32[]{:S(2)}) collective-permute-start(bf16[8,6144]{1,0:T(8,128)(2,1)S(1)} %shard_map.103), channel_id=1, source_target_pairs={{0,14},{2,0},{4,2},{6,4},{8,6},{10,8},{12,10},{14,12},{1,15},{3,1}... | collective-permute-start | bytes 294920 | tf_op jit(solution)/shard_map/ppermute | solution.py:257
  75.7 6.4 %collective-permute-start.37 = (bf16[8,6144]{1,0:T(8,128)(2,1)S(1)}, bf16[8,6144]{1,0:T(8,128)(2,1)S(1)}, u32[]{:S(2)}, u32[]{:S(2)}) collective-permute-start(bf16[8,6144]{1,0:T(8,128)(2,1)S(1)} %shard_map.107), channel_id=1, source_target_pairs={{0,2},{2,4},{4,6},{6,8},{8,10},{10,12},{12,14},{14,0},{1,3},{3,5},... | collective-permute-start | bytes 294920 | tf_op jit(solution)/shard_map/ppermute | solution.py:257
  75.9 7.3 %collective-permute-start.30 = (bf16[8,6144]{1,0:T(8,128)(2,1)S(1)}, bf16[8,6144]{1,0:T(8,128)(2,1)S(1)}, u32[]{:S(2)}, u32[]{:S(2)}) collective-permute-start(bf16[8,6144]{1,0:T(8,128)(2,1)S(1)} %shard_map.99), channel_id=1, source_target_pairs={{0,2},{2,4},{4,6},{6,8},{8,10},{10,12},{12,14},{14,0},{1,3},{3,5},... | collective-permute-start | bytes 294920 | tf_op jit(solution)/shard_map/ppermute | solution.py:257
  76.3 7.0 %collective-permute-start.27 = (bf16[8,6144]{1,0:T(8,128)(2,1)S(1)}, bf16[8,6144]{1,0:T(8,128)(2,1)S(1)}, u32[]{:S(2)}, u32[]{:S(2)}) collective-permute-start(bf16[8,6144]{1,0:T(8,128)(2,1)S(1)} %shard_map.96), channel_id=1, source_target_pairs={{0,14},{2,0},{4,2},{6,4},{8,6},{10,8},{12,10},{14,12},{1,15},{3,1}... | collective-permute-start | bytes 294920 | tf_op jit(solution)/shard_map/ppermute | solution.py:257
  79.7 7.0 %collective-permute-start.34 = (bf16[8,6144]{1,0:T(8,128)(2,1)S(1)}, bf16[8,6144]{1,0:T(8,128)(2,1)S(1)}, u32[]{:S(2)}, u32[]{:S(2)}) collective-permute-start(bf16[8,6144]{1,0:T(8,128)(2,1)S(1)} %shard_map.104), channel_id=1, source_target_pairs={{0,14},{2,0},{4,2},{6,4},{8,6},{10,8},{12,10},{14,12},{1,15},{3,1}... | collective-permute-start | bytes 294920 | tf_op jit(solution)/shard_map/ppermute | solution.py:257
  83.2 9.5 %collective-permute-start.31 = (bf16[8,6144]{1,0:T(8,128)(2,1)S(1)}, bf16[8,6144]{1,0:T(8,128)(2,1)S(1)}, u32[]{:S(2)}, u32[]{:S(2)}) collective-permute-start(bf16[8,6144]{1,0:T(8,128)(2,1)S(1)} %shard_map.100), channel_id=1, source_target_pairs={{0,2},{2,4},{4,6},{6,8},{8,10},{10,12},{12,14},{14,0},{1,3},{3,5},... | collective-permute-start | bytes 294920 | tf_op jit(solution)/shard_map/ppermute | solution.py:257
  86.7 6.1 %collective-permute-start.35 = (bf16[8,6144]{1,0:T(8,128)(2,1)S(1)}, bf16[8,6144]{1,0:T(8,128)(2,1)S(1)}, u32[]{:S(2)}, u32[]{:S(2)}) collective-permute-start(bf16[8,6144]{1,0:T(8,128)(2,1)S(1)} %shard_map.105), channel_id=1, source_target_pairs={{0,14},{2,0},{4,2},{6,4},{8,6},{10,8},{12,10},{14,12},{1,15},{3,1}... | collective-permute-start | bytes 294920 | tf_op jit(solution)/shard_map/ppermute | solution.py:257
  88.1 6.6 %collective-permute-start.39 = (bf16[8,6144]{1,0:T(8,128)(2,1)S(1)}, bf16[8,6144]{1,0:T(8,128)(2,1)S(1)}, u32[]{:S(2)}, u32[]{:S(2)}) collective-permute-start(bf16[8,6144]{1,0:T(8,128)(2,1)S(1)} %shard_map.109), channel_id=1, source_target_pairs={{0,2},{2,4},{4,6},{6,8},{8,10},{10,12},{12,14},{14,0},{1,3},{3,5},... | collective-permute-start | bytes 294920 | tf_op jit(solution)/shard_map/ppermute | solution.py:257
  89.1 6.9 %collective-permute-start.29 = (bf16[8,6144]{1,0:T(8,128)(2,1)S(1)}, bf16[8,6144]{1,0:T(8,128)(2,1)S(1)}, u32[]{:S(2)}, u32[]{:S(2)}) collective-permute-start(bf16[8,6144]{1,0:T(8,128)(2,1)S(1)} %shard_map.98), channel_id=1, source_target_pairs={{0,14},{2,0},{4,2},{6,4},{8,6},{10,8},{12,10},{14,12},{1,15},{3,1}... | collective-permute-start | bytes 294920 | tf_op jit(solution)/shard_map/ppermute | solution.py:257
  99.6 8.1 %collective-permute-start.41 = (bf16[2,6144]{1,0:T(2,128)(2,1)S(1)}, bf16[2,6144]{1,0:T(2,128)(2,1)S(1)}, u32[]{:S(2)}, u32[]{:S(2)}) collective-permute-start(bf16[2,6144]{1,0:T(2,128)(2,1)S(1)} %get-tuple-element.38), channel_id=1, source_target_pairs={{0,96},{32,0},{64,32},{96,64},{1,97},{33,1},{65,33},{97,65},{2,98}... | collective-permute-start | bytes 73736 | tf_op jit(solution)/shard_map/ppermute | solution.py:249
  103.0 7.7 %collective-permute-start.42 = (bf16[2,6144]{1,0:T(2,128)(2,1)S(1)}, bf16[2,6144]{1,0:T(2,128)(2,1)S(1)}, u32[]{:S(2)}, u32[]{:S(2)}) collective-permute-start(bf16[2,6144]{1,0:T(2,128)(2,1)S(1)} %get-tuple-element.39), channel_id=1, source_target_pairs={{0,64},{32,96},{64,0},{96,32},{1,65},{33,97},{65,1},{97,33},{2,66}... | collective-permute-start | bytes 73736 | tf_op jit(solution)/shard_map/ppermute | solution.py:249
  (12 other events, 58.6 us)
